TPU v7x, 32 devices: a whole 2x2x4 slice. The times are simulated.
32 devices in a mesh: group: 8 (over y, x, core), blk: 4 (over z).
Axes of the slice: x: 2, y: 2, z: 4, core: 2. Of those that a mesh axis runs over, the one named last changes fastest.
Arguments:
- embeddings: bfloat16 [8192, 1024], P(('group', 'blk')), may hold values from -6 to 6
- dest_group: int32 [8192, 1], P(('group', 'blk')), may hold values from 0 to 7; in each aligned block of 256 rows (0 to 255, 256 to 511, ...) at most 64 rows name the same one
- order_rank: int32 [8192], P(('group', 'blk')), may hold values from 0 to 8191, each once
Outputs:
- best: float32 [8192], P(('group', 'blk'))
Inputs may be any that keep to these rules, and one draw needn't show every extreme that they name: `dest_group`: among the 256 members of one device, at most 64 name the same cluster. `order_rank`: all values differ.
All inputs are finite; a program needn't handle non-finite values.
Results may differ from a plain program's by a relative error of at most 0.0013.
Values may be sent and summed in bfloat16 or wider, within the bound.
No kernel may reach another device: no remote copies, remote signals or barrier semaphores. Data moves between devices by JAX's collectives and lax.ppermute only.
A program may use at most 128 MiB of HBM per device.

v0:
```python
import jax
import jax.numpy as jnp
from jax import lax
from jax.sharding import PartitionSpec as P


def shifted(value, axis, steps):
    count = lax.axis_size(axis)
    pairs = [(source, (source + steps) % count) for source in range(count)]
    return lax.ppermute(value, axis, pairs)


def masked_rows(scores, query_cluster, query_rank, key_cluster, key_rank):
    valid = (
        (key_cluster[None, :] == query_cluster[:, None])
        & (key_cluster[None, :] >= 0)
        & (key_rank[None, :] < query_rank[:, None])
    )
    return jnp.max(jnp.where(valid, scores, -1.0), axis=1)


def masked_columns(scores, query_cluster, query_rank, key_cluster, key_rank):
    valid = (
        (query_cluster[:, None] == key_cluster[None, :])
        & (query_cluster[:, None] >= 0)
        & (query_rank[:, None] < key_rank[None, :])
    )
    return jnp.max(jnp.where(valid, scores, -1.0), axis=0)


def similar(left, right):
    return jnp.einsum("qd,kd->qk", left, right, preferred_element_type=jnp.float32)


def on_device(embeddings, dest_group, order_rank):
    row_count = embeddings.shape[0]
    width = embeddings.shape[1]
    groups = lax.axis_size("group")
    capacity = row_count // 4
    buffered = groups * capacity
    values = embeddings.astype(jnp.float32)
    unit = (values * lax.rsqrt(jnp.sum(values * values, axis=1, keepdims=True) + 1e-06)).astype(
        jnp.bfloat16
    )
    target = dest_group[:, 0]
    onehot = (target[:, None] == jnp.arange(groups, dtype=jnp.int32)[None, :]).astype(jnp.int32)
    slot_index = jnp.sum((jnp.cumsum(onehot, axis=0) - onehot) * onehot, axis=1)
    position = target * capacity + slot_index
    send_unit = (
        jnp.zeros((buffered, width), jnp.bfloat16)
        .at[position]
        .set(unit)
        .reshape(groups, capacity, width)
    )
    send_cluster = (
        jnp.full((buffered,), -1, jnp.int32).at[position].set(target).reshape(groups, capacity)
    )
    send_rank = (
        jnp.zeros((buffered,), jnp.int32).at[position].set(order_rank).reshape(groups, capacity)
    )
    got_unit, got_cluster, got_rank = (
        lax.all_to_all(send_unit, "group", split_axis=0, concat_axis=0, tiled=True),
        lax.all_to_all(send_cluster, "group", split_axis=0, concat_axis=0, tiled=True),
        lax.all_to_all(send_rank, "group", split_axis=0, concat_axis=0, tiled=True),
    )
    mine_unit = got_unit.reshape(buffered, width)
    mine_cluster = got_cluster.reshape(buffered)
    mine_rank = got_rank.reshape(buffered)
    cycle_size = lax.axis_size("blk")
    running = masked_rows(
        similar(mine_unit, mine_unit), mine_cluster, mine_rank, mine_cluster, mine_rank
    )
    moving = (mine_unit, mine_cluster, mine_rank)
    for offset in range(1, cycle_size // 2 + 1):
        moving = shifted((moving[0], moving[1], moving[2]), "blk", 1)
        scores = similar(mine_unit, moving[0])
        running = jnp.maximum(
            running, masked_rows(scores, mine_cluster, mine_rank, moving[1], moving[2])
        )
        if 2 * offset < cycle_size:
            column_best = masked_columns(scores, mine_cluster, mine_rank, moving[1], moving[2])
            running = jnp.maximum(running, shifted(column_best, "blk", -offset))
    returned = lax.all_to_all(
        running.reshape(groups, capacity), "group", split_axis=0, concat_axis=0, tiled=True
    )
    return returned.reshape(buffered)[position]


def solution(mesh):
    placed = (P(("group", "blk"), None), P(("group", "blk"), None), P(("group", "blk")))
    return jax.shard_map(
        on_device, mesh=mesh, in_specs=placed, out_specs=P(("group", "blk")), check_vma=False
    )
```

profile of v0, /device:TPU:0, one launch (start us, length us, event | category | flops | bytes accessed | tf_op | source)
XLA Modules:
  0.0 102.2 jit_solution(673383244894404432)
XLA Ops:
  0.0 0.7 copy-done.1
  0.7 0.6 reduce-window.6
  1.6 1.2 %fusion.1 = f32[256]{0:T(256)S(1)} fusion(bf16[256,1024]{1,0:T(8,128)(2,1)} %param.3), kind=kLoop, calls=%fused_computation.8 | loop fusion | flops 786176 | bytes 525312 | tf_op jit(solution)/shard_map/reduce_sum | solution.py:42
  2.9 2.0 %scatter_custom_fusion.2 = bf16[512,1024]{1,0:T(8,128)(2,1)S(1)} fusion(s32[256]{0:T(256)S(1)} %bitcast.28, bf16[256,1024]{1,0:T(8,128)(2,1)S(1)} %copy-done, f32[256]{0:T(256)S(1)} %add_rsqrt_fusion, bf16[]{:T(256)} %constant.13.clone.1), kind=kCustom, calls=%fused_computation.13 | custom fusion | flops 786432 | bytes 1573890 | tf_op jit(solution)/shard_map/scatter | solution.py:52
  4.8 20.3 %all_to_all.32 = bf16[8,64,1024]{2,1,0:T(8,128)(2,1)S(1)} all-to-all(bf16[8,64,1024]{2,1,0:T(8,128)(2,1)S(1)} %bitcast.20), channel_id=1, replica_groups=mesh['group'=8,'blk'=4] {'group'}, dimensions={0} | all-to-all | bytes 2097152 | tf_op jit(solution)/shard_map/all_to_all | solution.py:62
  25.2 1.6 %collective-permute-start.2 = (bf16[512,1024]{1,0:T(8,128)(2,1)S(1)}, bf16[512,1024]{1,0:T(8,128)(2,1)}, u32[]{:S(2)}, u32[]{:S(2)}) collective-permute-start(bf16[512,1024]{1,0:T(8,128)(2,1)S(1)} %bitcast.21), channel_id=1, source_target_pairs={{0,1},{1,2},{2,3},{3,0},{4,5},{5,6},{6,7},{7,4},{8,9},{9,10},{10,1... | collective-permute-start | bytes 3145736 | tf_op jit(solution)/shard_map/ppermute | solution.py:10
  26.7 24.7 %collective-permute-done.2 = bf16[512,1024]{1,0:T(8,128)(2,1)} collective-permute-done((bf16[512,1024]{1,0:T(8,128)(2,1)S(1)}, bf16[512,1024]{1,0:T(8,128)(2,1)}, u32[]{:S(2)}, u32[]{:S(2)}) %collective-permute-start.2) | collective-permute-done | bytes 1048608 | tf_op jit(solution)/shard_map/ppermute | solution.py:10
  51.5 1.4 %scatter_custom_fusion = s32[512]{0:T(512)S(1)} fusion(s32[256]{0:T(256)S(1)} %bitcast.29, s32[256]{0:T(256)S(1)} %bitcast.27, s32[]{:T(128)} %constant.9.clone.1), kind=kCustom, calls=%fused_computation.32 | custom fusion | bytes 2052 | tf_op jit(solution)/shard_map/scatter | solution.py:56
  52.9 0.7 all_to_all.21
  53.6 3.3 %all-to-all-start = ((s32[8,1,64]{2,1,0:T(1,128)}), s32[8,1,64]{2,1,0:T(1,128)S(1)}, u32[]{:S(2)}, u32[]{:S(2)}) async-start(s32[8,1,64]{2,1,0:T(1,128)} %all_to_all.21), calls=%async_computation | async-start | bytes 8192 | tf_op jit(solution)/shard_map/all_to_all | solution.py:63
  56.8 1.6 %scatter_custom_fusion.1 = s32[512]{0:T(512)S(1)} fusion(s32[256]{0:T(256)S(1)} %bitcast.30, s32[256]{0:T(256)} %param.5, s32[]{:T(128)} %constant.11.clone.1), kind=kCustom, calls=%fused_computation.29 | custom fusion | bytes 2560 | tf_op jit(solution)/shard_map/scatter | solution.py:59
  58.4 0.7 all_to_all.23
  59.1 2.4 %all-to-all-done = s32[8,1,64]{2,1,0:T(1,128)S(1)} async-done(((s32[8,1,64]{2,1,0:T(1,128)}), s32[8,1,64]{2,1,0:T(1,128)S(1)}, u32[]{:S(2)}, u32[]{:S(2)}) %all-to-all-start) | async-done | bytes 2080 | tf_op jit(solution)/shard_map/all_to_all | solution.py:63
  61.4 3.3 %all-to-all-start.1 = ((s32[8,1,64]{2,1,0:T(1,128)}), s32[8,1,64]{2,1,0:T(1,128)S(1)}, u32[]{:S(2)}, u32[]{:S(2)}) async-start(s32[8,1,64]{2,1,0:T(1,128)} %all_to_all.23), calls=%async_computation.1 | async-start | bytes 8192 | tf_op jit(solution)/shard_map/all_to_all | solution.py:64
  64.8 0.5 broadcast.77
  65.3 0.7 reduce.12
  66.0 1.3 %collective-permute-start = (s32[512]{0:T(512)S(1)}, s32[512]{0:T(512)S(1)}, u32[]{:S(2)}, u32[]{:S(2)}) collective-permute-start(s32[512]{0:T(512)S(1)} %eq.79), channel_id=1, source_target_pairs={{0,1},{1,2},{2,3},{3,0},{4,5},{5,6},{6,7},{7,4},{8,9},{9,10},{10,1... | collective-permute-start | bytes 6152 | tf_op jit(solution)/shard_map/ppermute | solution.py:10
  67.3 2.1 %all-to-all-done.1 = s32[8,1,64]{2,1,0:T(1,128)S(1)} async-done(((s32[8,1,64]{2,1,0:T(1,128)}), s32[8,1,64]{2,1,0:T(1,128)S(1)}, u32[]{:S(2)}, u32[]{:S(2)}) %all-to-all-start.1) | async-done | bytes 2080 | tf_op jit(solution)/shard_map/all_to_all | solution.py:64
  69.4 0.7 reduce.11
  70.1 1.3 %collective-permute-start.1 = (s32[512]{0:T(512)S(1)}, s32[512]{0:T(512)S(1)}, u32[]{:S(2)}, u32[]{:S(2)}) collective-permute-start(s32[512]{0:T(512)S(1)} %lt.22), channel_id=1, source_target_pairs={{0,1},{1,2},{2,3},{3,0},{4,5},{5,6},{6,7},{7,4},{8,9},{9,10},{10,1... | collective-permute-start | bytes 6152 | tf_op jit(solution)/shard_map/ppermute | solution.py:10
  71.4 5.7 %collective-permute-done = s32[512]{0:T(512)S(1)} collective-permute-done((s32[512]{0:T(512)S(1)}, s32[512]{0:T(512)S(1)}, u32[]{:S(2)}, u32[]{:S(2)}) %collective-permute-start) | collective-permute-done | bytes 2080 | tf_op jit(solution)/shard_map/ppermute | solution.py:10
  77.2 5.3 %collective-permute-done.4 = s32[512]{0:T(512)S(1)} collective-permute-done((s32[512]{0:T(512)S(1)}, s32[512]{0:T(512)S(1)}, u32[]{:S(2)}, u32[]{:S(2)}) %collective-permute-start.4) | collective-permute-done | bytes 2080 | tf_op jit(solution)/shard_map/ppermute | solution.py:10
  82.5 2.0 %fusion.14 = f32[512,512]{0,1:T(8,128)S(1)} fusion(bf16[512,1024]{1,0:T(8,128)(2,1)S(1)} %bitcast.22, bf16[512,1024]{1,0:T(8,128)(2,1)} %collective-permute-done.2), kind=kOutput, calls=%fused_computation.34 | convolution fusion | flops 536870912 | bytes 3145728 | tf_op jit(solution)/shard_map/qd,kd->qk/dot_general | solution.py:32
  84.5 1.7 %select_reduce_fusion.2 = (f32[512]{0:T(512)S(1)}, f32[512]{0:T(512)S(1)}, f32[512]{0:T(512)S(1)}) fusion(f32[512,512]{0,1:T(8,128)S(1)} %fusion.14, s32[512]{0:T(512)S(1)} %lt.22, s32[512]{0:T(512)S(1)} %eq.79, s32[512]{0:T(512)S(1)} %collective-permute-done.1, s32[512]{0:T(512)S(1)} %collective-permute-done, ...), kind=kOutput, calls=%fused_computation.12 | convolution fusion | flops 541587968 | bytes 3165696 | tf_op jit(solution)/shard_map/qd,kd->qk/dot_general | solution.py:32
  86.3 0.8 fusion
  87.1 2.7 %collective-permute-done.3 = f32[512]{0:T(512)S(1)} collective-permute-done((f32[512]{0:T(512)S(1)}, f32[512]{0:T(512)S(1)}, u32[]{:S(2)}, u32[]{:S(2)}) %collective-permute-start.3) | collective-permute-done | bytes 2080 | tf_op jit(solution)/shard_map/ppermute | solution.py:10
  89.8 0.7 all_to_all.26
  90.5 3.3 %all-to-all-start.3 = ((f32[8,1,64]{2,1,0:T(1,128)}), f32[8,1,64]{2,1,0:T(1,128)S(1)}, u32[]{:S(2)}, u32[]{:S(2)}) async-start(f32[8,1,64]{2,1,0:T(1,128)} %all_to_all.26), calls=%async_computation.3 | async-start | bytes 8192 | tf_op jit(solution)/shard_map/all_to_all | solution.py:83
  93.8 4.6 %all-to-all-done.3 = f32[8,1,64]{2,1,0:T(1,128)S(1)} async-done(((f32[8,1,64]{2,1,0:T(1,128)}), f32[8,1,64]{2,1,0:T(1,128)S(1)}, u32[]{:S(2)}, u32[]{:S(2)}) %all-to-all-start.3) | async-done | bytes 2080 | tf_op jit(solution)/shard_map/all_to_all | solution.py:83
  98.4 0.5 broadcast.79
  98.9 0.7 reduce.13
  99.7 2.5 %gather_fusion = f32[256]{0:T(256)} fusion(f32[512]{0:T(512)S(1)} %reshape.84, s32[1024]{0:T(1024)S(1)} %pad_clamp_fusion), kind=kCustom, calls=%fused_computation | custom fusion | bytes 3072 | tf_op jit(solution)/shard_map/gather | solution.py:86
  (25 shorter events, 0.8 us)
Async XLA Ops:
  0.0 0.7 copy-start.1
  0.0 2.9 %copy-start = (bf16[256,1024]{1,0:T(8,128)(2,1)S(1)}, bf16[256,1024]{1,0:T(8,128)(2,1)}, u32[]{:S(2)}) copy-start(bf16[256,1024]{1,0:T(8,128)(2,1)} %param.3) | copy-start | bytes 1572868
  25.2 26.3 %collective-permute-start.2 = (bf16[512,1024]{1,0:T(8,128)(2,1)S(1)}, bf16[512,1024]{1,0:T(8,128)(2,1)}, u32[]{:S(2)}, u32[]{:S(2)}) collective-permute-start(bf16[512,1024]{1,0:T(8,128)(2,1)S(1)} %bitcast.21), channel_id=1, source_target_pairs={{0,1},{1,2},{2,3},{3,0},{4,5},{5,6},{6,7},{7,4},{8,9},{9,10},{10,1... | collective-permute-start | bytes 3145736 | tf_op jit(solution)/shard_map/ppermute | solution.py:10
  51.5 33.0 %collective-permute-start.6 = (bf16[512,1024]{1,0:T(8,128)(2,1)}, bf16[512,1024]{1,0:T(8,128)(2,1)S(1)}, u32[]{:S(2)}, u32[]{:S(2)}) collective-permute-start(bf16[512,1024]{1,0:T(8,128)(2,1)} %collective-permute-done.2), channel_id=1, source_target_pairs={{0,1},{1,2},{2,3},{3,0},{4,5},{5,6},{6,7},{7,4},{8,9},{9,10},{10,1... | collective-permute-start | bytes 3145736 | tf_op jit(solution)/shard_map/ppermute | solution.py:10
  53.6 7.9 %all-to-all-start = ((s32[8,1,64]{2,1,0:T(1,128)}), s32[8,1,64]{2,1,0:T(1,128)S(1)}, u32[]{:S(2)}, u32[]{:S(2)}) async-start(s32[8,1,64]{2,1,0:T(1,128)} %all_to_all.21), calls=%async_computation | async-start | bytes 8192 | tf_op jit(solution)/shard_map/all_to_all | solution.py:63
  61.4 7.9 %all-to-all-start.1 = ((s32[8,1,64]{2,1,0:T(1,128)}), s32[8,1,64]{2,1,0:T(1,128)S(1)}, u32[]{:S(2)}, u32[]{:S(2)}) async-start(s32[8,1,64]{2,1,0:T(1,128)} %all_to_all.23), calls=%async_computation.1 | async-start | bytes 8192 | tf_op jit(solution)/shard_map/all_to_all | solution.py:64
  66.0 11.1 %collective-permute-start = (s32[512]{0:T(512)S(1)}, s32[512]{0:T(512)S(1)}, u32[]{:S(2)}, u32[]{:S(2)}) collective-permute-start(s32[512]{0:T(512)S(1)} %eq.79), channel_id=1, source_target_pairs={{0,1},{1,2},{2,3},{3,0},{4,5},{5,6},{6,7},{7,4},{8,9},{9,10},{10,1... | collective-permute-start | bytes 6152 | tf_op jit(solution)/shard_map/ppermute | solution.py:10
  70.1 7.0 %collective-permute-start.1 = (s32[512]{0:T(512)S(1)}, s32[512]{0:T(512)S(1)}, u32[]{:S(2)}, u32[]{:S(2)}) collective-permute-start(s32[512]{0:T(512)S(1)} %lt.22), channel_id=1, source_target_pairs={{0,1},{1,2},{2,3},{3,0},{4,5},{5,6},{6,7},{7,4},{8,9},{9,10},{10,1... | collective-permute-start | bytes 6152 | tf_op jit(solution)/shard_map/ppermute | solution.py:10
  77.1 5.4 %collective-permute-start.4 = (s32[512]{0:T(512)S(1)}, s32[512]{0:T(512)S(1)}, u32[]{:S(2)}, u32[]{:S(2)}) collective-permute-start(s32[512]{0:T(512)S(1)} %collective-permute-done), channel_id=1, source_target_pairs={{0,1},{1,2},{2,3},{3,0},{4,5},{5,6},{6,7},{7,4},{8,9},{9,10},{10,1... | collective-permute-start | bytes 6152 | tf_op jit(solution)/shard_map/ppermute | solution.py:10
  77.1 7.3 %collective-permute-start.5 = (s32[512]{0:T(512)S(1)}, s32[512]{0:T(512)S(1)}, u32[]{:S(2)}, u32[]{:S(2)}) collective-permute-start(s32[512]{0:T(512)S(1)} %collective-permute-done.1), channel_id=1, source_target_pairs={{0,1},{1,2},{2,3},{3,0},{4,5},{5,6},{6,7},{7,4},{8,9},{9,10},{10,1... | collective-permute-start | bytes 6152 | tf_op jit(solution)/shard_map/ppermute | solution.py:10
  86.2 3.6 %collective-permute-start.3 = (f32[512]{0:T(512)S(1)}, f32[512]{0:T(512)S(1)}, u32[]{:S(2)}, u32[]{:S(2)}) collective-permute-start(f32[512]{0:T(512)S(1)} %get-tuple-element.6), channel_id=1, source_target_pairs={{0,3},{1,0},{2,1},{3,2},{4,7},{5,4},{6,5},{7,6},{8,11},{9,8},{10,9... | collective-permute-start | bytes 6152 | tf_op jit(solution)/shard_map/ppermute | solution.py:10
  90.5 8.0 %all-to-all-start.3 = ((f32[8,1,64]{2,1,0:T(1,128)}), f32[8,1,64]{2,1,0:T(1,128)S(1)}, u32[]{:S(2)}, u32[]{:S(2)}) async-start(f32[8,1,64]{2,1,0:T(1,128)} %all_to_all.26), calls=%async_computation.3 | async-start | bytes 8192 | tf_op jit(solution)/shard_map/all_to_all | solution.py:83
where the time goes:
time: 103 us; the launch traced here: 102 us
  waiting for transfers between devices  47.5 us (46%)
  blocking collectives  20.3 us (20%)
  starting transfers between devices  14.2 us (14%)
  local copies, waits for them, and re-layouts  9.62 us (9%)
  other arithmetic  5.92 us (6%)
  matrix products  4.46 us (4%)
    ppermute x7, waiting for transfers between devices, shifted(): return lax.ppermute(value, axis, pairs)  38.4 us
    all_to_all x1, blocking collectives, on_device(): lax.all_to_all(send_unit, 'group', split_axis=0, concat_axis=0, tiled=True)  20.3 us
    all_to_all x1, waiting for transfers between devices, on_device(): lax.all_to_all(running.reshape(groups, capacity), 'group', split_axis=0,...  4.6 us
    dot_general x3, matrix products, similar(): jnp.einsum('qd,kd->qk', left, right, preferred_element_type=jnp.float32)  4.46 us
    ppermute x7, starting transfers between devices, shifted(): return lax.ppermute(value, axis, pairs)  4.33 us
    all_to_all x1, starting transfers between devices, on_device(): lax.all_to_all(running.reshape(groups, capacity), 'group', split_axis=0,...  3.33 us
    all_to_all x1, starting transfers between devices, on_device(): lax.all_to_all(send_rank, 'group', split_axis=0, concat_axis=0, tiled=True)  3.33 us
    all_to_all x1, starting transfers between devices, on_device(): lax.all_to_all(send_cluster, 'group', split_axis=0, concat_axis=0, tiled=...  3.26 us
  transfers between devices with their start and end apart: 10, of which 7 were waited for; matrix products, arithmetic and copies ran while one was open for 8% of the time, Pallas kernels for 0%

commit v1 on v0

v1 whole, which is shorter than its diff:
```python
import functools

import jax
import jax.numpy as jnp
from jax import lax
from jax.experimental import pallas as pl
from jax.experimental.pallas import tpu as pltpu
from jax.sharding import PartitionSpec as P


LANES = 128
META = 16
VMEM = pl.BlockSpec(memory_space=pltpu.VMEM)
F32 = jnp.float32
BF16 = jnp.bfloat16


def nt(left, right):
    return lax.dot_general(left, right, (((1,), (1,)), ((), ())), preferred_element_type=F32)


def call(body, outs, operands, flops, moved, limit, scratch=()):
    return pl.pallas_call(
        body,
        out_shape=outs,
        in_specs=[VMEM] * len(operands),
        out_specs=jax.tree.map(lambda _: VMEM, outs),
        scratch_shapes=list(scratch),
        cost_estimate=pl.CostEstimate(flops=flops, bytes_accessed=moved, transcendentals=0),
        compiler_params=pltpu.CompilerParams(vmem_limit_bytes=limit),
    )(*operands)


def gathered(emb_ref, code_ref, chip, core, chips, cap):
    rows = emb_ref.shape[0]
    clusters = max(16, 2 * chips)
    values = emb_ref[...].astype(F32)
    norm = lax.rsqrt(jnp.sum(values * values, axis=1, keepdims=True) + 1e-06)
    unit = (values * norm).astype(BF16)
    code = code_ref[...]
    dest, rank = code >> 16, code & 65535
    onehot = (lax.broadcasted_iota(jnp.int32, (clusters, rows), 0) == dest).astype(F32)
    row = lax.broadcasted_iota(jnp.int32, (rows, rows), 0)
    column = lax.broadcasted_iota(jnp.int32, (rows, rows), 1)
    before = (row < column).astype(F32).astype(BF16)
    count = jnp.dot(onehot.astype(BF16), before, preferred_element_type=F32)
    slot = jnp.sum(count * onehot, axis=0, keepdims=True).astype(jnp.int32)
    where = ((dest >> 1) ^ chip) * cap + slot
    pos = jnp.where((dest & 1) == core, where, -1)
    pick = lax.broadcasted_iota(jnp.int32, (chips * cap, rows), 0) == pos
    pick = pick.astype(F32).astype(BF16)
    digits = lax.broadcasted_iota(jnp.int32, (META, rows), 0)
    digits = jnp.where(
        digits == 0, rank >> 8, jnp.where(digits == 1, rank & 255, jnp.where(digits == 2, 1, 0))
    )
    digits = nt(digits.astype(F32).astype(BF16), pick)
    top = lax.broadcasted_iota(jnp.int32, digits.shape, 0) == 0
    digits = jnp.where(top & (digits[2:3, :] < 0.5), 256.0, digits)
    packed = jnp.dot(pick, unit, preferred_element_type=F32).astype(BF16)
    return packed, digits, where, dest


def pack_body(cap, chips, own_ref, mate_ref, own_code, mate_code, *refs):
    group = lax.axis_index("group")
    chip, core = group >> 1, group & 1
    pieces = own_ref.shape[1] // LANES
    own, own_digits, where, dest = gathered(own_ref, own_code, chip, core, chips, cap)
    mate, mate_digits, _, _ = gathered(mate_ref, mate_code, chip, core, chips, cap)
    refs[-1][...] = where * 2 + ((dest & 1) ^ core)
    for s in range(chips):
        part = slice(s * cap, (s + 1) * cap)
        for k in range(pieces):
            lanes = slice(k * LANES, (k + 1) * LANES)
            refs[s][k * LANES : k * LANES + cap, :] = own[part, lanes]
            refs[s][k * LANES + cap : (k + 1) * LANES, :] = mate[part, lanes]
        refs[s][pieces * LANES : pieces * LANES + META, :] = jnp.concatenate(
            [own_digits[:, part], mate_digits[:, part]], axis=1
        ).astype(BF16)


def join_body(*refs):
    out_ref, base = refs[-1], 0
    for ref in refs[:-1]:
        out_ref[base : base + ref.shape[0], :] = ref[...]
        base += ref.shape[0]


def unfold(refs, pieces, x_ref, column_ref, row_ref):
    size = pieces * LANES + META
    base = 0
    for ref in refs:
        for b in range(ref.shape[0] // size):
            rows = slice(base, base + LANES)
            for k in range(pieces):
                x_ref[rows, k * LANES : (k + 1) * LANES] = ref[
                    b * size + k * LANES : b * size + (k + 1) * LANES, :
                ]
            meta = ref[b * size + pieces * LANES : (b + 1) * size, :].astype(F32)
            rank = meta[0:1, :] * 256.0 + meta[1:2, :]
            row_ref[:, rows] = rank
            column_ref[rows, :] = jnp.transpose(jnp.broadcast_to(rank, (LANES, LANES)))
            base += LANES


def wide_max(scores):
    return jnp.max(scores.reshape(-1, 8, scores.shape[1]), axis=0)


def lane_max(scores):
    parts = [scores[:, i : i + LANES] for i in range(0, scores.shape[1], LANES)]
    return functools.reduce(jnp.maximum, parts)


def across(column, width):
    return jnp.concatenate([column] * (width // LANES), axis=1)


def tile_for(count):
    return next(t for t in (512, 256, 128) if count % t == 0)


def old_body(pieces, many, *refs):
    blocks, (x_ref, column_ref, row_ref, best_ref, side_ref) = refs[:many], refs[many:]
    unfold(blocks, pieces, x_ref, column_ref, row_ref)
    count = x_ref.shape[0]
    tile = tile_for(count)
    best_ref[...] = jnp.full(best_ref.shape, -1.0, F32)
    side_ref[...] = jnp.full(side_ref.shape, -1.0, F32)

    def outer(i, _):
        mine = pl.ds(pl.multiple_of(i * tile, tile), tile)
        query, query_rank = x_ref[mine, :], row_ref[:, mine]
        scores = nt(query, query)
        earlier = across(column_ref[mine, :], tile) < query_rank
        best_ref[:, mine] = jnp.maximum(
            best_ref[:, mine], wide_max(jnp.where(earlier, scores, -1.0))
        )

        def inner(j, _):
            keys = pl.ds(pl.multiple_of(j * tile, tile), tile)
            scores = nt(x_ref[keys, :], x_ref[mine, :])
            earlier = across(column_ref[keys, :], tile) < row_ref[:, mine]
            best_ref[:, mine] = jnp.maximum(
                best_ref[:, mine], wide_max(jnp.where(earlier, scores, -1.0))
            )
            side_ref[keys, :] = jnp.maximum(
                side_ref[keys, :], lane_max(jnp.where(earlier, -1.0, scores))
            )
            return 0

        lax.fori_loop(0, i, inner, 0)
        return 0

    lax.fori_loop(0, count // tile, outer, 0)
    for i in range(0, count, LANES):
        turned = jnp.transpose(side_ref[i : i + LANES, :])
        best_ref[:, i : i + LANES] = jnp.maximum(best_ref[:, i : i + LANES], wide_max(turned))


def new_body(pieces, planes, shares, many, x_ref, column_ref, row_ref, old_ref, *refs):
    blocks, outs = refs[:many], refs[many : many + planes]
    new_ref, new_column, new_row, best_ref, side_ref, acc_ref = refs[many + planes :]
    unfold(blocks, pieces, new_ref, new_column, new_row)
    old, new = x_ref.shape[0], new_ref.shape[0]
    tile, wide = tile_for(new), tile_for(old)
    acc_ref[...] = old_ref[...]
    best_ref[...] = jnp.full(best_ref.shape, -1.0, F32)
    side_ref[...] = jnp.full(side_ref.shape, -1.0, F32)

    def outer(j, _):
        keys = pl.ds(pl.multiple_of(j * tile, tile), tile)

        def inner(i, _):
            mine = pl.ds(pl.multiple_of(i * wide, wide), wide)
            scores = nt(new_ref[keys, :], x_ref[mine, :])
            earlier = across(new_column[keys, :], wide) < row_ref[:, mine]
            acc_ref[:, mine] = jnp.maximum(
                acc_ref[:, mine], wide_max(jnp.where(earlier, scores, -1.0))
            )
            side_ref[keys, :] = jnp.maximum(
                side_ref[keys, :], lane_max(jnp.where(earlier, -1.0, scores))
            )
            return 0

        lax.fori_loop(0, old // wide, inner, 0)

        def among(i, _):
            mine = pl.ds(pl.multiple_of(i * tile, tile), tile)
            scores = nt(new_ref[keys, :], new_ref[mine, :])
            earlier = across(new_column[keys, :], tile) < new_row[:, mine]
            best_ref[:, mine] = jnp.maximum(
                best_ref[:, mine], wide_max(jnp.where(earlier, scores, -1.0))
            )
            return 0

        lax.fori_loop(0, new // tile, among, 0)
        return 0

    lax.fori_loop(0, new // tile, outer, 0)
    early, late = shares
    for p in range(planes):
        row = 0
        for start, share in ((p, 1), (planes + p * early, early)):
            for i in range(share):
                at = (start + i) * LANES
                outs[p][row : row + 1, :] = jnp.max(
                    acc_ref[:, at : at + LANES], axis=0, keepdims=True
                )
                row += 1
        for i in range(late):
            at = (p * late + i) * LANES
            side = jnp.transpose(side_ref[at : at + LANES, :])
            best = jnp.maximum(best_ref[:, at : at + LANES], wide_max(side))
            outs[p][row : row + 1, :] = jnp.max(best, axis=0, keepdims=True)
            row += 1


def final_body(cap, chips, pos_ref, own_ref, mate_ref, out_ref):
    rows = pos_ref.shape[1]
    pos = pos_ref[...]
    other, where = pos & 1, pos >> 1
    chip, slot = where // cap, where % cap
    place = lax.broadcasted_iota(jnp.int32, (LANES, rows), 0)
    pick = (place == slot + cap * other).astype(F32)
    table = jnp.concatenate([own_ref[...], mate_ref[...]], axis=0)
    got = lax.dot_general(
        table,
        pick,
        (((1,), (0,)), ((), ())),
        precision=lax.Precision.HIGHEST,
        preferred_element_type=F32,
    )
    mine = lax.broadcasted_iota(jnp.int32, (2 * chips, rows), 0) == chip + chips * other
    out_ref[...] = jnp.sum(jnp.where(mine, got, 0.0), axis=0, keepdims=True)


def on_device(embeddings, dest_group, order_rank):
    rows, width = embeddings.shape
    groups = lax.axis_size("group")
    planes = lax.axis_size("blk")
    chips, half = groups // 2, planes // 2
    cap = rows // 4
    pieces = width // LANES
    size = pieces * LANES + META
    group, plane = lax.axis_index("group"), lax.axis_index("blk")

    def blocks(n):
        return jax.ShapeDtypeStruct((n * size, LANES), BF16)

    def floats(*shape):
        return jax.ShapeDtypeStruct(shape, F32)

    def to_chip(value, s):
        return lax.ppermute(value, "group", [(i, i ^ (2 * s)) for i in range(groups)])

    def to_core(value):
        return lax.ppermute(value, "group", [(i, i ^ 1) for i in range(groups)])

    meet = [half, half - 1]
    sources = [[z for z in range(planes) if z != half]]
    sources.append([planes - 1 - z for z in sources[0]])

    def meeting(step, back=False):
        pairs = []
        for g in range(groups):
            there = g * planes + meet[g & 1]
            here = g * planes + sources[g & 1][step]
            pairs.append((there, here) if back else (here, there))
        return pairs

    def gather(value):
        arrived = [value]
        for step in range(planes - 1):
            arrived.append(lax.ppermute(value, ("group", "blk"), meeting(step)))
        return arrived

    code = (dest_group.reshape(1, rows) << 16) | order_rank.reshape(1, rows)
    mate = to_core(embeddings)
    mate_code = to_core(code)
    packed = call(
        functools.partial(pack_body, cap, chips),
        [blocks(1)] * chips + [jax.ShapeDtypeStruct((1, rows), jnp.int32)],
        [embeddings, mate, code, mate_code],
        4 * chips * cap * rows * width,
        8 * rows * width,
        16 << 20,
    )
    pos = packed[-1]
    sent = []
    for s in range(1, chips):
        sent.append(to_chip(packed[s], s))
    early = max(1, (chips - 1) * 2 // 3)
    late = chips - 1 - early

    def join(arrays):
        if len(arrays) == 1:
            return arrays[0]
        total = sum(a.shape[0] for a in arrays)
        moved = 4 * total * LANES
        out = jax.ShapeDtypeStruct((total, LANES), BF16)
        return call(join_body, out, arrays, 1000, moved, 2 * moved)

    first = gather(packed[0])
    second = gather(join(sent[:early]))
    third = gather(join(sent[early:]))
    n_old, n_new = planes * (1 + early) * LANES, planes * late * LANES

    def room(n):
        return [floats(n, LANES), floats(1, n), floats(8, n)]

    side = pltpu.VMEM((n_old, LANES), F32)
    old = call(
        functools.partial(old_body, pieces, 2 * planes),
        [jax.ShapeDtypeStruct((n_old, width), BF16)] + room(n_old),
        first + second,
        n_old * n_old * width,
        4 * n_old * width,
        6 * n_old * width,
        scratch=[side],
    )
    held = [pltpu.VMEM((n_new, width), BF16)]
    held += [pltpu.VMEM(s, F32) for s in ((n_new, LANES), (1, n_new), (8, n_new), (n_new, LANES))]
    held.append(pltpu.VMEM((8, n_old), F32))
    best = call(
        functools.partial(new_body, pieces, planes, (early, late), planes),
        [floats(chips, LANES)] * planes,
        list(old) + third,
        2 * n_new * (n_old + n_new) * width,
        2 * (n_old + n_new) * width,
        6 * (n_old + n_new) * width,
        scratch=held,
    )
    returned = [
        lax.ppermute(best[1 + step], ("group", "blk"), meeting(step, back=True))
        for step in range(planes - 1)
    ]
    at_meeting = plane == jnp.where((group & 1) == 0, half, half - 1)
    mine = jnp.where(at_meeting, best[0], functools.reduce(jnp.add, returned))
    rows_of = [mine[0:1]] + [to_chip(mine, s)[s : s + 1] for s in range(1, chips)]
    table = jnp.concatenate(rows_of, axis=0)
    result = call(
        functools.partial(final_body, cap, chips),
        floats(1, rows),
        [pos, table, to_core(table)],
        1000000,
        100000,
        4 << 20,
    )
    return result.reshape(rows)


def solution(mesh):
    placed = (P(("group", "blk"), None), P(("group", "blk"), None), P(("group", "blk")))

    return jax.shard_map(
        on_device, mesh=mesh, in_specs=placed, out_specs=P(("group", "blk")), check_vma=False
    )
```

time: 103 us -> 64.4 us (0.63)
  waiting for transfers between devices: 47.5 us -> 21.6 us
  blocking collectives: 20.3 us -> 0 us
  starting transfers between devices: 14.2 us -> 28.8 us
  Pallas kernels: 0 us -> 10.9 us
  local copies, waits for them, and re-layouts: 9.62 us -> 1.06 us
  other arithmetic: 5.92 us -> 1.38 us
  matrix products: 4.46 us -> 0 us
    ppermute x7 -> x21, starting transfers between devices: 4.33 us -> 28.8 us  [the longest x9 15.9 us: gather(): arrived.append(lax.ppermute(value, ('group', 'blk'), meeting(step)))]
    all_to_all x1 -> x0, blocking collectives: 20.3 us -> none  [on_device(): lax.all_to_all(send_unit, 'group', split_axis=0, concat_axis=0, tiled=True)]
    ppermute x7 -> x21, waiting for transfers between devices: 38.4 us -> 21.6 us  [the longest x6 10.8 us: to_chip(): return lax.ppermute(value, 'group', [(i, i ^ 2 * s) for i in range(groups)])]
    pallas_call x0 -> x5, Pallas kernels: none -> 10.9 us  [call(): pl.pallas_call(body, out_shape=outs, in_specs=[VMEM] * len(operands), out...]
    all_to_all x3 -> x0, starting transfers between devices: 9.91 us -> none  [the longest x1 3.33 us: on_device(): lax.all_to_all(running.reshape(groups, capacity), 'group', split_axis=0,...]
    all_to_all x3 -> x0, waiting for transfers between devices: 9.05 us -> none  [the longest x1 4.6 us: on_device(): lax.all_to_all(running.reshape(groups, capacity), 'group', split_axis=0,...]
    dot_general x3 -> x0, matrix products: 4.46 us -> none  [similar(): jnp.einsum('qd,kd->qk', left, right, preferred_element_type=jnp.float32)]
    all_to_all x5 -> x0, local copies, waits for them, and re-layouts: 3.04 us -> none  [the longest x2 1.19 us: on_device(): lax.all_to_all(running.reshape(groups, capacity), 'group', split_axis=0,...]
  transfers between devices with their start and end apart: 10 -> 21, of which waited for: 7 -> 9; matrix products, arithmetic and copies ran while one was open for 8% -> 2% of each run, Pallas kernels for 0% -> 9%
where the time goes in v1:
time: 64.4 us; the launch traced here: 63.9 us
  starting transfers between devices  28.8 us (45%)
  waiting for transfers between devices  21.6 us (34%)
  Pallas kernels  10.9 us (17%)
  other arithmetic  1.38 us (2%)
  local copies, waits for them, and re-layouts  1.06 us (2%)
    ppermute x9, starting transfers between devices, gather(): arrived.append(lax.ppermute(value, ('group', 'blk'), meeting(step)))  15.9 us
    pallas_call x5, Pallas kernels, call(): pl.pallas_call(body, out_shape=outs, in_specs=[VMEM] * len(operands), out...  10.9 us
    ppermute x6, waiting for transfers between devices, to_chip(): return lax.ppermute(value, 'group', [(i, i ^ 2 * s) for i in range(groups)])  10.8 us
    ppermute x6, starting transfers between devices, to_chip(): return lax.ppermute(value, 'group', [(i, i ^ 2 * s) for i in range(groups)])  9.34 us
    ppermute x3, waiting for transfers between devices, on_device(): lax.ppermute(best[1 + step], ('group', 'blk'), meeting(step, back=True))  8.8 us
    ppermute x3, starting transfers between devices, on_device(): lax.ppermute(best[1 + step], ('group', 'blk'), meeting(step, back=True))  2.62 us
    ppermute x3, waiting for transfers between devices, to_core(): return lax.ppermute(value, 'group', [(i, i ^ 1) for i in range(groups)])  1.97 us
  transfers between devices with their start and end apart: 21, of which 9 were waited for; matrix products, arithmetic and copies ran while one was open for 2% of the time, Pallas kernels for 9%

profile of v1, /device:TPU:0, one launch (start us, length us, event | category | flops | bytes accessed | tf_op | source)
XLA Modules:
  0.0 63.9 jit_solution(15928028933061767542)
XLA Ops:
  0.5 0.7 %broadcast_shift-left_fusion = s32[256,1]{0,1:T(1,128)S(1)} fusion(s32[256,1]{0,1:T(1,128)} %param.4), kind=kLoop, calls=%fused_computation.2 | loop fusion | flops 256 | bytes 2048 | tf_op jit(solution)/shard_map/shift_left | solution.py:277
  1.2 0.7 %or.5 = s32[256]{0:T(256)S(1)} or(s32[256]{0:T(256)S(1)} %bitcast.5, s32[256]{0:T(256)} %param.5) | non-fusion elementwise | flops 256 | bytes 3072 | tf_op jit(solution)/shard_map/or | solution.py:277
  1.9 1.1 %collective-permute-done.1.mate_code = s32[1,256]{1,0:T(1,128)S(1)} collective-permute-done((s32[1,256]{1,0:T(1,128)S(1)}, s32[1,256]{1,0:T(1,128)S(1)}, u32[]{:S(2)}, u32[]{:S(2)}) %collective-permute-start.1) | collective-permute-done | bytes 1056 | tf_op jit(solution)/shard_map/ppermute | solution.py:257
  3.0 1.0 %copy-done = bf16[256,1024]{1,0:T(8,128)(2,1)S(1)} copy-done((bf16[256,1024]{1,0:T(8,128)(2,1)S(1)}, bf16[256,1024]{1,0:T(8,128)(2,1)}, u32[]{:S(2)}) %copy-start) | copy-done | bytes 524312
  4.1 0.8 %shard_map.37 = (bf16[1040,128]{1,0:T(8,128)(2,1)S(1)}, bf16[1040,128]{1,0:T(8,128)(2,1)S(1)}, bf16[1040,128]{1,0:T(8,128)(2,1)S(1)}, bf16[1040,128]{1,0:T(8,128)(2,1)S(1)}, s32[1,256]{1,0:T(1,128)S(1)}) custom-call(bf16[256,1024]{1,0:T(8,128)(2,1)S(1)} %copy-done, bf16[256,1024]{1,0:T(8,128)(2,1)S(1)} %collective-permute-done.mate_ref, ...), custom_call_target="tpu_custom_call" | custom-call | flops 268435456 | bytes 2097152 | tf_op jit(solution)/shard_map/pallas_call | solution.py:23
  4.9 2.7 %collective-permute-start.5 = (bf16[1040,128]{1,0:T(8,128)(2,1)S(1)}, bf16[1040,128]{1,0:T(8,128)(2,1)S(1)}, u32[]{:S(2)}, u32[]{:S(2)}) collective-permute-start(bf16[1040,128]{1,0:T(8,128)(2,1)S(1)} %get-tuple-element.20), channel_id=1, source_target_pairs={{0,8},{4,12},{8,0},{12,4},{16,24},{20,28},{24,16},{28,20},{1,9},{5... | collective-permute-start | bytes 798728 | tf_op jit(solution)/shard_map/ppermute | solution.py:254
  7.6 1.5 %collective-permute-start.6 = (bf16[1040,128]{1,0:T(8,128)(2,1)S(1)}, bf16[1040,128]{1,0:T(8,128)(2,1)S(1)}, u32[]{:S(2)}, u32[]{:S(2)}) collective-permute-start(bf16[1040,128]{1,0:T(8,128)(2,1)S(1)} %get-tuple-element.21), channel_id=1, source_target_pairs={{0,16},{4,20},{8,24},{12,28},{16,0},{20,4},{24,8},{28,12},{1,17},{... | collective-permute-start | bytes 798728 | tf_op jit(solution)/shard_map/ppermute | solution.py:254
  9.1 4.5 %collective-permute-start.2 = (bf16[1040,128]{1,0:T(8,128)(2,1)S(1)}, bf16[1040,128]{1,0:T(8,128)(2,1)S(1)}, u32[]{:S(2)}, u32[]{:S(2)}) collective-permute-start(bf16[1040,128]{1,0:T(8,128)(2,1)S(1)} %get-tuple-element.19.refs_0_), channel_id=1, source_target_pairs={{0,2},{7,5},{8,10},{15,13},{16,18},{23,21},{24,26},{31,29}} | collective-permute-start | bytes 798728 | tf_op jit(solution)/shard_map/ppermute | solution.py:274
  13.7 0.7 %collective-permute-start.3 = (bf16[1040,128]{1,0:T(8,128)(2,1)S(1)}, bf16[1040,128]{1,0:T(8,128)(2,1)S(1)}, u32[]{:S(2)}, u32[]{:S(2)}) collective-permute-start(bf16[1040,128]{1,0:T(8,128)(2,1)S(1)} %get-tuple-element.19.refs_0_), channel_id=1, source_target_pairs={{1,2},{6,5},{9,10},{14,13},{17,18},{22,21},{25,26},{30,29}} | collective-permute-start | bytes 798728 | tf_op jit(solution)/shard_map/ppermute | solution.py:274
  14.5 1.5 %collective-permute-done.6.refs_1_ = bf16[1040,128]{1,0:T(8,128)(2,1)S(1)} collective-permute-done((bf16[1040,128]{1,0:T(8,128)(2,1)S(1)}, bf16[1040,128]{1,0:T(8,128)(2,1)S(1)}, u32[]{:S(2)}, u32[]{:S(2)}) %collective-permute-start.6) | collective-permute-done | bytes 266272 | tf_op jit(solution)/shard_map/ppermute | solution.py:254
  16.0 4.5 %collective-permute-start.7 = (bf16[2080,128]{1,0:T(8,128)(2,1)S(1)}, bf16[2080,128]{1,0:T(8,128)(2,1)S(1)}, u32[]{:S(2)}, u32[]{:S(2)}) collective-permute-start(bf16[2080,128]{1,0:T(8,128)(2,1)S(1)} %shard_map.38.refs_4_), channel_id=1, source_target_pairs={{0,2},{7,5},{8,10},{15,13},{16,18},{23,21},{24,26},{31,29}} | collective-permute-start | bytes 1597448 | tf_op jit(solution)/shard_map/ppermute | solution.py:274
  20.6 0.7 %collective-permute-start.8 = (bf16[2080,128]{1,0:T(8,128)(2,1)S(1)}, bf16[2080,128]{1,0:T(8,128)(2,1)S(1)}, u32[]{:S(2)}, u32[]{:S(2)}) collective-permute-start(bf16[2080,128]{1,0:T(8,128)(2,1)S(1)} %shard_map.38.refs_4_), channel_id=1, source_target_pairs={{1,2},{6,5},{9,10},{14,13},{17,18},{22,21},{25,26},{30,29}} | collective-permute-start | bytes 1597448 | tf_op jit(solution)/shard_map/ppermute | solution.py:274
  21.3 0.7 %collective-permute-start.9 = (bf16[2080,128]{1,0:T(8,128)(2,1)S(1)}, bf16[2080,128]{1,0:T(8,128)(2,1)S(1)}, u32[]{:S(2)}, u32[]{:S(2)}) collective-permute-start(bf16[2080,128]{1,0:T(8,128)(2,1)S(1)} %shard_map.38.refs_4_), channel_id=1, source_target_pairs={{3,2},{4,5},{11,10},{12,13},{19,18},{20,21},{27,26},{28,29}} | collective-permute-start | bytes 1597448 | tf_op jit(solution)/shard_map/ppermute | solution.py:274
  22.0 1.6 %collective-permute-start.10 = (bf16[1040,128]{1,0:T(8,128)(2,1)S(1)}, bf16[1040,128]{1,0:T(8,128)(2,1)S(1)}, u32[]{:S(2)}, u32[]{:S(2)}) collective-permute-start(bf16[1040,128]{1,0:T(8,128)(2,1)S(1)} %get-tuple-element.26), channel_id=1, source_target_pairs={{0,24},{4,28},{8,16},{12,20},{16,8},{20,12},{24,0},{28,4},{1,25},{... | collective-permute-start | bytes 798728 | tf_op jit(solution)/shard_map/ppermute | solution.py:254
  23.5 0.7 %collective-permute-start.4 = (bf16[1040,128]{1,0:T(8,128)(2,1)S(1)}, bf16[1040,128]{1,0:T(8,128)(2,1)S(1)}, u32[]{:S(2)}, u32[]{:S(2)}) collective-permute-start(bf16[1040,128]{1,0:T(8,128)(2,1)S(1)} %get-tuple-element.19.refs_0_), channel_id=1, source_target_pairs={{3,2},{4,5},{11,10},{12,13},{19,18},{20,21},{27,26},{28,29}} | collective-permute-start | bytes 798728 | tf_op jit(solution)/shard_map/ppermute | solution.py:274
  24.2 6.1 %collective-permute-done.10.refs_0_ = bf16[1040,128]{1,0:T(8,128)(2,1)S(1)} collective-permute-done((bf16[1040,128]{1,0:T(8,128)(2,1)S(1)}, bf16[1040,128]{1,0:T(8,128)(2,1)S(1)}, u32[]{:S(2)}, u32[]{:S(2)}) %collective-permute-start.10) | collective-permute-done | bytes 266272 | tf_op jit(solution)/shard_map/ppermute | solution.py:254
  30.3 2.8 %collective-permute-start.11 = (bf16[1040,128]{1,0:T(8,128)(2,1)S(1)}, bf16[1040,128]{1,0:T(8,128)(2,1)S(1)}, u32[]{:S(2)}, u32[]{:S(2)}) collective-permute-start(bf16[1040,128]{1,0:T(8,128)(2,1)S(1)} %collective-permute-done.10.refs_0_), channel_id=1, source_target_pairs={{0,2},{7,5},{8,10},{15,13},{16,18},{23,21},{24,26},{31,29}} | collective-permute-start | bytes 798728 | tf_op jit(solution)/shard_map/ppermute | solution.py:274
  33.1 0.7 %collective-permute-start.12 = (bf16[1040,128]{1,0:T(8,128)(2,1)S(1)}, bf16[1040,128]{1,0:T(8,128)(2,1)S(1)}, u32[]{:S(2)}, u32[]{:S(2)}) collective-permute-start(bf16[1040,128]{1,0:T(8,128)(2,1)S(1)} %collective-permute-done.10.refs_0_), channel_id=1, source_target_pairs={{1,2},{6,5},{9,10},{14,13},{17,18},{22,21},{25,26},{30,29}} | collective-permute-start | bytes 798728 | tf_op jit(solution)/shard_map/ppermute | solution.py:274
  33.8 0.7 %collective-permute-start.13 = (bf16[1040,128]{1,0:T(8,128)(2,1)S(1)}, bf16[1040,128]{1,0:T(8,128)(2,1)S(1)}, u32[]{:S(2)}, u32[]{:S(2)}) collective-permute-start(bf16[1040,128]{1,0:T(8,128)(2,1)S(1)} %collective-permute-done.10.refs_0_), channel_id=1, source_target_pairs={{3,2},{4,5},{11,10},{12,13},{19,18},{20,21},{27,26},{28,29}} | collective-permute-start | bytes 798728 | tf_op jit(solution)/shard_map/ppermute | solution.py:274
  34.5 5.8 %shard_map.39 = (bf16[1536,1024]{1,0:T(8,128)(2,1)S(1)}, f32[1536,128]{1,0:T(8,128)S(1)}, f32[1,1536]{1,0:T(1,128)S(1)}, f32[8,1536]{1,0:T(8,128)S(1)}) custom-call(bf16[1040,128]{1,0:T(8,128)(2,1)S(1)} %get-tuple-element.19.refs_0_, bf16[1040,128]{1,0:T(8,128)(2,1)S(1)} %collective-permute-done.2.refs_1_, ...), custom_call_target="tpu_custom_call" | custom-call | flops 2415919104 | bytes 6291456 | tf_op jit(solution)/shard_map/pallas_call | solution.py:23
  40.4 3.5 %shard_map.40 = (f32[4,128]{1,0:T(4,128)S(1)}, f32[4,128]{1,0:T(4,128)S(1)}, f32[4,128]{1,0:T(4,128)S(1)}, f32[4,128]{1,0:T(4,128)S(1)}) custom-call(bf16[1536,1024]{1,0:T(8,128)(2,1)S(1)} %get-tuple-element.22.x_ref, f32[1536,128]{1,0:T(8,128)S(1)} %get-tuple-element.23.column_ref, f32[1,1536]{1,0:T(1,128)S(1)} %get-tuple-element.24.row_ref, ...), custom_call_target="tpu_custom_call" | custom-call | flops 2147483648 | bytes 4194304 | tf_op jit(solution)/shard_map/pallas_call | solution.py:23
  43.8 1.3 %collective-permute-start.14 = (f32[4,128]{1,0:T(4,128)S(1)}, f32[4,128]{1,0:T(4,128)S(1)}, u32[]{:S(2)}, u32[]{:S(2)}) collective-permute-start(f32[4,128]{1,0:T(4,128)S(1)} %get-tuple-element.28), channel_id=1, source_target_pairs={{2,0},{5,7},{10,8},{13,15},{18,16},{21,23},{26,24},{29,31}} | collective-permute-start | bytes 6152 | tf_op jit(solution)/shard_map/ppermute | solution.py:334
  45.1 0.7 %collective-permute-start.15 = (f32[4,128]{1,0:T(4,128)S(1)}, f32[4,128]{1,0:T(4,128)S(1)}, u32[]{:S(2)}, u32[]{:S(2)}) collective-permute-start(f32[4,128]{1,0:T(4,128)S(1)} %get-tuple-element.29), channel_id=1, source_target_pairs={{2,1},{5,6},{10,9},{13,14},{18,17},{21,22},{26,25},{29,30}} | collective-permute-start | bytes 6152 | tf_op jit(solution)/shard_map/ppermute | solution.py:334
  45.8 0.7 %collective-permute-start.16 = (f32[4,128]{1,0:T(4,128)S(1)}, f32[4,128]{1,0:T(4,128)S(1)}, u32[]{:S(2)}, u32[]{:S(2)}) collective-permute-start(f32[4,128]{1,0:T(4,128)S(1)} %get-tuple-element.30), channel_id=1, source_target_pairs={{2,3},{5,4},{10,11},{13,12},{18,19},{21,20},{26,27},{29,28}} | collective-permute-start | bytes 6152 | tf_op jit(solution)/shard_map/ppermute | solution.py:334
  46.5 8.8 %collective-permute-done.14 = f32[4,128]{1,0:T(4,128)S(1)} collective-permute-done((f32[4,128]{1,0:T(4,128)S(1)}, f32[4,128]{1,0:T(4,128)S(1)}, u32[]{:S(2)}, u32[]{:S(2)}) %collective-permute-start.14) | collective-permute-done | bytes 2080 | tf_op jit(solution)/shard_map/ppermute | solution.py:334
  55.3 0.6 collective-permute-start.17
  55.9 1.5 %collective-permute-start.18 = (f32[4,128]{1,0:T(4,128)S(1)}, f32[4,128]{1,0:T(4,128)S(1)}, u32[]{:S(2)}, u32[]{:S(2)}) collective-permute-start(f32[4,128]{1,0:T(4,128)S(1)} %add_select_fusion), channel_id=1, source_target_pairs={{0,16},{4,20},{8,24},{12,28},{16,0},{20,4},{24,8},{28,12},{1,17},{... | collective-permute-start | bytes 6152 | tf_op jit(solution)/shard_map/ppermute | solution.py:254
  57.4 1.4 %collective-permute-start.19 = (f32[4,128]{1,0:T(4,128)S(1)}, f32[4,128]{1,0:T(4,128)S(1)}, u32[]{:S(2)}, u32[]{:S(2)}) collective-permute-start(f32[4,128]{1,0:T(4,128)S(1)} %add_select_fusion), channel_id=1, source_target_pairs={{0,24},{4,28},{8,16},{12,20},{16,8},{20,12},{24,0},{28,4},{1,25},{... | collective-permute-start | bytes 6152 | tf_op jit(solution)/shard_map/ppermute | solution.py:254
  58.9 0.6 collective-permute-done.18
  59.5 2.4 %collective-permute-done.19 = f32[4,128]{1,0:T(4,128)S(1)} collective-permute-done((f32[4,128]{1,0:T(4,128)S(1)}, f32[4,128]{1,0:T(4,128)S(1)}, u32[]{:S(2)}, u32[]{:S(2)}) %collective-permute-start.19) | collective-permute-done | bytes 2080 | tf_op jit(solution)/shard_map/ppermute | solution.py:254
  62.4 0.8 %collective-permute-done.20.mate_ref = f32[4,128]{1,0:T(4,128)S(1)} collective-permute-done((f32[4,128]{1,0:T(4,128)S(1)}, f32[4,128]{1,0:T(4,128)S(1)}, u32[]{:S(2)}, u32[]{:S(2)}) %collective-permute-start.20) | collective-permute-done | bytes 2080 | tf_op jit(solution)/shard_map/ppermute | solution.py:257
  63.2 0.8 %shard_map.41 = f32[1,256]{1,0:T(1,128)} custom-call(s32[1,256]{1,0:T(1,128)S(1)} %get-tuple-element.18.pos_ref, f32[4,128]{1,0:T(4,128)S(1)} %pad_maximum_fusion.own_ref, f32[4,128]{1,0:T(4,128)S(1)} %collective-permute-done.20.mate_ref), custom_call_target="tpu_custom_call" | custom-call | flops 1000000 | bytes 100000 | tf_op jit(solution)/shard_map/pallas_call | solution.py:23
  (25 shorter events, 1.3 us)
Async XLA Ops:
  0.0 3.0 %collective-permute-start = (bf16[256,1024]{1,0:T(8,128)(2,1)}, bf16[256,1024]{1,0:T(8,128)(2,1)S(1)}, u32[]{:S(2)}, u32[]{:S(2)}) collective-permute-start(bf16[256,1024]{1,0:T(8,128)(2,1)} %own_ref.1), channel_id=1, source_target_pairs={{0,4},{4,0},{8,12},{12,8},{16,20},{20,16},{24,28},{28,24},{1,5},{5... | collective-permute-start | bytes 1572872 | tf_op jit(solution)/shard_map/ppermute | solution.py:257
  1.9 1.2 %collective-permute-start.1 = (s32[1,256]{1,0:T(1,128)S(1)}, s32[1,256]{1,0:T(1,128)S(1)}, u32[]{:S(2)}, u32[]{:S(2)}) collective-permute-start(s32[1,256]{1,0:T(1,128)S(1)} %bitcast.3), channel_id=1, source_target_pairs={{0,4},{4,0},{8,12},{12,8},{16,20},{20,16},{24,28},{28,24},{1,5},{5... | collective-permute-start | bytes 3080 | tf_op jit(solution)/shard_map/ppermute | solution.py:257
  3.0 1.0 %copy-start = (bf16[256,1024]{1,0:T(8,128)(2,1)S(1)}, bf16[256,1024]{1,0:T(8,128)(2,1)}, u32[]{:S(2)}) copy-start(bf16[256,1024]{1,0:T(8,128)(2,1)} %own_ref.1) | copy-start | bytes 1572868
  4.9 9.6 %collective-permute-start.5 = (bf16[1040,128]{1,0:T(8,128)(2,1)S(1)}, bf16[1040,128]{1,0:T(8,128)(2,1)S(1)}, u32[]{:S(2)}, u32[]{:S(2)}) collective-permute-start(bf16[1040,128]{1,0:T(8,128)(2,1)S(1)} %get-tuple-element.20), channel_id=1, source_target_pairs={{0,8},{4,12},{8,0},{12,4},{16,24},{20,28},{24,16},{28,20},{1,9},{5... | collective-permute-start | bytes 798728 | tf_op jit(solution)/shard_map/ppermute | solution.py:254
  7.6 8.4 %collective-permute-start.6 = (bf16[1040,128]{1,0:T(8,128)(2,1)S(1)}, bf16[1040,128]{1,0:T(8,128)(2,1)S(1)}, u32[]{:S(2)}, u32[]{:S(2)}) collective-permute-start(bf16[1040,128]{1,0:T(8,128)(2,1)S(1)} %get-tuple-element.21), channel_id=1, source_target_pairs={{0,16},{4,20},{8,24},{12,28},{16,0},{20,4},{24,8},{28,12},{1,17},{... | collective-permute-start | bytes 798728 | tf_op jit(solution)/shard_map/ppermute | solution.py:254
  9.1 12.8 %collective-permute-start.2 = (bf16[1040,128]{1,0:T(8,128)(2,1)S(1)}, bf16[1040,128]{1,0:T(8,128)(2,1)S(1)}, u32[]{:S(2)}, u32[]{:S(2)}) collective-permute-start(bf16[1040,128]{1,0:T(8,128)(2,1)S(1)} %get-tuple-element.19.refs_0_), channel_id=1, source_target_pairs={{0,2},{7,5},{8,10},{15,13},{16,18},{23,21},{24,26},{31,29}} | collective-permute-start | bytes 798728 | tf_op jit(solution)/shard_map/ppermute | solution.py:274
  13.7 9.9 %collective-permute-start.3 = (bf16[1040,128]{1,0:T(8,128)(2,1)S(1)}, bf16[1040,128]{1,0:T(8,128)(2,1)S(1)}, u32[]{:S(2)}, u32[]{:S(2)}) collective-permute-start(bf16[1040,128]{1,0:T(8,128)(2,1)S(1)} %get-tuple-element.19.refs_0_), channel_id=1, source_target_pairs={{1,2},{6,5},{9,10},{14,13},{17,18},{22,21},{25,26},{30,29}} | collective-permute-start | bytes 798728 | tf_op jit(solution)/shard_map/ppermute | solution.py:274
  16.0 17.8 %collective-permute-start.7 = (bf16[2080,128]{1,0:T(8,128)(2,1)S(1)}, bf16[2080,128]{1,0:T(8,128)(2,1)S(1)}, u32[]{:S(2)}, u32[]{:S(2)}) collective-permute-start(bf16[2080,128]{1,0:T(8,128)(2,1)S(1)} %shard_map.38.refs_4_), channel_id=1, source_target_pairs={{0,2},{7,5},{8,10},{15,13},{16,18},{23,21},{24,26},{31,29}} | collective-permute-start | bytes 1597448 | tf_op jit(solution)/shard_map/ppermute | solution.py:274
  20.6 14.0 %collective-permute-start.8 = (bf16[2080,128]{1,0:T(8,128)(2,1)S(1)}, bf16[2080,128]{1,0:T(8,128)(2,1)S(1)}, u32[]{:S(2)}, u32[]{:S(2)}) collective-permute-start(bf16[2080,128]{1,0:T(8,128)(2,1)S(1)} %shard_map.38.refs_4_), channel_id=1, source_target_pairs={{1,2},{6,5},{9,10},{14,13},{17,18},{22,21},{25,26},{30,29}} | collective-permute-start | bytes 1597448 | tf_op jit(solution)/shard_map/ppermute | solution.py:274
  21.3 13.3 %collective-permute-start.9 = (bf16[2080,128]{1,0:T(8,128)(2,1)S(1)}, bf16[2080,128]{1,0:T(8,128)(2,1)S(1)}, u32[]{:S(2)}, u32[]{:S(2)}) collective-permute-start(bf16[2080,128]{1,0:T(8,128)(2,1)S(1)} %shard_map.38.refs_4_), channel_id=1, source_target_pairs={{3,2},{4,5},{11,10},{12,13},{19,18},{20,21},{27,26},{28,29}} | collective-permute-start | bytes 1597448 | tf_op jit(solution)/shard_map/ppermute | solution.py:274
  22.0 8.4 %collective-permute-start.10 = (bf16[1040,128]{1,0:T(8,128)(2,1)S(1)}, bf16[1040,128]{1,0:T(8,128)(2,1)S(1)}, u32[]{:S(2)}, u32[]{:S(2)}) collective-permute-start(bf16[1040,128]{1,0:T(8,128)(2,1)S(1)} %get-tuple-element.26), channel_id=1, source_target_pairs={{0,24},{4,28},{8,16},{12,20},{16,8},{20,12},{24,0},{28,4},{1,25},{... | collective-permute-start | bytes 798728 | tf_op jit(solution)/shard_map/ppermute | solution.py:254
  23.5 9.6 %collective-permute-start.4 = (bf16[1040,128]{1,0:T(8,128)(2,1)S(1)}, bf16[1040,128]{1,0:T(8,128)(2,1)S(1)}, u32[]{:S(2)}, u32[]{:S(2)}) collective-permute-start(bf16[1040,128]{1,0:T(8,128)(2,1)S(1)} %get-tuple-element.19.refs_0_), channel_id=1, source_target_pairs={{3,2},{4,5},{11,10},{12,13},{19,18},{20,21},{27,26},{28,29}} | collective-permute-start | bytes 798728 | tf_op jit(solution)/shard_map/ppermute | solution.py:274
  30.3 10.0 %collective-permute-start.11 = (bf16[1040,128]{1,0:T(8,128)(2,1)S(1)}, bf16[1040,128]{1,0:T(8,128)(2,1)S(1)}, u32[]{:S(2)}, u32[]{:S(2)}) collective-permute-start(bf16[1040,128]{1,0:T(8,128)(2,1)S(1)} %collective-permute-done.10.refs_0_), channel_id=1, source_target_pairs={{0,2},{7,5},{8,10},{15,13},{16,18},{23,21},{24,26},{31,29}} | collective-permute-start | bytes 798728 | tf_op jit(solution)/shard_map/ppermute | solution.py:274
  33.1 7.2 %collective-permute-start.12 = (bf16[1040,128]{1,0:T(8,128)(2,1)S(1)}, bf16[1040,128]{1,0:T(8,128)(2,1)S(1)}, u32[]{:S(2)}, u32[]{:S(2)}) collective-permute-start(bf16[1040,128]{1,0:T(8,128)(2,1)S(1)} %collective-permute-done.10.refs_0_), channel_id=1, source_target_pairs={{1,2},{6,5},{9,10},{14,13},{17,18},{22,21},{25,26},{30,29}} | collective-permute-start | bytes 798728 | tf_op jit(solution)/shard_map/ppermute | solution.py:274
  33.8 6.5 %collective-permute-start.13 = (bf16[1040,128]{1,0:T(8,128)(2,1)S(1)}, bf16[1040,128]{1,0:T(8,128)(2,1)S(1)}, u32[]{:S(2)}, u32[]{:S(2)}) collective-permute-start(bf16[1040,128]{1,0:T(8,128)(2,1)S(1)} %collective-permute-done.10.refs_0_), channel_id=1, source_target_pairs={{3,2},{4,5},{11,10},{12,13},{19,18},{20,21},{27,26},{28,29}} | collective-permute-start | bytes 798728 | tf_op jit(solution)/shard_map/ppermute | solution.py:274
  43.8 11.4 %collective-permute-start.14 = (f32[4,128]{1,0:T(4,128)S(1)}, f32[4,128]{1,0:T(4,128)S(1)}, u32[]{:S(2)}, u32[]{:S(2)}) collective-permute-start(f32[4,128]{1,0:T(4,128)S(1)} %get-tuple-element.28), channel_id=1, source_target_pairs={{2,0},{5,7},{10,8},{13,15},{18,16},{21,23},{26,24},{29,31}} | collective-permute-start | bytes 6152 | tf_op jit(solution)/shard_map/ppermute | solution.py:334
  45.1 10.1 %collective-permute-start.15 = (f32[4,128]{1,0:T(4,128)S(1)}, f32[4,128]{1,0:T(4,128)S(1)}, u32[]{:S(2)}, u32[]{:S(2)}) collective-permute-start(f32[4,128]{1,0:T(4,128)S(1)} %get-tuple-element.29), channel_id=1, source_target_pairs={{2,1},{5,6},{10,9},{13,14},{18,17},{21,22},{26,25},{29,30}} | collective-permute-start | bytes 6152 | tf_op jit(solution)/shard_map/ppermute | solution.py:334
  45.8 9.5 %collective-permute-start.16 = (f32[4,128]{1,0:T(4,128)S(1)}, f32[4,128]{1,0:T(4,128)S(1)}, u32[]{:S(2)}, u32[]{:S(2)}) collective-permute-start(f32[4,128]{1,0:T(4,128)S(1)} %get-tuple-element.30), channel_id=1, source_target_pairs={{2,3},{5,4},{10,11},{13,12},{18,19},{21,20},{26,27},{29,28}} | collective-permute-start | bytes 6152 | tf_op jit(solution)/shard_map/ppermute | solution.py:334
  55.3 3.7 %collective-permute-start.17 = (f32[4,128]{1,0:T(4,128)S(1)}, f32[4,128]{1,0:T(4,128)S(1)}, u32[]{:S(2)}, u32[]{:S(2)}) collective-permute-start(f32[4,128]{1,0:T(4,128)S(1)} %add_select_fusion), channel_id=1, source_target_pairs={{0,8},{4,12},{8,0},{12,4},{16,24},{20,28},{24,16},{28,20},{1,9},{5... | collective-permute-start | bytes 6152 | tf_op jit(solution)/shard_map/ppermute | solution.py:254
  55.9 3.6 %collective-permute-start.18 = (f32[4,128]{1,0:T(4,128)S(1)}, f32[4,128]{1,0:T(4,128)S(1)}, u32[]{:S(2)}, u32[]{:S(2)}) collective-permute-start(f32[4,128]{1,0:T(4,128)S(1)} %add_select_fusion), channel_id=1, source_target_pairs={{0,16},{4,20},{8,24},{12,28},{16,0},{20,4},{24,8},{28,12},{1,17},{... | collective-permute-start | bytes 6152 | tf_op jit(solution)/shard_map/ppermute | solution.py:254
  57.4 4.5 %collective-permute-start.19 = (f32[4,128]{1,0:T(4,128)S(1)}, f32[4,128]{1,0:T(4,128)S(1)}, u32[]{:S(2)}, u32[]{:S(2)}) collective-permute-start(f32[4,128]{1,0:T(4,128)S(1)} %add_select_fusion), channel_id=1, source_target_pairs={{0,24},{4,28},{8,16},{12,20},{16,8},{20,12},{24,0},{28,4},{1,25},{... | collective-permute-start | bytes 6152 | tf_op jit(solution)/shard_map/ppermute | solution.py:254
  61.9 1.3 %collective-permute-start.20 = (f32[4,128]{1,0:T(4,128)S(1)}, f32[4,128]{1,0:T(4,128)S(1)}, u32[]{:S(2)}, u32[]{:S(2)}) collective-permute-start(f32[4,128]{1,0:T(4,128)S(1)} %pad_maximum_fusion.own_ref), channel_id=1, source_target_pairs={{0,4},{4,0},{8,12},{12,8},{16,20},{20,16},{24,28},{28,24},{1,5},{5... | collective-permute-start | bytes 6152 | tf_op jit(solution)/shard_map/ppermute | solution.py:257

commit v2 on v1

v2 whole, which is shorter than its diff:
```python
import functools

import jax
import jax.numpy as jnp
from jax import lax
from jax.experimental import pallas as pl
from jax.experimental.pallas import tpu as pltpu
from jax.sharding import PartitionSpec as P


LANES = 128
META = 16
VMEM = pl.BlockSpec(memory_space=pltpu.VMEM)
F32 = jnp.float32
BF16 = jnp.bfloat16


def nt(left, right):
    return lax.dot_general(left, right, (((1,), (1,)), ((), ())), preferred_element_type=F32)


def call(body, outs, operands, flops, moved, limit, scratch=(), spec=VMEM):
    return pl.pallas_call(
        body,
        out_shape=outs,
        in_specs=[spec] * len(operands),
        out_specs=jax.tree.map(lambda _: VMEM, outs),
        scratch_shapes=list(scratch),
        cost_estimate=pl.CostEstimate(flops=flops, bytes_accessed=moved, transcendentals=0),
        compiler_params=pltpu.CompilerParams(vmem_limit_bytes=limit),
    )(*operands)


def gathered(emb_ref, dest_ref, rank_ref, chip, core, chips, cap):
    rows = emb_ref.shape[0]
    clusters = max(16, 2 * chips)
    values = emb_ref[...].astype(F32)
    norm = lax.rsqrt(jnp.sum(values * values, axis=1, keepdims=True) + 1e-06)
    unit = (values * norm).astype(BF16)
    dest, rank = dest_ref[...], rank_ref[...]
    onehot = (lax.broadcasted_iota(jnp.int32, (clusters, rows), 0) == dest).astype(F32)
    row = lax.broadcasted_iota(jnp.int32, (rows, rows), 0)
    column = lax.broadcasted_iota(jnp.int32, (rows, rows), 1)
    before = (row < column).astype(F32).astype(BF16)
    count = jnp.dot(onehot.astype(BF16), before, preferred_element_type=F32)
    slot = jnp.sum(count * onehot, axis=0, keepdims=True).astype(jnp.int32)
    where = ((dest >> 1) ^ chip) * cap + slot
    pos = jnp.where((dest & 1) == core, where, -1)
    pick = lax.broadcasted_iota(jnp.int32, (chips * cap, rows), 0) == pos
    pick = pick.astype(F32).astype(BF16)
    digits = lax.broadcasted_iota(jnp.int32, (META, rows), 0)
    digits = jnp.where(
        digits == 0, rank >> 8, jnp.where(digits == 1, rank & 255, jnp.where(digits == 2, 1, 0))
    )
    digits = nt(digits.astype(F32).astype(BF16), pick)
    top = lax.broadcasted_iota(jnp.int32, digits.shape, 0) == 0
    digits = jnp.where(top & (digits[2:3, :] < 0.5), 256.0, digits)
    packed = jnp.dot(pick, unit, preferred_element_type=F32).astype(BF16)
    return packed, digits, where, dest


def own_body(cap, chips, emb_hbm, dest_hbm, rank_hbm, *refs):
    packed_ref, digits_ref, pos_ref, emb_ref, dest_ref, rank_ref, sems = refs
    copies = [
        pltpu.make_async_copy(source, target, sems.at[i])
        for i, (source, target) in enumerate(
            ((emb_hbm, emb_ref), (dest_hbm, dest_ref), (rank_hbm, rank_ref))
        )
    ]
    for copy in copies:
        copy.start()
    for copy in copies:
        copy.wait()
    group = lax.axis_index("group")
    packed, digits, where, dest = gathered(
        emb_ref, dest_ref, rank_ref, group >> 1, group & 1, chips, cap
    )
    packed_ref[...] = packed
    digits_ref[...] = digits
    pos_ref[...] = where * 2 + ((dest & 1) ^ (group & 1))


def pack_body(cap, chips, emb_ref, dest_ref, rank_ref, own, own_digits, *refs):
    group = lax.axis_index("group")
    pieces = emb_ref.shape[1] // LANES
    mate, mate_digits, _, _ = gathered(
        emb_ref, dest_ref, rank_ref, group >> 1, group & 1, chips, cap
    )
    for s in range(chips):
        part = slice(s * cap, (s + 1) * cap)
        for k in range(pieces):
            lanes = slice(k * LANES, (k + 1) * LANES)
            refs[s][k * LANES : k * LANES + cap, :] = own[part, lanes]
            refs[s][k * LANES + cap : (k + 1) * LANES, :] = mate[part, lanes]
        refs[s][pieces * LANES : pieces * LANES + META, :] = jnp.concatenate(
            [own_digits[:, part], mate_digits[:, part]], axis=1
        ).astype(BF16)


def join_body(*refs):
    out_ref, base = refs[-1], 0
    for ref in refs[:-1]:
        out_ref[base : base + ref.shape[0], :] = ref[...]
        base += ref.shape[0]


def unfold(refs, pieces, x_ref, column_ref, row_ref):
    size = pieces * LANES + META
    base = 0
    for ref in refs:
        for b in range(ref.shape[0] // size):
            rows = slice(base, base + LANES)
            for k in range(pieces):
                x_ref[rows, k * LANES : (k + 1) * LANES] = ref[
                    b * size + k * LANES : b * size + (k + 1) * LANES, :
                ]
            meta = ref[b * size + pieces * LANES : (b + 1) * size, :].astype(F32)
            rank = meta[0:1, :] * 256.0 + meta[1:2, :]
            row_ref[:, rows] = rank
            column_ref[rows, :] = jnp.transpose(jnp.broadcast_to(rank, (LANES, LANES)))
            base += LANES


def wide_max(scores):
    return jnp.max(scores.reshape(-1, 8, scores.shape[1]), axis=0)


def lane_max(scores):
    parts = [scores[:, i : i + LANES] for i in range(0, scores.shape[1], LANES)]
    return functools.reduce(jnp.maximum, parts)


def across(column, width):
    return jnp.concatenate([column] * (width // LANES), axis=1)


def tile_for(count):
    return next(t for t in (512, 256, 128) if count % t == 0)


def fold(keys_ref, rank_ref, best_ref, side_ref, query_ref, query_rank, symmetric):
    tall, wide = tile_for(keys_ref.shape[0]), tile_for(query_ref.shape[0])

    def outer(i, _):
        mine = pl.ds(pl.multiple_of(i * wide, wide), wide)

        def inner(j, _):
            keys = pl.ds(pl.multiple_of(j * tall, tall), tall)
            scores = nt(keys_ref[keys, :], query_ref[mine, :])
            earlier = across(rank_ref[keys, :], wide) < query_rank[:, mine]
            best_ref[:, mine] = jnp.maximum(
                best_ref[:, mine], wide_max(jnp.where(earlier, scores, -1.0))
            )
            if symmetric:
                side_ref[keys, :] = jnp.maximum(
                    side_ref[keys, :], lane_max(jnp.where(earlier, -1.0, scores))
                )
            return 0

        loop(keys_ref.shape[0] // tall, inner)
        return 0

    loop(query_ref.shape[0] // wide, outer)


def loop(count, body):
    if count == 1:
        body(0, 0)
    else:
        lax.fori_loop(0, count, body, 0)


def stage_body(pieces, olds, many, places, *refs):
    refs = list(refs)

    def take(n):
        taken = refs[:n]
        del refs[:n]
        return taken

    xs, rows, blocks = take(olds), take(olds), take(many)
    found = take(sum(range(olds + 1))) if places else []
    if places:
        outs = take(len(places))
        news, (x_ref, row_ref, best_ref) = take(olds), take(3)
    else:
        x_ref, row_ref, best_ref = take(3)
        news = take(olds)
    column_ref, side_ref = take(2)
    unfold(blocks, pieces, x_ref, column_ref, row_ref)
    best_ref[...] = jnp.full(best_ref.shape, -1.0, F32)
    side_ref[...] = jnp.full(side_ref.shape, -1.0, F32)
    for x, row, new in zip(xs, rows, news):
        new[...] = jnp.full(new.shape, -1.0, F32)
        fold(x_ref, column_ref, new, side_ref, x, row, True)
    fold(x_ref, column_ref, best_ref, side_ref, x_ref, row_ref, False)
    if not places:
        for i in range(0, x_ref.shape[0], LANES):
            side = jnp.transpose(side_ref[i : i + LANES, :])
            best_ref[:, i : i + LANES] = jnp.maximum(best_ref[:, i : i + LANES], wide_max(side))
        return
    for out, place in zip(outs, places):
        for row, (stage, block) in enumerate(place):
            lanes = slice(block * LANES, (block + 1) * LANES)
            if stage == olds:
                side = jnp.transpose(side_ref[lanes, :])
                best = jnp.maximum(best_ref[:, lanes], wide_max(side))
            else:
                best = news[stage][:, lanes]
                for later in range(stage, olds):
                    best = jnp.maximum(best, found[sum(range(later + 1)) + stage][:, lanes])
            out[row : row + 1, :] = jnp.max(best, axis=0, keepdims=True)


def final_body(cap, chips, pos_ref, own_ref, mate_ref, out_ref):
    rows = pos_ref.shape[1]
    pos = pos_ref[...]
    other, where = pos & 1, pos >> 1
    chip, slot = where // cap, where % cap
    place = lax.broadcasted_iota(jnp.int32, (LANES, rows), 0)
    pick = (place == slot + cap * other).astype(F32)
    table = jnp.concatenate([own_ref[...], mate_ref[...]], axis=0)
    got = lax.dot_general(
        table,
        pick,
        (((1,), (0,)), ((), ())),
        precision=lax.Precision.HIGHEST,
        preferred_element_type=F32,
    )
    mine = lax.broadcasted_iota(jnp.int32, (2 * chips, rows), 0) == chip + chips * other
    out_ref[...] = jnp.sum(jnp.where(mine, got, 0.0), axis=0, keepdims=True)


def chunks_of(chips):
    away = list(range(1, chips))
    cuts = [len(away) * i // 3 for i in range(4)]
    return [[0]] + [away[a:b] for a, b in zip(cuts, cuts[1:])]


def on_device(embeddings, dest_group, order_rank):
    rows, width = embeddings.shape
    groups = lax.axis_size("group")
    planes = lax.axis_size("blk")
    chips, half = groups // 2, planes // 2
    cap = rows // 4
    pieces = width // LANES
    size = pieces * LANES + META
    group, plane = lax.axis_index("group"), lax.axis_index("blk")

    def blocks(n):
        return jax.ShapeDtypeStruct((n * size, LANES), BF16)

    def floats(*shape):
        return jax.ShapeDtypeStruct(shape, F32)

    def to_chip(value, s):
        return lax.ppermute(value, "group", [(i, i ^ (2 * s)) for i in range(groups)])

    def to_core(value):
        return lax.ppermute(value, "group", [(i, i ^ 1) for i in range(groups)])

    meet = [half, half - 1]
    sources = [[z for z in range(planes) if z != half]]
    sources.append([planes - 1 - z for z in sources[0]])

    def meeting(step, back=False):
        pairs = []
        for g in range(groups):
            there = g * planes + meet[g & 1]
            here = g * planes + sources[g & 1][step]
            pairs.append((there, here) if back else (here, there))
        return pairs

    def gather(value):
        arrived = [value]
        for step in range(planes - 1):
            arrived.append(lax.ppermute(value, ("group", "blk"), meeting(step)))
        return arrived

    dest, rank = dest_group.reshape(1, rows), order_rank.reshape(1, rows)
    mate = to_core(embeddings)
    mate_dest, mate_rank = to_core(dest), to_core(rank)
    flops = 2 * chips * cap * rows * width
    own = call(
        functools.partial(own_body, cap, chips),
        [
            jax.ShapeDtypeStruct((chips * cap, width), BF16),
            floats(META, chips * cap),
            jax.ShapeDtypeStruct((1, rows), jnp.int32),
        ],
        [embeddings, dest, rank],
        flops,
        4 * rows * width,
        16 << 20,
        scratch=[
            pltpu.VMEM((rows, width), BF16),
            pltpu.VMEM((1, rows), jnp.int32),
            pltpu.VMEM((1, rows), jnp.int32),
            pltpu.SemaphoreType.DMA((3,)),
        ],
        spec=pl.BlockSpec(memory_space=pltpu.HBM),
    )
    packed = call(
        functools.partial(pack_body, cap, chips),
        [blocks(1)] * chips,
        [mate, mate_dest, mate_rank, own[0], own[1]],
        flops,
        8 * rows * width,
        16 << 20,
    )
    pos = own[2]
    sent = [packed[0]]
    for s in range(1, chips):
        sent.append(to_chip(packed[s], s))

    def join(arrays):
        if len(arrays) == 1:
            return arrays[0]
        total = sum(a.shape[0] for a in arrays)
        moved = 4 * total * LANES
        out = jax.ShapeDtypeStruct((total, LANES), BF16)
        return call(join_body, out, arrays, 1000, moved, 2 * moved)

    chunks = chunks_of(chips)
    arrived = []
    for chunk in chunks:
        arrived.append(gather(join([sent[s] for s in chunk])))
    stages = [[(c, p) for p in range(planes)] for c in range(len(chunks) - 1)]
    last = [(len(chunks) - 1, p) for p in range(planes)]
    stages += [last[:1] + last[1 + half :], last[1 : 1 + half]]
    places = [[None] * chips for _ in range(planes)]
    for i, stage in enumerate(stages):
        block = 0
        for c, p in stage:
            for s in chunks[c]:
                places[p][s] = (i, block)
                block += 1
    xs, ranks, found = [], [], []
    for i, stage in enumerate(stages):
        n = sum(len(chunks[c]) for c, _ in stage) * LANES
        flops = 2 * n * width * (n + sum(x.shape[0] for x in xs))
        made = [((n, width), BF16), ((1, n), F32), ((8, n), F32)]
        kept = [((8, x.shape[0]), F32) for x in xs]
        spare = [pltpu.VMEM((n, LANES), F32)] * 2
        operands = xs + ranks + [arrived[c][p] for c, p in stage]
        if i == len(stages) - 1:
            operands += found
            outs = [floats(chips, LANES)] * planes
            spare = [pltpu.VMEM(*m) for m in kept + made] + spare
        else:
            outs = [jax.ShapeDtypeStruct(*m) for m in made + kept]
        best = call(
            functools.partial(
                stage_body, pieces, i, len(stage), places if i == len(stages) - 1 else None
            ),
            outs,
            operands,
            flops,
            2 * width * (n + sum(x.shape[0] for x in xs)),
            6 * width * 2 * n + (12 << 20),
            scratch=spare,
        )
        if i < len(stages) - 1:
            xs.append(best[0])
            ranks.append(best[1])
            found += best[3:] + best[2:3]
    returned = [
        lax.ppermute(best[1 + step], ("group", "blk"), meeting(step, back=True))
        for step in range(planes - 1)
    ]
    at_meeting = plane == jnp.where((group & 1) == 0, half, half - 1)
    mine = jnp.where(at_meeting, best[0], functools.reduce(jnp.add, returned))
    rows_of = {(0, s): mine[s : s + 1] for s in range(chips)}
    for step in range(chips.bit_length() - 1):
        bit = 1 << step
        keys = sorted(key for key in rows_of if key[1] & bit)
        got = to_chip(jnp.concatenate([rows_of.pop(key) for key in keys], axis=0), bit)
        for i, (t, s) in enumerate(keys):
            rows_of[t ^ bit, s ^ bit] = got[i : i + 1]
    table = jnp.concatenate([rows_of[t, 0] for t in range(chips)], axis=0)
    result = call(
        functools.partial(final_body, cap, chips),
        floats(1, rows),
        [pos, table, to_core(table)],
        1000000,
        100000,
        4 << 20,
    )
    return result.reshape(rows)


def solution(mesh):
    placed = (P(("group", "blk"), None), P(("group", "blk"), None), P(("group", "blk")))

    return jax.shard_map(
        on_device, mesh=mesh, in_specs=placed, out_specs=P(("group", "blk")), check_vma=False
    )
```

time: 64.4 us -> 62.1 us (0.964)
  starting transfers between devices: 28.8 us -> 36.3 us
  waiting for transfers between devices: 21.6 us -> 14.7 us
  Pallas kernels: 10.9 us -> 8.88 us
  other arithmetic: 1.38 us -> 0.03 us
    ppermute x9 -> x12, starting transfers between devices: 15.9 us -> 23.6 us  [gather(): arrived.append(lax.ppermute(value, ('group', 'blk'), meeting(step)))]
    ppermute x3, waiting for transfers between devices: 8.8 us -> 5.67 us  [on_device(): lax.ppermute(best[1 + step], ('group', 'blk'), meeting(step, back=True))]
    ppermute x6 -> x5, waiting for transfers between devices: 10.8 us -> 7.81 us  [to_chip(): return lax.ppermute(value, 'group', [(i, i ^ 2 * s) for i in range(groups)])]
    pallas_call x5 -> x8, Pallas kernels: 10.9 us -> 8.88 us  [call(): pl.pallas_call(body, out_shape=outs, in_specs=[spec] * len(operands), out...]
    ppermute x3 -> x4, waiting for transfers between devices: 1.97 us -> 1.16 us  [to_core(): return lax.ppermute(value, 'group', [(i, i ^ 1) for i in range(groups)])]
    ppermute x6 -> x5, starting transfers between devices: 9.34 us -> 8.56 us  [to_chip(): return lax.ppermute(value, 'group', [(i, i ^ 2 * s) for i in range(groups)])]
    or x1 -> x0, other arithmetic: 0.68 us -> none  [on_device(): code = dest_group.reshape(1, rows) << 16 | order_rank.reshape(1, rows)]
    shift_left x1 -> x0, other arithmetic: 0.68 us -> none  [on_device(): code = dest_group.reshape(1, rows) << 16 | order_rank.reshape(1, rows)]
  transfers between devices with their start and end apart: 21 -> 24, of which waited for: 9 -> 5; matrix products, arithmetic and copies ran while one was open for 2% -> 0% of each run, Pallas kernels for 9% -> 10%
where the time goes in v2:
time: 62.1 us; the launch traced here: 61.6 us
  starting transfers between devices  36.3 us (58%)
  waiting for transfers between devices  14.7 us (24%)
  Pallas kernels  8.88 us (14%)
  local copies, waits for them, and re-layouts  1.42 us (2%)
    ppermute x12, starting transfers between devices, gather(): arrived.append(lax.ppermute(value, ('group', 'blk'), meeting(step)))  23.6 us
    pallas_call x8, Pallas kernels, call(): pl.pallas_call(body, out_shape=outs, in_specs=[spec] * len(operands), out...  8.88 us
    ppermute x5, starting transfers between devices, to_chip(): return lax.ppermute(value, 'group', [(i, i ^ 2 * s) for i in range(groups)])  8.56 us
    ppermute x5, waiting for transfers between devices, to_chip(): return lax.ppermute(value, 'group', [(i, i ^ 2 * s) for i in range(groups)])  7.81 us
    ppermute x3, waiting for transfers between devices, on_device(): lax.ppermute(best[1 + step], ('group', 'blk'), meeting(step, back=True))  5.67 us
    ppermute x3, starting transfers between devices, on_device(): lax.ppermute(best[1 + step], ('group', 'blk'), meeting(step, back=True))  2.62 us
    ppermute x4, starting transfers between devices, to_core(): return lax.ppermute(value, 'group', [(i, i ^ 1) for i in range(groups)])  1.55 us
    unnamed x6, local copies, waits for them, and re-layouts  1.41 us
  transfers between devices with their start and end apart: 24, of which 5 were waited for; matrix products, arithmetic and copies ran while one was open for 0% of the time, Pallas kernels for 10%

profile of v2, /device:TPU:0, one launch (start us, length us, event | category | flops | bytes accessed | tf_op | source)
XLA Modules:
  0.0 61.6 jit_solution(10677641173325460375)
XLA Ops:
  1.9 1.0 %copy-done = bf16[256,1024]{1,0:T(8,128)(2,1)S(1)} copy-done((bf16[256,1024]{1,0:T(8,128)(2,1)S(1)}, bf16[256,1024]{1,0:T(8,128)(2,1)}, u32[]{:S(2)}) %copy-start) | copy-done | bytes 524312
  2.9 0.6 shard_map.37
  4.1 5.5 %collective-permute-start.3 = (bf16[1040,128]{1,0:T(8,128)(2,1)S(1)}, bf16[1040,128]{1,0:T(8,128)(2,1)S(1)}, u32[]{:S(2)}, u32[]{:S(2)}) collective-permute-start(bf16[1040,128]{1,0:T(8,128)(2,1)S(1)} %get-tuple-element.37.refs_0_), channel_id=1, source_target_pairs={{0,2},{7,5},{8,10},{15,13},{16,18},{23,21},{24,26},{31,29}} | collective-permute-start | bytes 798728 | tf_op jit(solution)/shard_map/ppermute | solution.py:277
  9.6 1.6 %collective-permute-start.6 = (bf16[1040,128]{1,0:T(8,128)(2,1)S(1)}, bf16[1040,128]{1,0:T(8,128)(2,1)S(1)}, u32[]{:S(2)}, u32[]{:S(2)}) collective-permute-start(bf16[1040,128]{1,0:T(8,128)(2,1)S(1)} %get-tuple-element.40), channel_id=1, source_target_pairs={{0,8},{4,12},{8,0},{12,4},{16,24},{20,28},{24,16},{28,20},{1,9},{5... | collective-permute-start | bytes 798728 | tf_op jit(solution)/shard_map/ppermute | solution.py:257
  11.1 0.7 %collective-permute-start.4 = (bf16[1040,128]{1,0:T(8,128)(2,1)S(1)}, bf16[1040,128]{1,0:T(8,128)(2,1)S(1)}, u32[]{:S(2)}, u32[]{:S(2)}) collective-permute-start(bf16[1040,128]{1,0:T(8,128)(2,1)S(1)} %get-tuple-element.37.refs_0_), channel_id=1, source_target_pairs={{1,2},{6,5},{9,10},{14,13},{17,18},{22,21},{25,26},{30,29}} | collective-permute-start | bytes 798728 | tf_op jit(solution)/shard_map/ppermute | solution.py:277
  11.8 0.7 %collective-permute-start.5 = (bf16[1040,128]{1,0:T(8,128)(2,1)S(1)}, bf16[1040,128]{1,0:T(8,128)(2,1)S(1)}, u32[]{:S(2)}, u32[]{:S(2)}) collective-permute-start(bf16[1040,128]{1,0:T(8,128)(2,1)S(1)} %get-tuple-element.37.refs_0_), channel_id=1, source_target_pairs={{3,2},{4,5},{11,10},{12,13},{19,18},{20,21},{27,26},{28,29}} | collective-permute-start | bytes 798728 | tf_op jit(solution)/shard_map/ppermute | solution.py:277
  12.5 1.6 %collective-permute-start.10 = (bf16[1040,128]{1,0:T(8,128)(2,1)S(1)}, bf16[1040,128]{1,0:T(8,128)(2,1)S(1)}, u32[]{:S(2)}, u32[]{:S(2)}) collective-permute-start(bf16[1040,128]{1,0:T(8,128)(2,1)S(1)} %get-tuple-element.43), channel_id=1, source_target_pairs={{0,16},{4,20},{8,24},{12,28},{16,0},{20,4},{24,8},{28,12},{1,17},{... | collective-permute-start | bytes 798728 | tf_op jit(solution)/shard_map/ppermute | solution.py:257
  14.1 3.3 %collective-permute-start.14 = (bf16[1040,128]{1,0:T(8,128)(2,1)S(1)}, bf16[1040,128]{1,0:T(8,128)(2,1)S(1)}, u32[]{:S(2)}, u32[]{:S(2)}) collective-permute-start(bf16[1040,128]{1,0:T(8,128)(2,1)S(1)} %get-tuple-element.46), channel_id=1, source_target_pairs={{0,24},{4,28},{8,16},{12,20},{16,8},{20,12},{24,0},{28,4},{1,25},{... | collective-permute-start | bytes 798728 | tf_op jit(solution)/shard_map/ppermute | solution.py:257
  17.3 5.3 %collective-permute-start.7 = (bf16[1040,128]{1,0:T(8,128)(2,1)S(1)}, bf16[1040,128]{1,0:T(8,128)(2,1)S(1)}, u32[]{:S(2)}, u32[]{:S(2)}) collective-permute-start(bf16[1040,128]{1,0:T(8,128)(2,1)S(1)} %collective-permute-done.6.refs_2_), channel_id=1, source_target_pairs={{0,2},{7,5},{8,10},{15,13},{16,18},{23,21},{24,26},{31,29}} | collective-permute-start | bytes 798728 | tf_op jit(solution)/shard_map/ppermute | solution.py:277
  22.6 0.7 %collective-permute-start.8 = (bf16[1040,128]{1,0:T(8,128)(2,1)S(1)}, bf16[1040,128]{1,0:T(8,128)(2,1)S(1)}, u32[]{:S(2)}, u32[]{:S(2)}) collective-permute-start(bf16[1040,128]{1,0:T(8,128)(2,1)S(1)} %collective-permute-done.6.refs_2_), channel_id=1, source_target_pairs={{1,2},{6,5},{9,10},{14,13},{17,18},{22,21},{25,26},{30,29}} | collective-permute-start | bytes 798728 | tf_op jit(solution)/shard_map/ppermute | solution.py:277
  23.3 0.7 %collective-permute-start.9 = (bf16[1040,128]{1,0:T(8,128)(2,1)S(1)}, bf16[1040,128]{1,0:T(8,128)(2,1)S(1)}, u32[]{:S(2)}, u32[]{:S(2)}) collective-permute-start(bf16[1040,128]{1,0:T(8,128)(2,1)S(1)} %collective-permute-done.6.refs_2_), channel_id=1, source_target_pairs={{3,2},{4,5},{11,10},{12,13},{19,18},{20,21},{27,26},{28,29}} | collective-permute-start | bytes 798728 | tf_op jit(solution)/shard_map/ppermute | solution.py:277
  24.0 2.7 %collective-permute-done.10.refs_4_ = bf16[1040,128]{1,0:T(8,128)(2,1)S(1)} collective-permute-done((bf16[1040,128]{1,0:T(8,128)(2,1)S(1)}, bf16[1040,128]{1,0:T(8,128)(2,1)S(1)}, u32[]{:S(2)}, u32[]{:S(2)}) %collective-permute-start.10) | collective-permute-done | bytes 266272 | tf_op jit(solution)/shard_map/ppermute | solution.py:257
  26.7 2.8 %collective-permute-start.11 = (bf16[1040,128]{1,0:T(8,128)(2,1)S(1)}, bf16[1040,128]{1,0:T(8,128)(2,1)S(1)}, u32[]{:S(2)}, u32[]{:S(2)}) collective-permute-start(bf16[1040,128]{1,0:T(8,128)(2,1)S(1)} %collective-permute-done.10.refs_4_), channel_id=1, source_target_pairs={{0,2},{7,5},{8,10},{15,13},{16,18},{23,21},{24,26},{31,29}} | collective-permute-start | bytes 798728 | tf_op jit(solution)/shard_map/ppermute | solution.py:277
  29.5 0.7 %collective-permute-start.12 = (bf16[1040,128]{1,0:T(8,128)(2,1)S(1)}, bf16[1040,128]{1,0:T(8,128)(2,1)S(1)}, u32[]{:S(2)}, u32[]{:S(2)}) collective-permute-start(bf16[1040,128]{1,0:T(8,128)(2,1)S(1)} %collective-permute-done.10.refs_4_), channel_id=1, source_target_pairs={{1,2},{6,5},{9,10},{14,13},{17,18},{22,21},{25,26},{30,29}} | collective-permute-start | bytes 798728 | tf_op jit(solution)/shard_map/ppermute | solution.py:277
  30.2 0.7 %collective-permute-start.13 = (bf16[1040,128]{1,0:T(8,128)(2,1)S(1)}, bf16[1040,128]{1,0:T(8,128)(2,1)S(1)}, u32[]{:S(2)}, u32[]{:S(2)}) collective-permute-start(bf16[1040,128]{1,0:T(8,128)(2,1)S(1)} %collective-permute-done.10.refs_4_), channel_id=1, source_target_pairs={{3,2},{4,5},{11,10},{12,13},{19,18},{20,21},{27,26},{28,29}} | collective-permute-start | bytes 798728 | tf_op jit(solution)/shard_map/ppermute | solution.py:277
  30.9 0.7 %collective-permute-start.15 = (bf16[1040,128]{1,0:T(8,128)(2,1)S(1)}, bf16[1040,128]{1,0:T(8,128)(2,1)S(1)}, u32[]{:S(2)}, u32[]{:S(2)}) collective-permute-start(bf16[1040,128]{1,0:T(8,128)(2,1)S(1)} %collective-permute-done.14.refs_6_), channel_id=1, source_target_pairs={{3,2},{4,5},{11,10},{12,13},{19,18},{20,21},{27,26},{28,29}} | collective-permute-start | bytes 798728 | tf_op jit(solution)/shard_map/ppermute | solution.py:277
  31.6 0.8 %shard_map.39 = (bf16[512,1024]{1,0:T(8,128)(2,1)S(1)}, f32[1,512]{1,0:T(1,128)S(1)}, f32[8,512]{1,0:T(8,128)S(1)}) custom-call(bf16[1040,128]{1,0:T(8,128)(2,1)S(1)} %get-tuple-element.37.refs_0_, bf16[1040,128]{1,0:T(8,128)(2,1)S(1)} %collective-permute-done.3.refs_1_, bf16[1040,128]{1,0:T(8,128)(2,1)S(1)} %collective-permute-done.4.refs_2_, ...), custom_call_target="tpu_custom_call" | custom-call | flops 536870912 | bytes 1048576 | tf_op jit(solution)/shard_map/pallas_call | solution.py:23
  32.4 4.6 %collective-permute-start.16 = (bf16[1040,128]{1,0:T(8,128)(2,1)S(1)}, bf16[1040,128]{1,0:T(8,128)(2,1)S(1)}, u32[]{:S(2)}, u32[]{:S(2)}) collective-permute-start(bf16[1040,128]{1,0:T(8,128)(2,1)S(1)} %collective-permute-done.14.refs_6_), channel_id=1, source_target_pairs={{0,2},{7,5},{8,10},{15,13},{16,18},{23,21},{24,26},{31,29}} | collective-permute-start | bytes 798728 | tf_op jit(solution)/shard_map/ppermute | solution.py:277
  37.0 0.7 %collective-permute-start.17 = (bf16[1040,128]{1,0:T(8,128)(2,1)S(1)}, bf16[1040,128]{1,0:T(8,128)(2,1)S(1)}, u32[]{:S(2)}, u32[]{:S(2)}) collective-permute-start(bf16[1040,128]{1,0:T(8,128)(2,1)S(1)} %collective-permute-done.14.refs_6_), channel_id=1, source_target_pairs={{1,2},{6,5},{9,10},{14,13},{17,18},{22,21},{25,26},{30,29}} | collective-permute-start | bytes 798728 | tf_op jit(solution)/shard_map/ppermute | solution.py:277
  37.7 1.4 %shard_map.40 = (bf16[512,1024]{1,0:T(8,128)(2,1)S(1)}, f32[1,512]{1,0:T(1,128)S(1)}, f32[8,512]{1,0:T(8,128)S(1)}, f32[8,512]{1,0:T(8,128)S(1)}) custom-call(bf16[512,1024]{1,0:T(8,128)(2,1)S(1)} %get-tuple-element.38.refs_0_, f32[1,512]{1,0:T(1,128)S(1)} %get-tuple-element.39.refs_1_.refs_2_.refs_3_.refs_4_, ...), custom_call_target="tpu_custom_call" | custom-call | flops 1073741824 | bytes 2097152 | tf_op jit(solution)/shard_map/pallas_call | solution.py:23
  39.1 1.9 %shard_map.41 = (bf16[512,1024]{1,0:T(8,128)(2,1)S(1)}, f32[1,512]{1,0:T(1,128)S(1)}, f32[8,512]{1,0:T(8,128)S(1)}, f32[8,512]{1,0:T(8,128)S(1)}, f32[8,512]{1,0:T(8,128)S(1)}) custom-call(bf16[512,1024]{1,0:T(8,128)(2,1)S(1)} %get-tuple-element.38.refs_0_, bf16[512,1024]{1,0:T(8,128)(2,1)S(1)} %get-tuple-element.41.refs_1_, ...), custom_call_target="tpu_custom_call" | custom-call | flops 1610612736 | bytes 3145728 | tf_op jit(solution)/shard_map/pallas_call | solution.py:23
  41.1 1.3 %shard_map.42 = (bf16[256,1024]{1,0:T(8,128)(2,1)S(1)}, f32[1,256]{1,0:T(1,128)S(1)}, f32[8,256]{1,0:T(8,128)S(1)}, f32[8,512]{1,0:T(8,128)S(1)}, f32[8,512]{1,0:T(8,128)S(1)}, /*index=5*/f32[8,512]{1,0:T(8,128)S(1)}) custom-call(bf16[512,1024]{1,0:T(8,128)(2,1)S(1)} %get-tuple-element.38.refs_0_, bf16[512,1024]{1,0:T(8,128)(2,1)S(1)} %get-tuple-element.41.refs_1_, ...), custom_call_target="tpu_custom_call" | custom-call | flops 939524096 | bytes 3670016 | tf_op jit(solution)/shard_map/pallas_call | solution.py:23
  42.4 1.6 %shard_map.43 = (f32[4,128]{1,0:T(4,128)S(1)}, f32[4,128]{1,0:T(4,128)S(1)}, f32[4,128]{1,0:T(4,128)S(1)}, f32[4,128]{1,0:T(4,128)S(1)}) custom-call(bf16[512,1024]{1,0:T(8,128)(2,1)S(1)} %get-tuple-element.38.refs_0_, bf16[512,1024]{1,0:T(8,128)(2,1)S(1)} %get-tuple-element.41.refs_1_, bf16[512,1024]{1,0:T(8,128)(2,1)S(1)} %get-tuple-element.44.refs_2_, ...), custom_call_target="tpu_custom_call" | custom-call | flops 1073741824 | bytes 4194304 | tf_op jit(solution)/shard_map/pallas_call | solution.py:23
  44.0 1.3 %collective-permute-start.18 = (f32[4,128]{1,0:T(4,128)S(1)}, f32[4,128]{1,0:T(4,128)S(1)}, u32[]{:S(2)}, u32[]{:S(2)}) collective-permute-start(f32[4,128]{1,0:T(4,128)S(1)} %get-tuple-element.60), channel_id=1, source_target_pairs={{2,0},{5,7},{10,8},{13,15},{18,16},{21,23},{26,24},{29,31}} | collective-permute-start | bytes 6152 | tf_op jit(solution)/shard_map/ppermute | solution.py:368
  45.3 0.7 %collective-permute-start.19 = (f32[4,128]{1,0:T(4,128)S(1)}, f32[4,128]{1,0:T(4,128)S(1)}, u32[]{:S(2)}, u32[]{:S(2)}) collective-permute-start(f32[4,128]{1,0:T(4,128)S(1)} %get-tuple-element.61), channel_id=1, source_target_pairs={{2,1},{5,6},{10,9},{13,14},{18,17},{21,22},{26,25},{29,30}} | collective-permute-start | bytes 6152 | tf_op jit(solution)/shard_map/ppermute | solution.py:368
  46.0 0.7 %collective-permute-start.20 = (f32[4,128]{1,0:T(4,128)S(1)}, f32[4,128]{1,0:T(4,128)S(1)}, u32[]{:S(2)}, u32[]{:S(2)}) collective-permute-start(f32[4,128]{1,0:T(4,128)S(1)} %get-tuple-element.62), channel_id=1, source_target_pairs={{2,3},{5,4},{10,11},{13,12},{18,19},{21,20},{26,27},{29,28}} | collective-permute-start | bytes 6152 | tf_op jit(solution)/shard_map/ppermute | solution.py:368
  46.6 5.7 %collective-permute-done.18 = f32[4,128]{1,0:T(4,128)S(1)} collective-permute-done((f32[4,128]{1,0:T(4,128)S(1)}, f32[4,128]{1,0:T(4,128)S(1)}, u32[]{:S(2)}, u32[]{:S(2)}) %collective-permute-start.18) | collective-permute-done | bytes 2080 | tf_op jit(solution)/shard_map/ppermute | solution.py:368
  52.9 3.1 %collective-permute-done.21 = f32[2,128]{1,0:T(2,128)S(1)} collective-permute-done((f32[2,128]{1,0:T(2,128)S(1)}, f32[2,128]{1,0:T(2,128)S(1)}, u32[]{:S(2)}, u32[]{:S(2)}) %collective-permute-start.21) | collective-permute-done | bytes 1056 | tf_op jit(solution)/shard_map/ppermute | solution.py:257
  56.0 1.6 %collective-permute-start.22 = (f32[2,128]{1,0:T(2,128)S(1)}, f32[2,128]{1,0:T(2,128)S(1)}, u32[]{:S(2)}, u32[]{:S(2)}) collective-permute-start(f32[2,128]{1,0:T(2,128)S(1)} %pad_maximum_fusion.2), channel_id=1, source_target_pairs={{0,16},{4,20},{8,24},{12,28},{16,0},{20,4},{24,8},{28,12},{1,17},{... | collective-permute-start | bytes 3080 | tf_op jit(solution)/shard_map/ppermute | solution.py:257
  57.6 2.1 %collective-permute-done.22 = f32[2,128]{1,0:T(2,128)S(1)} collective-permute-done((f32[2,128]{1,0:T(2,128)S(1)}, f32[2,128]{1,0:T(2,128)S(1)}, u32[]{:S(2)}, u32[]{:S(2)}) %collective-permute-start.22) | collective-permute-done | bytes 1056 | tf_op jit(solution)/shard_map/ppermute | solution.py:257
  59.7 1.1 %collective-permute-done.23.mate_ref = f32[4,128]{1,0:T(4,128)S(1)} collective-permute-done((f32[4,128]{1,0:T(4,128)S(1)}, f32[4,128]{1,0:T(4,128)S(1)}, u32[]{:S(2)}, u32[]{:S(2)}) %collective-permute-start.23) | collective-permute-done | bytes 2080 | tf_op jit(solution)/shard_map/ppermute | solution.py:260
  60.9 0.8 %shard_map.44 = f32[1,256]{1,0:T(1,128)} custom-call(s32[1,256]{1,0:T(1,128)S(1)} %get-tuple-element.34.pos_ref, f32[4,128]{1,0:T(4,128)S(1)} %pad_maximum_fusion.own_ref, f32[4,128]{1,0:T(4,128)S(1)} %collective-permute-done.23.mate_ref), custom_call_target="tpu_custom_call" | custom-call | flops 1000000 | bytes 100000 | tf_op jit(solution)/shard_map/pallas_call | solution.py:23
  (36 shorter events, 3.1 us)
Async XLA Ops:
  0.0 0.7 %copy-start.1 = (s32[256,1]{0,1:T(1,128)S(1)}, s32[256,1]{0,1:T(1,128)}, u32[]{:S(2)}) copy-start(s32[256,1]{0,1:T(1,128)} %param.4) | copy-start | bytes 3076
  0.0 3.5 %collective-permute-start = (bf16[256,1024]{1,0:T(8,128)(2,1)}, bf16[256,1024]{1,0:T(8,128)(2,1)S(1)}, u32[]{:S(2)}, u32[]{:S(2)}) collective-permute-start(bf16[256,1024]{1,0:T(8,128)(2,1)} %emb_hbm.1), channel_id=1, source_target_pairs={{0,4},{4,0},{8,12},{12,8},{16,20},{20,16},{24,28},{28,24},{1,5},{5... | collective-permute-start | bytes 1572872 | tf_op jit(solution)/shard_map/ppermute | solution.py:260
  0.7 0.7 %copy-start.2 = (s32[256]{0:T(256)S(1)}, s32[256]{0:T(256)}, u32[]{:S(2)}) copy-start(s32[256]{0:T(256)} %param.5) | copy-start | bytes 3076
  0.7 2.8 %collective-permute-start.1 = (s32[1,256]{1,0:T(1,128)S(1)}, s32[1,256]{1,0:T(1,128)S(1)}, u32[]{:S(2)}, u32[]{:S(2)}) collective-permute-start(s32[1,256]{1,0:T(1,128)S(1)} %bitcast.3), channel_id=1, source_target_pairs={{0,4},{4,0},{8,12},{12,8},{16,20},{20,16},{24,28},{28,24},{1,5},{5... | collective-permute-start | bytes 3080 | tf_op jit(solution)/shard_map/ppermute | solution.py:260
  1.4 2.1 %collective-permute-start.2 = (s32[1,256]{1,0:T(1,128)S(1)}, s32[1,256]{1,0:T(1,128)S(1)}, u32[]{:S(2)}, u32[]{:S(2)}) collective-permute-start(s32[1,256]{1,0:T(1,128)S(1)} %bitcast.5), channel_id=1, source_target_pairs={{0,4},{4,0},{8,12},{12,8},{16,20},{20,16},{24,28},{28,24},{1,5},{5... | collective-permute-start | bytes 3080 | tf_op jit(solution)/shard_map/ppermute | solution.py:260
  1.9 1.0 %copy-start = (bf16[256,1024]{1,0:T(8,128)(2,1)S(1)}, bf16[256,1024]{1,0:T(8,128)(2,1)}, u32[]{:S(2)}) copy-start(bf16[256,1024]{1,0:T(8,128)(2,1)} %emb_hbm.1) | copy-start | bytes 1572868
  4.1 10.0 %collective-permute-start.3 = (bf16[1040,128]{1,0:T(8,128)(2,1)S(1)}, bf16[1040,128]{1,0:T(8,128)(2,1)S(1)}, u32[]{:S(2)}, u32[]{:S(2)}) collective-permute-start(bf16[1040,128]{1,0:T(8,128)(2,1)S(1)} %get-tuple-element.37.refs_0_), channel_id=1, source_target_pairs={{0,2},{7,5},{8,10},{15,13},{16,18},{23,21},{24,26},{31,29}} | collective-permute-start | bytes 798728 | tf_op jit(solution)/shard_map/ppermute | solution.py:277
  9.6 7.8 %collective-permute-start.6 = (bf16[1040,128]{1,0:T(8,128)(2,1)S(1)}, bf16[1040,128]{1,0:T(8,128)(2,1)S(1)}, u32[]{:S(2)}, u32[]{:S(2)}) collective-permute-start(bf16[1040,128]{1,0:T(8,128)(2,1)S(1)} %get-tuple-element.40), channel_id=1, source_target_pairs={{0,8},{4,12},{8,0},{12,4},{16,24},{20,28},{24,16},{28,20},{1,9},{5... | collective-permute-start | bytes 798728 | tf_op jit(solution)/shard_map/ppermute | solution.py:257
  11.1 11.5 %collective-permute-start.4 = (bf16[1040,128]{1,0:T(8,128)(2,1)S(1)}, bf16[1040,128]{1,0:T(8,128)(2,1)S(1)}, u32[]{:S(2)}, u32[]{:S(2)}) collective-permute-start(bf16[1040,128]{1,0:T(8,128)(2,1)S(1)} %get-tuple-element.37.refs_0_), channel_id=1, source_target_pairs={{1,2},{6,5},{9,10},{14,13},{17,18},{22,21},{25,26},{30,29}} | collective-permute-start | bytes 798728 | tf_op jit(solution)/shard_map/ppermute | solution.py:277
  11.8 11.5 %collective-permute-start.5 = (bf16[1040,128]{1,0:T(8,128)(2,1)S(1)}, bf16[1040,128]{1,0:T(8,128)(2,1)S(1)}, u32[]{:S(2)}, u32[]{:S(2)}) collective-permute-start(bf16[1040,128]{1,0:T(8,128)(2,1)S(1)} %get-tuple-element.37.refs_0_), channel_id=1, source_target_pairs={{3,2},{4,5},{11,10},{12,13},{19,18},{20,21},{27,26},{28,29}} | collective-permute-start | bytes 798728 | tf_op jit(solution)/shard_map/ppermute | solution.py:277
  12.5 14.2 %collective-permute-start.10 = (bf16[1040,128]{1,0:T(8,128)(2,1)S(1)}, bf16[1040,128]{1,0:T(8,128)(2,1)S(1)}, u32[]{:S(2)}, u32[]{:S(2)}) collective-permute-start(bf16[1040,128]{1,0:T(8,128)(2,1)S(1)} %get-tuple-element.43), channel_id=1, source_target_pairs={{0,16},{4,20},{8,24},{12,28},{16,0},{20,4},{24,8},{28,12},{1,17},{... | collective-permute-start | bytes 798728 | tf_op jit(solution)/shard_map/ppermute | solution.py:257
  14.1 15.4 %collective-permute-start.14 = (bf16[1040,128]{1,0:T(8,128)(2,1)S(1)}, bf16[1040,128]{1,0:T(8,128)(2,1)S(1)}, u32[]{:S(2)}, u32[]{:S(2)}) collective-permute-start(bf16[1040,128]{1,0:T(8,128)(2,1)S(1)} %get-tuple-element.46), channel_id=1, source_target_pairs={{0,24},{4,28},{8,16},{12,20},{16,8},{20,12},{24,0},{28,4},{1,25},{... | collective-permute-start | bytes 798728 | tf_op jit(solution)/shard_map/ppermute | solution.py:257
  17.3 12.8 %collective-permute-start.7 = (bf16[1040,128]{1,0:T(8,128)(2,1)S(1)}, bf16[1040,128]{1,0:T(8,128)(2,1)S(1)}, u32[]{:S(2)}, u32[]{:S(2)}) collective-permute-start(bf16[1040,128]{1,0:T(8,128)(2,1)S(1)} %collective-permute-done.6.refs_2_), channel_id=1, source_target_pairs={{0,2},{7,5},{8,10},{15,13},{16,18},{23,21},{24,26},{31,29}} | collective-permute-start | bytes 798728 | tf_op jit(solution)/shard_map/ppermute | solution.py:277
  22.6 8.2 %collective-permute-start.8 = (bf16[1040,128]{1,0:T(8,128)(2,1)S(1)}, bf16[1040,128]{1,0:T(8,128)(2,1)S(1)}, u32[]{:S(2)}, u32[]{:S(2)}) collective-permute-start(bf16[1040,128]{1,0:T(8,128)(2,1)S(1)} %collective-permute-done.6.refs_2_), channel_id=1, source_target_pairs={{1,2},{6,5},{9,10},{14,13},{17,18},{22,21},{25,26},{30,29}} | collective-permute-start | bytes 798728 | tf_op jit(solution)/shard_map/ppermute | solution.py:277
  23.3 9.0 %collective-permute-start.9 = (bf16[1040,128]{1,0:T(8,128)(2,1)S(1)}, bf16[1040,128]{1,0:T(8,128)(2,1)S(1)}, u32[]{:S(2)}, u32[]{:S(2)}) collective-permute-start(bf16[1040,128]{1,0:T(8,128)(2,1)S(1)} %collective-permute-done.6.refs_2_), channel_id=1, source_target_pairs={{3,2},{4,5},{11,10},{12,13},{19,18},{20,21},{27,26},{28,29}} | collective-permute-start | bytes 798728 | tf_op jit(solution)/shard_map/ppermute | solution.py:277
  26.7 10.3 %collective-permute-start.11 = (bf16[1040,128]{1,0:T(8,128)(2,1)S(1)}, bf16[1040,128]{1,0:T(8,128)(2,1)S(1)}, u32[]{:S(2)}, u32[]{:S(2)}) collective-permute-start(bf16[1040,128]{1,0:T(8,128)(2,1)S(1)} %collective-permute-done.10.refs_4_), channel_id=1, source_target_pairs={{0,2},{7,5},{8,10},{15,13},{16,18},{23,21},{24,26},{31,29}} | collective-permute-start | bytes 798728 | tf_op jit(solution)/shard_map/ppermute | solution.py:277
  29.5 9.6 %collective-permute-start.12 = (bf16[1040,128]{1,0:T(8,128)(2,1)S(1)}, bf16[1040,128]{1,0:T(8,128)(2,1)S(1)}, u32[]{:S(2)}, u32[]{:S(2)}) collective-permute-start(bf16[1040,128]{1,0:T(8,128)(2,1)S(1)} %collective-permute-done.10.refs_4_), channel_id=1, source_target_pairs={{1,2},{6,5},{9,10},{14,13},{17,18},{22,21},{25,26},{30,29}} | collective-permute-start | bytes 798728 | tf_op jit(solution)/shard_map/ppermute | solution.py:277
  30.2 8.9 %collective-permute-start.13 = (bf16[1040,128]{1,0:T(8,128)(2,1)S(1)}, bf16[1040,128]{1,0:T(8,128)(2,1)S(1)}, u32[]{:S(2)}, u32[]{:S(2)}) collective-permute-start(bf16[1040,128]{1,0:T(8,128)(2,1)S(1)} %collective-permute-done.10.refs_4_), channel_id=1, source_target_pairs={{3,2},{4,5},{11,10},{12,13},{19,18},{20,21},{27,26},{28,29}} | collective-permute-start | bytes 798728 | tf_op jit(solution)/shard_map/ppermute | solution.py:277
  30.9 10.2 %collective-permute-start.15 = (bf16[1040,128]{1,0:T(8,128)(2,1)S(1)}, bf16[1040,128]{1,0:T(8,128)(2,1)S(1)}, u32[]{:S(2)}, u32[]{:S(2)}) collective-permute-start(bf16[1040,128]{1,0:T(8,128)(2,1)S(1)} %collective-permute-done.14.refs_6_), channel_id=1, source_target_pairs={{3,2},{4,5},{11,10},{12,13},{19,18},{20,21},{27,26},{28,29}} | collective-permute-start | bytes 798728 | tf_op jit(solution)/shard_map/ppermute | solution.py:277
  32.4 10.0 %collective-permute-start.16 = (bf16[1040,128]{1,0:T(8,128)(2,1)S(1)}, bf16[1040,128]{1,0:T(8,128)(2,1)S(1)}, u32[]{:S(2)}, u32[]{:S(2)}) collective-permute-start(bf16[1040,128]{1,0:T(8,128)(2,1)S(1)} %collective-permute-done.14.refs_6_), channel_id=1, source_target_pairs={{0,2},{7,5},{8,10},{15,13},{16,18},{23,21},{24,26},{31,29}} | collective-permute-start | bytes 798728 | tf_op jit(solution)/shard_map/ppermute | solution.py:277
  37.0 5.4 %collective-permute-start.17 = (bf16[1040,128]{1,0:T(8,128)(2,1)S(1)}, bf16[1040,128]{1,0:T(8,128)(2,1)S(1)}, u32[]{:S(2)}, u32[]{:S(2)}) collective-permute-start(bf16[1040,128]{1,0:T(8,128)(2,1)S(1)} %collective-permute-done.14.refs_6_), channel_id=1, source_target_pairs={{1,2},{6,5},{9,10},{14,13},{17,18},{22,21},{25,26},{30,29}} | collective-permute-start | bytes 798728 | tf_op jit(solution)/shard_map/ppermute | solution.py:277
  44.0 8.3 %collective-permute-start.18 = (f32[4,128]{1,0:T(4,128)S(1)}, f32[4,128]{1,0:T(4,128)S(1)}, u32[]{:S(2)}, u32[]{:S(2)}) collective-permute-start(f32[4,128]{1,0:T(4,128)S(1)} %get-tuple-element.60), channel_id=1, source_target_pairs={{2,0},{5,7},{10,8},{13,15},{18,16},{21,23},{26,24},{29,31}} | collective-permute-start | bytes 6152 | tf_op jit(solution)/shard_map/ppermute | solution.py:368
  45.3 7.0 %collective-permute-start.19 = (f32[4,128]{1,0:T(4,128)S(1)}, f32[4,128]{1,0:T(4,128)S(1)}, u32[]{:S(2)}, u32[]{:S(2)}) collective-permute-start(f32[4,128]{1,0:T(4,128)S(1)} %get-tuple-element.61), channel_id=1, source_target_pairs={{2,1},{5,6},{10,9},{13,14},{18,17},{21,22},{26,25},{29,30}} | collective-permute-start | bytes 6152 | tf_op jit(solution)/shard_map/ppermute | solution.py:368
  46.0 6.4 %collective-permute-start.20 = (f32[4,128]{1,0:T(4,128)S(1)}, f32[4,128]{1,0:T(4,128)S(1)}, u32[]{:S(2)}, u32[]{:S(2)}) collective-permute-start(f32[4,128]{1,0:T(4,128)S(1)} %get-tuple-element.62), channel_id=1, source_target_pairs={{2,3},{5,4},{10,11},{13,12},{18,19},{21,20},{26,27},{29,28}} | collective-permute-start | bytes 6152 | tf_op jit(solution)/shard_map/ppermute | solution.py:368
  52.3 3.6 %collective-permute-start.21 = (f32[2,128]{1,0:T(2,128)S(1)}, f32[2,128]{1,0:T(2,128)S(1)}, u32[]{:S(2)}, u32[]{:S(2)}) collective-permute-start(f32[2,128]{1,0:T(2,128)S(1)} %pad_maximum_fusion.1), channel_id=1, source_target_pairs={{0,8},{4,12},{8,0},{12,4},{16,24},{20,28},{24,16},{28,20},{1,9},{5... | collective-permute-start | bytes 3080 | tf_op jit(solution)/shard_map/ppermute | solution.py:257
  56.0 3.6 %collective-permute-start.22 = (f32[2,128]{1,0:T(2,128)S(1)}, f32[2,128]{1,0:T(2,128)S(1)}, u32[]{:S(2)}, u32[]{:S(2)}) collective-permute-start(f32[2,128]{1,0:T(2,128)S(1)} %pad_maximum_fusion.2), channel_id=1, source_target_pairs={{0,16},{4,20},{8,24},{12,28},{16,0},{20,4},{24,8},{28,12},{1,17},{... | collective-permute-start | bytes 3080 | tf_op jit(solution)/shard_map/ppermute | solution.py:257
  59.6 1.2 %collective-permute-start.23 = (f32[4,128]{1,0:T(4,128)S(1)}, f32[4,128]{1,0:T(4,128)S(1)}, u32[]{:S(2)}, u32[]{:S(2)}) collective-permute-start(f32[4,128]{1,0:T(4,128)S(1)} %pad_maximum_fusion.own_ref), channel_id=1, source_target_pairs={{0,4},{4,0},{8,12},{12,8},{16,20},{20,16},{24,28},{28,24},{1,5},{5... | collective-permute-start | bytes 6152 | tf_op jit(solution)/shard_map/ppermute | solution.py:260

commit v3 on v2

--- a/solution.py
+++ b/solution.py
@@ -59,7 +59,7 @@
     return packed, digits, where, dest
 
 
-def own_body(cap, chips, emb_hbm, dest_hbm, rank_hbm, *refs):
+def own_body(cap, chips, planes, emb_hbm, dest_hbm, rank_hbm, *refs):
     packed_ref, digits_ref, pos_ref, emb_ref, dest_ref, rank_ref, sems = refs
     copies = [
         pltpu.make_async_copy(source, target, sems.at[i])
@@ -77,7 +77,9 @@
     )
     packed_ref[...] = packed
     digits_ref[...] = digits
-    pos_ref[...] = where * 2 + ((dest & 1) ^ (group & 1))
+    parity = dest & 1
+    row, lane = dest * planes + planes // 2 - parity, where % cap + cap * (parity ^ (group & 1))
+    pos_ref[...] = row * LANES + lane
 
 
 def pack_body(cap, chips, emb_ref, dest_ref, rank_ref, own, own_digits, *refs):
@@ -170,7 +172,7 @@
         lax.fori_loop(0, count, body, 0)
 
 
-def stage_body(pieces, olds, many, places, *refs):
+def stage_body(pieces, olds, many, places, sources, *refs):
     refs = list(refs)
 
     def take(n):
@@ -181,7 +183,7 @@
     xs, rows, blocks = take(olds), take(olds), take(many)
     found = take(sum(range(olds + 1))) if places else []
     if places:
-        outs = take(len(places))
+        (out,) = take(1)
         news, (x_ref, row_ref, best_ref) = take(olds), take(3)
     else:
         x_ref, row_ref, best_ref = take(3)
@@ -199,8 +201,11 @@
             side = jnp.transpose(side_ref[i : i + LANES, :])
             best_ref[:, i : i + LANES] = jnp.maximum(best_ref[:, i : i + LANES], wide_max(side))
         return
-    for out, place in zip(outs, places):
-        for row, (stage, block) in enumerate(place):
+    planes = len(places)
+    group = lax.axis_index("group")
+    for p, place in enumerate(places):
+        plane = jnp.where((group & 1) == 0, sources[0][p], sources[1][p])
+        for s, (stage, block) in enumerate(place):
             lanes = slice(block * LANES, (block + 1) * LANES)
             if stage == olds:
                 side = jnp.transpose(side_ref[lanes, :])
@@ -209,25 +214,23 @@
                 best = news[stage][:, lanes]
                 for later in range(stage, olds):
                     best = jnp.maximum(best, found[sum(range(later + 1)) + stage][:, lanes])
-            out[row : row + 1, :] = jnp.max(best, axis=0, keepdims=True)
-
-
-def final_body(cap, chips, pos_ref, own_ref, mate_ref, out_ref):
-    rows = pos_ref.shape[1]
-    pos = pos_ref[...]
-    other, where = pos & 1, pos >> 1
-    chip, slot = where // cap, where % cap
-    place = lax.broadcasted_iota(jnp.int32, (LANES, rows), 0)
-    pick = (place == slot + cap * other).astype(F32)
-    table = jnp.concatenate([own_ref[...], mate_ref[...]], axis=0)
+            best = jnp.max(best, axis=0, keepdims=True)
+            device = ((group >> 1) ^ s) * 2 * planes + plane
+            out[pl.ds(device, 1), :] = best
+            out[pl.ds(device + planes, 1), :] = best
+
+
+def final_body(pos_ref, table_ref, out_ref):
+    rows, pos = pos_ref.shape[1], pos_ref[...]
+    pick = lax.broadcasted_iota(jnp.int32, (LANES, rows), 0) == pos % LANES
     got = lax.dot_general(
-        table,
-        pick,
+        table_ref[...],
+        pick.astype(F32),
         (((1,), (0,)), ((), ())),
         precision=lax.Precision.HIGHEST,
         preferred_element_type=F32,
     )
-    mine = lax.broadcasted_iota(jnp.int32, (2 * chips, rows), 0) == chip + chips * other
+    mine = lax.broadcasted_iota(jnp.int32, got.shape, 0) == pos // LANES
     out_ref[...] = jnp.sum(jnp.where(mine, got, 0.0), axis=0, keepdims=True)
 
 
@@ -245,7 +248,6 @@
     cap = rows // 4
     pieces = width // LANES
     size = pieces * LANES + META
-    group, plane = lax.axis_index("group"), lax.axis_index("blk")
 
     def blocks(n):
         return jax.ShapeDtypeStruct((n * size, LANES), BF16)
@@ -263,13 +265,10 @@
     sources = [[z for z in range(planes) if z != half]]
     sources.append([planes - 1 - z for z in sources[0]])
 
-    def meeting(step, back=False):
-        pairs = []
-        for g in range(groups):
-            there = g * planes + meet[g & 1]
-            here = g * planes + sources[g & 1][step]
-            pairs.append((there, here) if back else (here, there))
-        return pairs
+    def meeting(step):
+        return [
+            (g * planes + sources[g & 1][step], g * planes + meet[g & 1]) for g in range(groups)
+        ]
 
     def gather(value):
         arrived = [value]
@@ -282,7 +281,7 @@
     mate_dest, mate_rank = to_core(dest), to_core(rank)
     flops = 2 * chips * cap * rows * width
     own = call(
-        functools.partial(own_body, cap, chips),
+        functools.partial(own_body, cap, chips, planes),
         [
             jax.ShapeDtypeStruct((chips * cap, width), BF16),
             floats(META, chips * cap),
@@ -345,13 +344,18 @@
         operands = xs + ranks + [arrived[c][p] for c, p in stage]
         if i == len(stages) - 1:
             operands += found
-            outs = [floats(chips, LANES)] * planes
+            outs = floats(groups * planes, LANES)
             spare = [pltpu.VMEM(*m) for m in kept + made] + spare
         else:
             outs = [jax.ShapeDtypeStruct(*m) for m in made + kept]
         best = call(
             functools.partial(
-                stage_body, pieces, i, len(stage), places if i == len(stages) - 1 else None
+                stage_body,
+                pieces,
+                i,
+                len(stage),
+                places if i == len(stages) - 1 else None,
+                [[meet[parity]] + sources[parity] for parity in range(2)],
             ),
             outs,
             operands,
@@ -364,28 +368,8 @@
             xs.append(best[0])
             ranks.append(best[1])
             found += best[3:] + best[2:3]
-    returned = [
-        lax.ppermute(best[1 + step], ("group", "blk"), meeting(step, back=True))
-        for step in range(planes - 1)
-    ]
-    at_meeting = plane == jnp.where((group & 1) == 0, half, half - 1)
-    mine = jnp.where(at_meeting, best[0], functools.reduce(jnp.add, returned))
-    rows_of = {(0, s): mine[s : s + 1] for s in range(chips)}
-    for step in range(chips.bit_length() - 1):
-        bit = 1 << step
-        keys = sorted(key for key in rows_of if key[1] & bit)
-        got = to_chip(jnp.concatenate([rows_of.pop(key) for key in keys], axis=0), bit)
-        for i, (t, s) in enumerate(keys):
-            rows_of[t ^ bit, s ^ bit] = got[i : i + 1]
-    table = jnp.concatenate([rows_of[t, 0] for t in range(chips)], axis=0)
-    result = call(
-        functools.partial(final_body, cap, chips),
-        floats(1, rows),
-        [pos, table, to_core(table)],
-        1000000,
-        100000,
-        4 << 20,
-    )
+    table = lax.all_to_all(best, ("group", "blk"), 0, 0, tiled=True)
+    result = call(final_body, floats(1, rows), [pos, table], 1000000, 100000, 4 << 20)
     return result.reshape(rows)
 
 

time: 62.1 us -> 58.9 us (0.948)
  blocking collectives: 0 us -> 13.8 us
  waiting for transfers between devices: 14.7 us -> 2.74 us
  starting transfers between devices: 36.3 us -> 31.4 us
    all_to_all x0 -> x1, blocking collectives: none -> 13.8 us  [on_device(): table = lax.all_to_all(best, ('group', 'blk'), 0, 0, tiled=True)]
    ppermute x3 -> x0, waiting for transfers between devices: 5.67 us -> none  [on_device(): lax.ppermute(best[1 + step], ('group', 'blk'), meeting(step, back=True))]
    ppermute x5 -> x3, waiting for transfers between devices: 7.81 us -> 2.7 us  [to_chip(): return lax.ppermute(value, 'group', [(i, i ^ 2 * s) for i in range(groups)])]
    ppermute x3 -> x0, starting transfers between devices: 2.62 us -> none  [on_device(): lax.ppermute(best[1 + step], ('group', 'blk'), meeting(step, back=True))]
    ppermute x5 -> x3, starting transfers between devices: 8.56 us -> 6.4 us  [to_chip(): return lax.ppermute(value, 'group', [(i, i ^ 2 * s) for i in range(groups)])]
    ppermute x4 -> x3, waiting for transfers between devices: 1.16 us -> 0.01 us  [to_core(): return lax.ppermute(value, 'group', [(i, i ^ 1) for i in range(groups)])]
    ppermute x4 -> x3, starting transfers between devices: 1.55 us -> 1.48 us  [to_core(): return lax.ppermute(value, 'group', [(i, i ^ 1) for i in range(groups)])]
  transfers between devices with their start and end apart: 24 -> 18, of which waited for: 5 -> 1; matrix products, arithmetic and copies ran while one was open for 0% -> 0% of each run, Pallas kernels for 10% -> 10%
where the time goes in v3:
time: 58.9 us; the launch traced here: 58.5 us
  starting transfers between devices  31.4 us (53%)
  blocking collectives  13.8 us (23%)
  Pallas kernels  8.86 us (15%)
  waiting for transfers between devices  2.74 us (5%)
  local copies, waits for them, and re-layouts  1.41 us (2%)
    ppermute x12, starting transfers between devices, gather(): arrived.append(lax.ppermute(value, ('group', 'blk'), meeting(step)))  23.6 us
    all_to_all x1, blocking collectives, on_device(): table = lax.all_to_all(best, ('group', 'blk'), 0, 0, tiled=True)  13.8 us
    pallas_call x8, Pallas kernels, call(): pl.pallas_call(body, out_shape=outs, in_specs=[spec] * len(operands), out...  8.86 us
    ppermute x3, starting transfers between devices, to_chip(): return lax.ppermute(value, 'group', [(i, i ^ 2 * s) for i in range(groups)])  6.4 us
    ppermute x3, waiting for transfers between devices, to_chip(): return lax.ppermute(value, 'group', [(i, i ^ 2 * s) for i in range(groups)])  2.7 us
    ppermute x3, starting transfers between devices, to_core(): return lax.ppermute(value, 'group', [(i, i ^ 1) for i in range(groups)])  1.48 us
    unnamed x6, local copies, waits for them, and re-layouts  1.41 us
  transfers between devices with their start and end apart: 18, of which 1 were waited for; matrix products, arithmetic and copies ran while one was open for 0% of the time, Pallas kernels for 10%

profile of v3, /device:TPU:0, one launch (start us, length us, event | category | flops | bytes accessed | tf_op | source)
XLA Modules:
  0.0 58.5 jit_solution(5090164162698153621)
XLA Ops:
  0.0 0.5 collective-permute-start
  0.5 0.2 copy-done.1
  0.7 0.5 collective-permute-start.1
  1.2 0.2 copy-done.2
  1.4 0.5 collective-permute-start.2
  1.9 1.0 %copy-done = bf16[256,1024]{1,0:T(8,128)(2,1)S(1)} copy-done((bf16[256,1024]{1,0:T(8,128)(2,1)S(1)}, bf16[256,1024]{1,0:T(8,128)(2,1)}, u32[]{:S(2)}) %copy-start) | copy-done | bytes 524312
  2.9 0.6 shard_map.37
  3.5 0.0 collective-permute-done.emb_ref
  3.5 0.5 shard_map.38
  4.1 5.5 %collective-permute-start.3 = (bf16[1040,128]{1,0:T(8,128)(2,1)S(1)}, bf16[1040,128]{1,0:T(8,128)(2,1)S(1)}, u32[]{:S(2)}, u32[]{:S(2)}) collective-permute-start(bf16[1040,128]{1,0:T(8,128)(2,1)S(1)} %get-tuple-element.33.refs_0_), channel_id=1, source_target_pairs={{0,2},{7,5},{8,10},{15,13},{16,18},{23,21},{24,26},{31,29}} | collective-permute-start | bytes 798728 | tf_op jit(solution)/shard_map/ppermute | solution.py:276
  9.6 1.6 %collective-permute-start.6 = (bf16[1040,128]{1,0:T(8,128)(2,1)S(1)}, bf16[1040,128]{1,0:T(8,128)(2,1)S(1)}, u32[]{:S(2)}, u32[]{:S(2)}) collective-permute-start(bf16[1040,128]{1,0:T(8,128)(2,1)S(1)} %get-tuple-element.36), channel_id=1, source_target_pairs={{0,8},{4,12},{8,0},{12,4},{16,24},{20,28},{24,16},{28,20},{1,9},{5... | collective-permute-start | bytes 798728 | tf_op jit(solution)/shard_map/ppermute | solution.py:259
  11.1 0.7 %collective-permute-start.4 = (bf16[1040,128]{1,0:T(8,128)(2,1)S(1)}, bf16[1040,128]{1,0:T(8,128)(2,1)S(1)}, u32[]{:S(2)}, u32[]{:S(2)}) collective-permute-start(bf16[1040,128]{1,0:T(8,128)(2,1)S(1)} %get-tuple-element.33.refs_0_), channel_id=1, source_target_pairs={{1,2},{6,5},{9,10},{14,13},{17,18},{22,21},{25,26},{30,29}} | collective-permute-start | bytes 798728 | tf_op jit(solution)/shard_map/ppermute | solution.py:276
  11.8 0.7 %collective-permute-start.5 = (bf16[1040,128]{1,0:T(8,128)(2,1)S(1)}, bf16[1040,128]{1,0:T(8,128)(2,1)S(1)}, u32[]{:S(2)}, u32[]{:S(2)}) collective-permute-start(bf16[1040,128]{1,0:T(8,128)(2,1)S(1)} %get-tuple-element.33.refs_0_), channel_id=1, source_target_pairs={{3,2},{4,5},{11,10},{12,13},{19,18},{20,21},{27,26},{28,29}} | collective-permute-start | bytes 798728 | tf_op jit(solution)/shard_map/ppermute | solution.py:276
  12.5 1.6 %collective-permute-start.10 = (bf16[1040,128]{1,0:T(8,128)(2,1)S(1)}, bf16[1040,128]{1,0:T(8,128)(2,1)S(1)}, u32[]{:S(2)}, u32[]{:S(2)}) collective-permute-start(bf16[1040,128]{1,0:T(8,128)(2,1)S(1)} %get-tuple-element.39), channel_id=1, source_target_pairs={{0,16},{4,20},{8,24},{12,28},{16,0},{20,4},{24,8},{28,12},{1,17},{... | collective-permute-start | bytes 798728 | tf_op jit(solution)/shard_map/ppermute | solution.py:259
  14.1 3.3 %collective-permute-start.14 = (bf16[1040,128]{1,0:T(8,128)(2,1)S(1)}, bf16[1040,128]{1,0:T(8,128)(2,1)S(1)}, u32[]{:S(2)}, u32[]{:S(2)}) collective-permute-start(bf16[1040,128]{1,0:T(8,128)(2,1)S(1)} %get-tuple-element.42), channel_id=1, source_target_pairs={{0,24},{4,28},{8,16},{12,20},{16,8},{20,12},{24,0},{28,4},{1,25},{... | collective-permute-start | bytes 798728 | tf_op jit(solution)/shard_map/ppermute | solution.py:259
  17.3 5.3 %collective-permute-start.7 = (bf16[1040,128]{1,0:T(8,128)(2,1)S(1)}, bf16[1040,128]{1,0:T(8,128)(2,1)S(1)}, u32[]{:S(2)}, u32[]{:S(2)}) collective-permute-start(bf16[1040,128]{1,0:T(8,128)(2,1)S(1)} %collective-permute-done.6.refs_2_), channel_id=1, source_target_pairs={{0,2},{7,5},{8,10},{15,13},{16,18},{23,21},{24,26},{31,29}} | collective-permute-start | bytes 798728 | tf_op jit(solution)/shard_map/ppermute | solution.py:276
  22.6 0.7 %collective-permute-start.8 = (bf16[1040,128]{1,0:T(8,128)(2,1)S(1)}, bf16[1040,128]{1,0:T(8,128)(2,1)S(1)}, u32[]{:S(2)}, u32[]{:S(2)}) collective-permute-start(bf16[1040,128]{1,0:T(8,128)(2,1)S(1)} %collective-permute-done.6.refs_2_), channel_id=1, source_target_pairs={{1,2},{6,5},{9,10},{14,13},{17,18},{22,21},{25,26},{30,29}} | collective-permute-start | bytes 798728 | tf_op jit(solution)/shard_map/ppermute | solution.py:276
  23.3 0.7 %collective-permute-start.9 = (bf16[1040,128]{1,0:T(8,128)(2,1)S(1)}, bf16[1040,128]{1,0:T(8,128)(2,1)S(1)}, u32[]{:S(2)}, u32[]{:S(2)}) collective-permute-start(bf16[1040,128]{1,0:T(8,128)(2,1)S(1)} %collective-permute-done.6.refs_2_), channel_id=1, source_target_pairs={{3,2},{4,5},{11,10},{12,13},{19,18},{20,21},{27,26},{28,29}} | collective-permute-start | bytes 798728 | tf_op jit(solution)/shard_map/ppermute | solution.py:276
  24.0 2.7 %collective-permute-done.10.refs_4_ = bf16[1040,128]{1,0:T(8,128)(2,1)S(1)} collective-permute-done((bf16[1040,128]{1,0:T(8,128)(2,1)S(1)}, bf16[1040,128]{1,0:T(8,128)(2,1)S(1)}, u32[]{:S(2)}, u32[]{:S(2)}) %collective-permute-start.10) | collective-permute-done | bytes 266272 | tf_op jit(solution)/shard_map/ppermute | solution.py:259
  26.7 2.8 %collective-permute-start.11 = (bf16[1040,128]{1,0:T(8,128)(2,1)S(1)}, bf16[1040,128]{1,0:T(8,128)(2,1)S(1)}, u32[]{:S(2)}, u32[]{:S(2)}) collective-permute-start(bf16[1040,128]{1,0:T(8,128)(2,1)S(1)} %collective-permute-done.10.refs_4_), channel_id=1, source_target_pairs={{0,2},{7,5},{8,10},{15,13},{16,18},{23,21},{24,26},{31,29}} | collective-permute-start | bytes 798728 | tf_op jit(solution)/shard_map/ppermute | solution.py:276
  29.5 0.7 %collective-permute-start.12 = (bf16[1040,128]{1,0:T(8,128)(2,1)S(1)}, bf16[1040,128]{1,0:T(8,128)(2,1)S(1)}, u32[]{:S(2)}, u32[]{:S(2)}) collective-permute-start(bf16[1040,128]{1,0:T(8,128)(2,1)S(1)} %collective-permute-done.10.refs_4_), channel_id=1, source_target_pairs={{1,2},{6,5},{9,10},{14,13},{17,18},{22,21},{25,26},{30,29}} | collective-permute-start | bytes 798728 | tf_op jit(solution)/shard_map/ppermute | solution.py:276
  30.2 0.7 %collective-permute-start.13 = (bf16[1040,128]{1,0:T(8,128)(2,1)S(1)}, bf16[1040,128]{1,0:T(8,128)(2,1)S(1)}, u32[]{:S(2)}, u32[]{:S(2)}) collective-permute-start(bf16[1040,128]{1,0:T(8,128)(2,1)S(1)} %collective-permute-done.10.refs_4_), channel_id=1, source_target_pairs={{3,2},{4,5},{11,10},{12,13},{19,18},{20,21},{27,26},{28,29}} | collective-permute-start | bytes 798728 | tf_op jit(solution)/shard_map/ppermute | solution.py:276
  30.9 0.7 %collective-permute-start.15 = (bf16[1040,128]{1,0:T(8,128)(2,1)S(1)}, bf16[1040,128]{1,0:T(8,128)(2,1)S(1)}, u32[]{:S(2)}, u32[]{:S(2)}) collective-permute-start(bf16[1040,128]{1,0:T(8,128)(2,1)S(1)} %collective-permute-done.14.refs_6_), channel_id=1, source_target_pairs={{3,2},{4,5},{11,10},{12,13},{19,18},{20,21},{27,26},{28,29}} | collective-permute-start | bytes 798728 | tf_op jit(solution)/shard_map/ppermute | solution.py:276
  31.6 0.8 %shard_map.39 = (bf16[512,1024]{1,0:T(8,128)(2,1)S(1)}, f32[1,512]{1,0:T(1,128)S(1)}, f32[8,512]{1,0:T(8,128)S(1)}) custom-call(bf16[1040,128]{1,0:T(8,128)(2,1)S(1)} %get-tuple-element.33.refs_0_, bf16[1040,128]{1,0:T(8,128)(2,1)S(1)} %collective-permute-done.3.refs_1_, bf16[1040,128]{1,0:T(8,128)(2,1)S(1)} %collective-permute-done.4.refs_2_, ...), custom_call_target="tpu_custom_call" | custom-call | flops 536870912 | bytes 1048576 | tf_op jit(solution)/shard_map/pallas_call | solution.py:23
  32.4 4.6 %collective-permute-start.16 = (bf16[1040,128]{1,0:T(8,128)(2,1)S(1)}, bf16[1040,128]{1,0:T(8,128)(2,1)S(1)}, u32[]{:S(2)}, u32[]{:S(2)}) collective-permute-start(bf16[1040,128]{1,0:T(8,128)(2,1)S(1)} %collective-permute-done.14.refs_6_), channel_id=1, source_target_pairs={{0,2},{7,5},{8,10},{15,13},{16,18},{23,21},{24,26},{31,29}} | collective-permute-start | bytes 798728 | tf_op jit(solution)/shard_map/ppermute | solution.py:276
  37.0 0.7 %collective-permute-start.17 = (bf16[1040,128]{1,0:T(8,128)(2,1)S(1)}, bf16[1040,128]{1,0:T(8,128)(2,1)S(1)}, u32[]{:S(2)}, u32[]{:S(2)}) collective-permute-start(bf16[1040,128]{1,0:T(8,128)(2,1)S(1)} %collective-permute-done.14.refs_6_), channel_id=1, source_target_pairs={{1,2},{6,5},{9,10},{14,13},{17,18},{22,21},{25,26},{30,29}} | collective-permute-start | bytes 798728 | tf_op jit(solution)/shard_map/ppermute | solution.py:276
  37.7 1.4 %shard_map.40 = (bf16[512,1024]{1,0:T(8,128)(2,1)S(1)}, f32[1,512]{1,0:T(1,128)S(1)}, f32[8,512]{1,0:T(8,128)S(1)}, f32[8,512]{1,0:T(8,128)S(1)}) custom-call(bf16[512,1024]{1,0:T(8,128)(2,1)S(1)} %get-tuple-element.34.refs_0_, f32[1,512]{1,0:T(1,128)S(1)} %get-tuple-element.35.refs_1_.refs_2_.refs_3_.refs_4_, ...), custom_call_target="tpu_custom_call" | custom-call | flops 1073741824 | bytes 2097152 | tf_op jit(solution)/shard_map/pallas_call | solution.py:23
  39.1 1.9 %shard_map.41 = (bf16[512,1024]{1,0:T(8,128)(2,1)S(1)}, f32[1,512]{1,0:T(1,128)S(1)}, f32[8,512]{1,0:T(8,128)S(1)}, f32[8,512]{1,0:T(8,128)S(1)}, f32[8,512]{1,0:T(8,128)S(1)}) custom-call(bf16[512,1024]{1,0:T(8,128)(2,1)S(1)} %get-tuple-element.34.refs_0_, bf16[512,1024]{1,0:T(8,128)(2,1)S(1)} %get-tuple-element.37.refs_1_, ...), custom_call_target="tpu_custom_call" | custom-call | flops 1610612736 | bytes 3145728 | tf_op jit(solution)/shard_map/pallas_call | solution.py:23
  41.1 1.3 %shard_map.42 = (bf16[256,1024]{1,0:T(8,128)(2,1)S(1)}, f32[1,256]{1,0:T(1,128)S(1)}, f32[8,256]{1,0:T(8,128)S(1)}, f32[8,512]{1,0:T(8,128)S(1)}, f32[8,512]{1,0:T(8,128)S(1)}, /*index=5*/f32[8,512]{1,0:T(8,128)S(1)}) custom-call(bf16[512,1024]{1,0:T(8,128)(2,1)S(1)} %get-tuple-element.34.refs_0_, bf16[512,1024]{1,0:T(8,128)(2,1)S(1)} %get-tuple-element.37.refs_1_, ...), custom_call_target="tpu_custom_call" | custom-call | flops 939524096 | bytes 3670016 | tf_op jit(solution)/shard_map/pallas_call | solution.py:23
  42.4 1.5 %shard_map.43 = f32[32,128]{1,0:T(8,128)S(1)} custom-call(bf16[512,1024]{1,0:T(8,128)(2,1)S(1)} %get-tuple-element.34.refs_0_, bf16[512,1024]{1,0:T(8,128)(2,1)S(1)} %get-tuple-element.37.refs_1_, bf16[512,1024]{1,0:T(8,128)(2,1)S(1)} %get-tuple-element.40.refs_2_, bf16[256,1024]{1,0:T(8,128)(2,1)S(1)} %get-tuple-element.43.refs_3_, ...), custom_call_target="tpu_custom_call" | custom-call | flops 1073741824 | bytes 4194304 | tf_op jit(solution)/shard_map/pallas_call | solution.py:23
  44.0 13.8 %all_to_all.11 = f32[32,1,128]{2,1,0:T(1,128)S(1)} all-to-all(f32[32,1,128]{2,1,0:T(1,128)S(1)} %bitcast.7), channel_id=1, replica_groups=mesh['group'=8,'blk'=4] {'group','blk'}, dimensions={0} | all-to-all | bytes 32768 | tf_op jit(solution)/shard_map/all_to_all | solution.py:371
  57.8 0.8 %shard_map.44 = f32[1,256]{1,0:T(1,128)} custom-call(s32[1,256]{1,0:T(1,128)S(1)} %get-tuple-element.30.pos_ref, f32[32,128]{1,0:T(8,128)S(1)} %bitcast.8), custom_call_target="tpu_custom_call" | custom-call | flops 1000000 | bytes 100000 | tf_op jit(solution)/shard_map/pallas_call | solution.py:23
  (19 shorter events, 0.0 us)
Async XLA Ops:
  0.0 0.7 %copy-start.1 = (s32[256,1]{0,1:T(1,128)S(1)}, s32[256,1]{0,1:T(1,128)}, u32[]{:S(2)}) copy-start(s32[256,1]{0,1:T(1,128)} %param.4) | copy-start | bytes 3076
  0.0 3.5 %collective-permute-start = (bf16[256,1024]{1,0:T(8,128)(2,1)}, bf16[256,1024]{1,0:T(8,128)(2,1)S(1)}, u32[]{:S(2)}, u32[]{:S(2)}) collective-permute-start(bf16[256,1024]{1,0:T(8,128)(2,1)} %emb_hbm.1), channel_id=1, source_target_pairs={{0,4},{4,0},{8,12},{12,8},{16,20},{20,16},{24,28},{28,24},{1,5},{5... | collective-permute-start | bytes 1572872 | tf_op jit(solution)/shard_map/ppermute | solution.py:262
  0.7 0.7 %copy-start.2 = (s32[256]{0:T(256)S(1)}, s32[256]{0:T(256)}, u32[]{:S(2)}) copy-start(s32[256]{0:T(256)} %param.5) | copy-start | bytes 3076
  0.7 2.8 %collective-permute-start.1 = (s32[1,256]{1,0:T(1,128)S(1)}, s32[1,256]{1,0:T(1,128)S(1)}, u32[]{:S(2)}, u32[]{:S(2)}) collective-permute-start(s32[1,256]{1,0:T(1,128)S(1)} %bitcast.9), channel_id=1, source_target_pairs={{0,4},{4,0},{8,12},{12,8},{16,20},{20,16},{24,28},{28,24},{1,5},{5... | collective-permute-start | bytes 3080 | tf_op jit(solution)/shard_map/ppermute | solution.py:262
  1.4 2.1 %collective-permute-start.2 = (s32[1,256]{1,0:T(1,128)S(1)}, s32[1,256]{1,0:T(1,128)S(1)}, u32[]{:S(2)}, u32[]{:S(2)}) collective-permute-start(s32[1,256]{1,0:T(1,128)S(1)} %bitcast.11), channel_id=1, source_target_pairs={{0,4},{4,0},{8,12},{12,8},{16,20},{20,16},{24,28},{28,24},{1,5},{5... | collective-permute-start | bytes 3080 | tf_op jit(solution)/shard_map/ppermute | solution.py:262
  1.9 1.0 %copy-start = (bf16[256,1024]{1,0:T(8,128)(2,1)S(1)}, bf16[256,1024]{1,0:T(8,128)(2,1)}, u32[]{:S(2)}) copy-start(bf16[256,1024]{1,0:T(8,128)(2,1)} %emb_hbm.1) | copy-start | bytes 1572868
  4.1 10.0 %collective-permute-start.3 = (bf16[1040,128]{1,0:T(8,128)(2,1)S(1)}, bf16[1040,128]{1,0:T(8,128)(2,1)S(1)}, u32[]{:S(2)}, u32[]{:S(2)}) collective-permute-start(bf16[1040,128]{1,0:T(8,128)(2,1)S(1)} %get-tuple-element.33.refs_0_), channel_id=1, source_target_pairs={{0,2},{7,5},{8,10},{15,13},{16,18},{23,21},{24,26},{31,29}} | collective-permute-start | bytes 798728 | tf_op jit(solution)/shard_map/ppermute | solution.py:276
  9.6 7.8 %collective-permute-start.6 = (bf16[1040,128]{1,0:T(8,128)(2,1)S(1)}, bf16[1040,128]{1,0:T(8,128)(2,1)S(1)}, u32[]{:S(2)}, u32[]{:S(2)}) collective-permute-start(bf16[1040,128]{1,0:T(8,128)(2,1)S(1)} %get-tuple-element.36), channel_id=1, source_target_pairs={{0,8},{4,12},{8,0},{12,4},{16,24},{20,28},{24,16},{28,20},{1,9},{5... | collective-permute-start | bytes 798728 | tf_op jit(solution)/shard_map/ppermute | solution.py:259
  11.1 11.5 %collective-permute-start.4 = (bf16[1040,128]{1,0:T(8,128)(2,1)S(1)}, bf16[1040,128]{1,0:T(8,128)(2,1)S(1)}, u32[]{:S(2)}, u32[]{:S(2)}) collective-permute-start(bf16[1040,128]{1,0:T(8,128)(2,1)S(1)} %get-tuple-element.33.refs_0_), channel_id=1, source_target_pairs={{1,2},{6,5},{9,10},{14,13},{17,18},{22,21},{25,26},{30,29}} | collective-permute-start | bytes 798728 | tf_op jit(solution)/shard_map/ppermute | solution.py:276
  11.8 11.5 %collective-permute-start.5 = (bf16[1040,128]{1,0:T(8,128)(2,1)S(1)}, bf16[1040,128]{1,0:T(8,128)(2,1)S(1)}, u32[]{:S(2)}, u32[]{:S(2)}) collective-permute-start(bf16[1040,128]{1,0:T(8,128)(2,1)S(1)} %get-tuple-element.33.refs_0_), channel_id=1, source_target_pairs={{3,2},{4,5},{11,10},{12,13},{19,18},{20,21},{27,26},{28,29}} | collective-permute-start | bytes 798728 | tf_op jit(solution)/shard_map/ppermute | solution.py:276
  12.5 14.2 %collective-permute-start.10 = (bf16[1040,128]{1,0:T(8,128)(2,1)S(1)}, bf16[1040,128]{1,0:T(8,128)(2,1)S(1)}, u32[]{:S(2)}, u32[]{:S(2)}) collective-permute-start(bf16[1040,128]{1,0:T(8,128)(2,1)S(1)} %get-tuple-element.39), channel_id=1, source_target_pairs={{0,16},{4,20},{8,24},{12,28},{16,0},{20,4},{24,8},{28,12},{1,17},{... | collective-permute-start | bytes 798728 | tf_op jit(solution)/shard_map/ppermute | solution.py:259
  14.1 15.4 %collective-permute-start.14 = (bf16[1040,128]{1,0:T(8,128)(2,1)S(1)}, bf16[1040,128]{1,0:T(8,128)(2,1)S(1)}, u32[]{:S(2)}, u32[]{:S(2)}) collective-permute-start(bf16[1040,128]{1,0:T(8,128)(2,1)S(1)} %get-tuple-element.42), channel_id=1, source_target_pairs={{0,24},{4,28},{8,16},{12,20},{16,8},{20,12},{24,0},{28,4},{1,25},{... | collective-permute-start | bytes 798728 | tf_op jit(solution)/shard_map/ppermute | solution.py:259
  17.3 12.8 %collective-permute-start.7 = (bf16[1040,128]{1,0:T(8,128)(2,1)S(1)}, bf16[1040,128]{1,0:T(8,128)(2,1)S(1)}, u32[]{:S(2)}, u32[]{:S(2)}) collective-permute-start(bf16[1040,128]{1,0:T(8,128)(2,1)S(1)} %collective-permute-done.6.refs_2_), channel_id=1, source_target_pairs={{0,2},{7,5},{8,10},{15,13},{16,18},{23,21},{24,26},{31,29}} | collective-permute-start | bytes 798728 | tf_op jit(solution)/shard_map/ppermute | solution.py:276
  22.6 8.2 %collective-permute-start.8 = (bf16[1040,128]{1,0:T(8,128)(2,1)S(1)}, bf16[1040,128]{1,0:T(8,128)(2,1)S(1)}, u32[]{:S(2)}, u32[]{:S(2)}) collective-permute-start(bf16[1040,128]{1,0:T(8,128)(2,1)S(1)} %collective-permute-done.6.refs_2_), channel_id=1, source_target_pairs={{1,2},{6,5},{9,10},{14,13},{17,18},{22,21},{25,26},{30,29}} | collective-permute-start | bytes 798728 | tf_op jit(solution)/shard_map/ppermute | solution.py:276
  23.3 9.0 %collective-permute-start.9 = (bf16[1040,128]{1,0:T(8,128)(2,1)S(1)}, bf16[1040,128]{1,0:T(8,128)(2,1)S(1)}, u32[]{:S(2)}, u32[]{:S(2)}) collective-permute-start(bf16[1040,128]{1,0:T(8,128)(2,1)S(1)} %collective-permute-done.6.refs_2_), channel_id=1, source_target_pairs={{3,2},{4,5},{11,10},{12,13},{19,18},{20,21},{27,26},{28,29}} | collective-permute-start | bytes 798728 | tf_op jit(solution)/shard_map/ppermute | solution.py:276
  26.7 10.3 %collective-permute-start.11 = (bf16[1040,128]{1,0:T(8,128)(2,1)S(1)}, bf16[1040,128]{1,0:T(8,128)(2,1)S(1)}, u32[]{:S(2)}, u32[]{:S(2)}) collective-permute-start(bf16[1040,128]{1,0:T(8,128)(2,1)S(1)} %collective-permute-done.10.refs_4_), channel_id=1, source_target_pairs={{0,2},{7,5},{8,10},{15,13},{16,18},{23,21},{24,26},{31,29}} | collective-permute-start | bytes 798728 | tf_op jit(solution)/shard_map/ppermute | solution.py:276
  29.5 9.6 %collective-permute-start.12 = (bf16[1040,128]{1,0:T(8,128)(2,1)S(1)}, bf16[1040,128]{1,0:T(8,128)(2,1)S(1)}, u32[]{:S(2)}, u32[]{:S(2)}) collective-permute-start(bf16[1040,128]{1,0:T(8,128)(2,1)S(1)} %collective-permute-done.10.refs_4_), channel_id=1, source_target_pairs={{1,2},{6,5},{9,10},{14,13},{17,18},{22,21},{25,26},{30,29}} | collective-permute-start | bytes 798728 | tf_op jit(solution)/shard_map/ppermute | solution.py:276
  30.2 8.9 %collective-permute-start.13 = (bf16[1040,128]{1,0:T(8,128)(2,1)S(1)}, bf16[1040,128]{1,0:T(8,128)(2,1)S(1)}, u32[]{:S(2)}, u32[]{:S(2)}) collective-permute-start(bf16[1040,128]{1,0:T(8,128)(2,1)S(1)} %collective-permute-done.10.refs_4_), channel_id=1, source_target_pairs={{3,2},{4,5},{11,10},{12,13},{19,18},{20,21},{27,26},{28,29}} | collective-permute-start | bytes 798728 | tf_op jit(solution)/shard_map/ppermute | solution.py:276
  30.9 10.2 %collective-permute-start.15 = (bf16[1040,128]{1,0:T(8,128)(2,1)S(1)}, bf16[1040,128]{1,0:T(8,128)(2,1)S(1)}, u32[]{:S(2)}, u32[]{:S(2)}) collective-permute-start(bf16[1040,128]{1,0:T(8,128)(2,1)S(1)} %collective-permute-done.14.refs_6_), channel_id=1, source_target_pairs={{3,2},{4,5},{11,10},{12,13},{19,18},{20,21},{27,26},{28,29}} | collective-permute-start | bytes 798728 | tf_op jit(solution)/shard_map/ppermute | solution.py:276
  32.4 10.0 %collective-permute-start.16 = (bf16[1040,128]{1,0:T(8,128)(2,1)S(1)}, bf16[1040,128]{1,0:T(8,128)(2,1)S(1)}, u32[]{:S(2)}, u32[]{:S(2)}) collective-permute-start(bf16[1040,128]{1,0:T(8,128)(2,1)S(1)} %collective-permute-done.14.refs_6_), channel_id=1, source_target_pairs={{0,2},{7,5},{8,10},{15,13},{16,18},{23,21},{24,26},{31,29}} | collective-permute-start | bytes 798728 | tf_op jit(solution)/shard_map/ppermute | solution.py:276
  37.0 5.4 %collective-permute-start.17 = (bf16[1040,128]{1,0:T(8,128)(2,1)S(1)}, bf16[1040,128]{1,0:T(8,128)(2,1)S(1)}, u32[]{:S(2)}, u32[]{:S(2)}) collective-permute-start(bf16[1040,128]{1,0:T(8,128)(2,1)S(1)} %collective-permute-done.14.refs_6_), channel_id=1, source_target_pairs={{1,2},{6,5},{9,10},{14,13},{17,18},{22,21},{25,26},{30,29}} | collective-permute-start | bytes 798728 | tf_op jit(solution)/shard_map/ppermute | solution.py:276

commit v4 on v3

--- a/solution.py
+++ b/solution.py
@@ -9,7 +9,7 @@
 
 
 LANES = 128
-META = 16
+META = 8
 VMEM = pl.BlockSpec(memory_space=pltpu.VMEM)
 F32 = jnp.float32
 BF16 = jnp.bfloat16
@@ -31,13 +31,13 @@
     )(*operands)
 
 
-def gathered(emb_ref, dest_ref, rank_ref, chip, core, chips, cap):
+def gathered(emb_ref, code_ref, chip, core, chips, cap):
     rows = emb_ref.shape[0]
     clusters = max(16, 2 * chips)
     values = emb_ref[...].astype(F32)
     norm = lax.rsqrt(jnp.sum(values * values, axis=1, keepdims=True) + 1e-06)
     unit = (values * norm).astype(BF16)
-    dest, rank = dest_ref[...], rank_ref[...]
+    dest, rank = code_ref[0:1, :], code_ref[1:2, :]
     onehot = (lax.broadcasted_iota(jnp.int32, (clusters, rows), 0) == dest).astype(F32)
     row = lax.broadcasted_iota(jnp.int32, (rows, rows), 0)
     column = lax.broadcasted_iota(jnp.int32, (rows, rows), 1)
@@ -48,7 +48,7 @@
     pos = jnp.where((dest & 1) == core, where, -1)
     pick = lax.broadcasted_iota(jnp.int32, (chips * cap, rows), 0) == pos
     pick = pick.astype(F32).astype(BF16)
-    digits = lax.broadcasted_iota(jnp.int32, (META, rows), 0)
+    digits = lax.broadcasted_iota(jnp.int32, (2 * META, rows), 0)
     digits = jnp.where(
         digits == 0, rank >> 8, jnp.where(digits == 1, rank & 255, jnp.where(digits == 2, 1, 0))
     )
@@ -59,35 +59,19 @@
     return packed, digits, where, dest
 
 
-def own_body(cap, chips, planes, emb_hbm, dest_hbm, rank_hbm, *refs):
-    packed_ref, digits_ref, pos_ref, emb_ref, dest_ref, rank_ref, sems = refs
-    copies = [
-        pltpu.make_async_copy(source, target, sems.at[i])
-        for i, (source, target) in enumerate(
-            ((emb_hbm, emb_ref), (dest_hbm, dest_ref), (rank_hbm, rank_ref))
-        )
-    ]
-    for copy in copies:
-        copy.start()
-    for copy in copies:
-        copy.wait()
+def own_body(cap, chips, emb_ref, code_ref, packed_ref, digits_ref, pos_ref):
     group = lax.axis_index("group")
-    packed, digits, where, dest = gathered(
-        emb_ref, dest_ref, rank_ref, group >> 1, group & 1, chips, cap
-    )
+    packed, digits, where, dest = gathered(emb_ref, code_ref, group >> 1, group & 1, chips, cap)
     packed_ref[...] = packed
     digits_ref[...] = digits
     parity = dest & 1
-    row, lane = dest * planes + planes // 2 - parity, where % cap + cap * (parity ^ (group & 1))
-    pos_ref[...] = row * LANES + lane
-
-
-def pack_body(cap, chips, emb_ref, dest_ref, rank_ref, own, own_digits, *refs):
+    pos_ref[...] = dest * LANES + where % cap + cap * (parity ^ (group & 1))
+
+
+def pack_body(cap, chips, emb_ref, code_ref, own, own_digits, *refs):
     group = lax.axis_index("group")
     pieces = emb_ref.shape[1] // LANES
-    mate, mate_digits, _, _ = gathered(
-        emb_ref, dest_ref, rank_ref, group >> 1, group & 1, chips, cap
-    )
+    mate, mate_digits, _, _ = gathered(emb_ref, code_ref, group >> 1, group & 1, chips, cap)
     for s in range(chips):
         part = slice(s * cap, (s + 1) * cap)
         for k in range(pieces):
@@ -95,7 +79,7 @@
             refs[s][k * LANES : k * LANES + cap, :] = own[part, lanes]
             refs[s][k * LANES + cap : (k + 1) * LANES, :] = mate[part, lanes]
         refs[s][pieces * LANES : pieces * LANES + META, :] = jnp.concatenate(
-            [own_digits[:, part], mate_digits[:, part]], axis=1
+            [own_digits[:META, part], mate_digits[:META, part]], axis=1
         ).astype(BF16)
 
 
@@ -220,18 +204,16 @@
             out[pl.ds(device + planes, 1), :] = best
 
 
-def final_body(pos_ref, table_ref, out_ref):
-    rows, pos = pos_ref.shape[1], pos_ref[...]
-    pick = lax.broadcasted_iota(jnp.int32, (LANES, rows), 0) == pos % LANES
-    got = lax.dot_general(
-        table_ref[...],
-        pick.astype(F32),
-        (((1,), (0,)), ((), ())),
-        precision=lax.Precision.HIGHEST,
-        preferred_element_type=F32,
-    )
-    mine = lax.broadcasted_iota(jnp.int32, got.shape, 0) == pos // LANES
-    out_ref[...] = jnp.sum(jnp.where(mine, got, 0.0), axis=0, keepdims=True)
+def final_body(planes, pos_ref, table_ref, out_ref):
+    groups = table_ref.shape[0] // planes
+    pos = pos_ref[...]
+    rows = [g * planes + planes // 2 - (g & 1) for g in range(groups)]
+    table = jnp.concatenate([table_ref[r : r + 1, :] for r in rows], axis=0)
+    for i in range(0, pos.shape[1], LANES):
+        here = jnp.broadcast_to(pos[:, i : i + LANES], (groups, LANES))
+        got = jnp.take_along_axis(table, here % LANES, axis=1)
+        mine = lax.broadcasted_iota(jnp.int32, here.shape, 0) == here // LANES
+        out_ref[:, i : i + LANES] = jnp.sum(jnp.where(mine, got, 0.0), axis=0, keepdims=True)
 
 
 def chunks_of(chips):
@@ -276,33 +258,26 @@
             arrived.append(lax.ppermute(value, ("group", "blk"), meeting(step)))
         return arrived
 
-    dest, rank = dest_group.reshape(1, rows), order_rank.reshape(1, rows)
+    code = jnp.concatenate([dest_group.reshape(1, rows), order_rank.reshape(1, rows)], axis=0)
     mate = to_core(embeddings)
-    mate_dest, mate_rank = to_core(dest), to_core(rank)
+    mate_code = to_core(code)
     flops = 2 * chips * cap * rows * width
     own = call(
-        functools.partial(own_body, cap, chips, planes),
+        functools.partial(own_body, cap, chips),
         [
             jax.ShapeDtypeStruct((chips * cap, width), BF16),
-            floats(META, chips * cap),
+            floats(2 * META, chips * cap),
             jax.ShapeDtypeStruct((1, rows), jnp.int32),
         ],
-        [embeddings, dest, rank],
+        [embeddings, code],
         flops,
         4 * rows * width,
         16 << 20,
-        scratch=[
-            pltpu.VMEM((rows, width), BF16),
-            pltpu.VMEM((1, rows), jnp.int32),
-            pltpu.VMEM((1, rows), jnp.int32),
-            pltpu.SemaphoreType.DMA((3,)),
-        ],
-        spec=pl.BlockSpec(memory_space=pltpu.HBM),
     )
     packed = call(
         functools.partial(pack_body, cap, chips),
         [blocks(1)] * chips,
-        [mate, mate_dest, mate_rank, own[0], own[1]],
+        [mate, mate_code, own[0], own[1]],
         flops,
         8 * rows * width,
         16 << 20,
@@ -369,7 +344,8 @@
             ranks.append(best[1])
             found += best[3:] + best[2:3]
     table = lax.all_to_all(best, ("group", "blk"), 0, 0, tiled=True)
-    result = call(final_body, floats(1, rows), [pos, table], 1000000, 100000, 4 << 20)
+    final = functools.partial(final_body, planes)
+    result = call(final, floats(1, rows), [pos, table], 1000000, 100000, 4 << 20)
     return result.reshape(rows)
 
 

time: 58.9 us -> 57.9 us (0.983)
  blocking collectives: 13.8 us -> 12.7 us
  starting transfers between devices: 31.4 us -> 32.2 us
  waiting for transfers between devices: 2.74 us -> 2.01 us
    ppermute x12, starting transfers between devices: 23.6 us -> 25.1 us  [gather(): arrived.append(lax.ppermute(value, ('group', 'blk'), meeting(step)))]
    all_to_all x1, blocking collectives: 13.8 us -> 12.7 us  [on_device(): table = lax.all_to_all(best, ('group', 'blk'), 0, 0, tiled=True)]
    ppermute x3, waiting for transfers between devices: 2.7 us -> 1.67 us  [to_chip(): return lax.ppermute(value, 'group', [(i, i ^ 2 * s) for i in range(groups)])]
    ppermute x3 -> x2, starting transfers between devices: 1.48 us -> 0.56 us  [to_core(): return lax.ppermute(value, 'group', [(i, i ^ 1) for i in range(groups)])]
  transfers between devices with their start and end apart: 18 -> 17, of which waited for: 1 -> 2; matrix products, arithmetic and copies ran while one was open for 0% -> 0% of each run, Pallas kernels for 10% -> 10%
where the time goes in v4:
time: 57.9 us; the launch traced here: 57.6 us
  starting transfers between devices  32.2 us (56%)
  blocking collectives  12.7 us (22%)
  Pallas kernels  8.68 us (15%)
  waiting for transfers between devices  2.01 us (3%)
  local copies, waits for them, and re-layouts  1.73 us (3%)
    ppermute x12, starting transfers between devices, gather(): arrived.append(lax.ppermute(value, ('group', 'blk'), meeting(step)))  25.1 us
    all_to_all x1, blocking collectives, on_device(): table = lax.all_to_all(best, ('group', 'blk'), 0, 0, tiled=True)  12.7 us
    pallas_call x8, Pallas kernels, call(): pl.pallas_call(body, out_shape=outs, in_specs=[spec] * len(operands), out...  8.68 us
    ppermute x3, starting transfers between devices, to_chip(): return lax.ppermute(value, 'group', [(i, i ^ 2 * s) for i in range(groups)])  6.55 us
    unnamed x6, local copies, waits for them, and re-layouts  1.73 us
    ppermute x3, waiting for transfers between devices, to_chip(): return lax.ppermute(value, 'group', [(i, i ^ 2 * s) for i in range(groups)])  1.67 us
  transfers between devices with their start and end apart: 17, of which 2 were waited for; matrix products, arithmetic and copies ran while one was open for 0% of the time, Pallas kernels for 10%

profile of v4, /device:TPU:0, one launch (start us, length us, event | category | flops | bytes accessed | tf_op | source)
XLA Modules:
  0.0 57.6 jit_solution(585944239674006055)
XLA Ops:
  0.0 0.5 collective-permute-start
  0.5 0.7 %copy-done.2 = s32[256,1]{0,1:T(1,128)S(1)} copy-done((s32[256,1]{0,1:T(1,128)S(1)}, s32[256,1]{0,1:T(1,128)}, u32[]{:S(2)}) %copy-start.2) | copy-done | bytes 1048
  1.2 0.0 copy-done.1
  1.2 0.1 collective-permute-start.1
  1.3 1.0 %copy-done = bf16[256,1024]{1,0:T(8,128)(2,1)S(1)} copy-done((bf16[256,1024]{1,0:T(8,128)(2,1)S(1)}, bf16[256,1024]{1,0:T(8,128)(2,1)}, u32[]{:S(2)}) %copy-start) | copy-done | bytes 524312
  2.3 0.5 shard_map.37
  2.8 0.0 collective-permute-done.1.code_ref
  2.8 0.5 shard_map.38
  3.4 6.0 %collective-permute-start.2 = (bf16[1032,128]{1,0:T(8,128)(2,1)S(1)}, bf16[1032,128]{1,0:T(8,128)(2,1)S(1)}, u32[]{:S(2)}, u32[]{:S(2)}) collective-permute-start(bf16[1032,128]{1,0:T(8,128)(2,1)S(1)} %get-tuple-element.33.refs_0_), channel_id=1, source_target_pairs={{0,2},{7,5},{8,10},{15,13},{16,18},{23,21},{24,26},{31,29}} | collective-permute-start | bytes 792584 | tf_op jit(solution)/shard_map/ppermute | solution.py:258
  9.4 1.6 %collective-permute-start.5 = (bf16[1032,128]{1,0:T(8,128)(2,1)S(1)}, bf16[1032,128]{1,0:T(8,128)(2,1)S(1)}, u32[]{:S(2)}, u32[]{:S(2)}) collective-permute-start(bf16[1032,128]{1,0:T(8,128)(2,1)S(1)} %get-tuple-element.36), channel_id=1, source_target_pairs={{0,8},{4,12},{8,0},{12,4},{16,24},{20,28},{24,16},{28,20},{1,9},{5... | collective-permute-start | bytes 792584 | tf_op jit(solution)/shard_map/ppermute | solution.py:241
  10.9 0.7 %collective-permute-start.3 = (bf16[1032,128]{1,0:T(8,128)(2,1)S(1)}, bf16[1032,128]{1,0:T(8,128)(2,1)S(1)}, u32[]{:S(2)}, u32[]{:S(2)}) collective-permute-start(bf16[1032,128]{1,0:T(8,128)(2,1)S(1)} %get-tuple-element.33.refs_0_), channel_id=1, source_target_pairs={{1,2},{6,5},{9,10},{14,13},{17,18},{22,21},{25,26},{30,29}} | collective-permute-start | bytes 792584 | tf_op jit(solution)/shard_map/ppermute | solution.py:258
  11.6 0.7 %collective-permute-start.4 = (bf16[1032,128]{1,0:T(8,128)(2,1)S(1)}, bf16[1032,128]{1,0:T(8,128)(2,1)S(1)}, u32[]{:S(2)}, u32[]{:S(2)}) collective-permute-start(bf16[1032,128]{1,0:T(8,128)(2,1)S(1)} %get-tuple-element.33.refs_0_), channel_id=1, source_target_pairs={{3,2},{4,5},{11,10},{12,13},{19,18},{20,21},{27,26},{28,29}} | collective-permute-start | bytes 792584 | tf_op jit(solution)/shard_map/ppermute | solution.py:258
  12.3 1.6 %collective-permute-start.9 = (bf16[1032,128]{1,0:T(8,128)(2,1)S(1)}, bf16[1032,128]{1,0:T(8,128)(2,1)S(1)}, u32[]{:S(2)}, u32[]{:S(2)}) collective-permute-start(bf16[1032,128]{1,0:T(8,128)(2,1)S(1)} %get-tuple-element.39), channel_id=1, source_target_pairs={{0,16},{4,20},{8,24},{12,28},{16,0},{20,4},{24,8},{28,12},{1,17},{... | collective-permute-start | bytes 792584 | tf_op jit(solution)/shard_map/ppermute | solution.py:241
  13.9 0.3 collective-permute-done.2.refs_1_
  14.2 3.4 %collective-permute-start.13 = (bf16[1032,128]{1,0:T(8,128)(2,1)S(1)}, bf16[1032,128]{1,0:T(8,128)(2,1)S(1)}, u32[]{:S(2)}, u32[]{:S(2)}) collective-permute-start(bf16[1032,128]{1,0:T(8,128)(2,1)S(1)} %get-tuple-element.42), channel_id=1, source_target_pairs={{0,24},{4,28},{8,16},{12,20},{16,8},{20,12},{24,0},{28,4},{1,25},{... | collective-permute-start | bytes 792584 | tf_op jit(solution)/shard_map/ppermute | solution.py:241
  17.6 5.3 %collective-permute-start.6 = (bf16[1032,128]{1,0:T(8,128)(2,1)S(1)}, bf16[1032,128]{1,0:T(8,128)(2,1)S(1)}, u32[]{:S(2)}, u32[]{:S(2)}) collective-permute-start(bf16[1032,128]{1,0:T(8,128)(2,1)S(1)} %collective-permute-done.5.refs_2_), channel_id=1, source_target_pairs={{0,2},{7,5},{8,10},{15,13},{16,18},{23,21},{24,26},{31,29}} | collective-permute-start | bytes 792584 | tf_op jit(solution)/shard_map/ppermute | solution.py:258
  22.9 0.7 %collective-permute-start.7 = (bf16[1032,128]{1,0:T(8,128)(2,1)S(1)}, bf16[1032,128]{1,0:T(8,128)(2,1)S(1)}, u32[]{:S(2)}, u32[]{:S(2)}) collective-permute-start(bf16[1032,128]{1,0:T(8,128)(2,1)S(1)} %collective-permute-done.5.refs_2_), channel_id=1, source_target_pairs={{1,2},{6,5},{9,10},{14,13},{17,18},{22,21},{25,26},{30,29}} | collective-permute-start | bytes 792584 | tf_op jit(solution)/shard_map/ppermute | solution.py:258
  23.6 0.7 %collective-permute-start.8 = (bf16[1032,128]{1,0:T(8,128)(2,1)S(1)}, bf16[1032,128]{1,0:T(8,128)(2,1)S(1)}, u32[]{:S(2)}, u32[]{:S(2)}) collective-permute-start(bf16[1032,128]{1,0:T(8,128)(2,1)S(1)} %collective-permute-done.5.refs_2_), channel_id=1, source_target_pairs={{3,2},{4,5},{11,10},{12,13},{19,18},{20,21},{27,26},{28,29}} | collective-permute-start | bytes 792584 | tf_op jit(solution)/shard_map/ppermute | solution.py:258
  24.3 1.7 %collective-permute-done.9.refs_4_ = bf16[1032,128]{1,0:T(8,128)(2,1)S(1)} collective-permute-done((bf16[1032,128]{1,0:T(8,128)(2,1)S(1)}, bf16[1032,128]{1,0:T(8,128)(2,1)S(1)}, u32[]{:S(2)}, u32[]{:S(2)}) %collective-permute-start.9) | collective-permute-done | bytes 264224 | tf_op jit(solution)/shard_map/ppermute | solution.py:241
  25.9 2.8 %collective-permute-start.10 = (bf16[1032,128]{1,0:T(8,128)(2,1)S(1)}, bf16[1032,128]{1,0:T(8,128)(2,1)S(1)}, u32[]{:S(2)}, u32[]{:S(2)}) collective-permute-start(bf16[1032,128]{1,0:T(8,128)(2,1)S(1)} %collective-permute-done.9.refs_4_), channel_id=1, source_target_pairs={{0,2},{7,5},{8,10},{15,13},{16,18},{23,21},{24,26},{31,29}} | collective-permute-start | bytes 792584 | tf_op jit(solution)/shard_map/ppermute | solution.py:258
  28.7 0.7 %collective-permute-start.11 = (bf16[1032,128]{1,0:T(8,128)(2,1)S(1)}, bf16[1032,128]{1,0:T(8,128)(2,1)S(1)}, u32[]{:S(2)}, u32[]{:S(2)}) collective-permute-start(bf16[1032,128]{1,0:T(8,128)(2,1)S(1)} %collective-permute-done.9.refs_4_), channel_id=1, source_target_pairs={{1,2},{6,5},{9,10},{14,13},{17,18},{22,21},{25,26},{30,29}} | collective-permute-start | bytes 792584 | tf_op jit(solution)/shard_map/ppermute | solution.py:258
  29.4 0.7 %collective-permute-start.12 = (bf16[1032,128]{1,0:T(8,128)(2,1)S(1)}, bf16[1032,128]{1,0:T(8,128)(2,1)S(1)}, u32[]{:S(2)}, u32[]{:S(2)}) collective-permute-start(bf16[1032,128]{1,0:T(8,128)(2,1)S(1)} %collective-permute-done.9.refs_4_), channel_id=1, source_target_pairs={{3,2},{4,5},{11,10},{12,13},{19,18},{20,21},{27,26},{28,29}} | collective-permute-start | bytes 792584 | tf_op jit(solution)/shard_map/ppermute | solution.py:258
  30.1 0.7 %collective-permute-start.14 = (bf16[1032,128]{1,0:T(8,128)(2,1)S(1)}, bf16[1032,128]{1,0:T(8,128)(2,1)S(1)}, u32[]{:S(2)}, u32[]{:S(2)}) collective-permute-start(bf16[1032,128]{1,0:T(8,128)(2,1)S(1)} %collective-permute-done.13.refs_6_), channel_id=1, source_target_pairs={{3,2},{4,5},{11,10},{12,13},{19,18},{20,21},{27,26},{28,29}} | collective-permute-start | bytes 792584 | tf_op jit(solution)/shard_map/ppermute | solution.py:258
  30.8 0.8 %shard_map.39 = (bf16[512,1024]{1,0:T(8,128)(2,1)S(1)}, f32[1,512]{1,0:T(1,128)S(1)}, f32[8,512]{1,0:T(8,128)S(1)}) custom-call(bf16[1032,128]{1,0:T(8,128)(2,1)S(1)} %get-tuple-element.33.refs_0_, bf16[1032,128]{1,0:T(8,128)(2,1)S(1)} %collective-permute-done.2.refs_1_, bf16[1032,128]{1,0:T(8,128)(2,1)S(1)} %collective-permute-done.3.refs_2_, ...), custom_call_target="tpu_custom_call" | custom-call | flops 536870912 | bytes 1048576 | tf_op jit(solution)/shard_map/pallas_call | solution.py:23
  31.6 5.6 %collective-permute-start.15 = (bf16[1032,128]{1,0:T(8,128)(2,1)S(1)}, bf16[1032,128]{1,0:T(8,128)(2,1)S(1)}, u32[]{:S(2)}, u32[]{:S(2)}) collective-permute-start(bf16[1032,128]{1,0:T(8,128)(2,1)S(1)} %collective-permute-done.13.refs_6_), channel_id=1, source_target_pairs={{0,2},{7,5},{8,10},{15,13},{16,18},{23,21},{24,26},{31,29}} | collective-permute-start | bytes 792584 | tf_op jit(solution)/shard_map/ppermute | solution.py:258
  37.3 0.7 %collective-permute-start.16 = (bf16[1032,128]{1,0:T(8,128)(2,1)S(1)}, bf16[1032,128]{1,0:T(8,128)(2,1)S(1)}, u32[]{:S(2)}, u32[]{:S(2)}) collective-permute-start(bf16[1032,128]{1,0:T(8,128)(2,1)S(1)} %collective-permute-done.13.refs_6_), channel_id=1, source_target_pairs={{1,2},{6,5},{9,10},{14,13},{17,18},{22,21},{25,26},{30,29}} | collective-permute-start | bytes 792584 | tf_op jit(solution)/shard_map/ppermute | solution.py:258
  38.0 1.4 %shard_map.40 = (bf16[512,1024]{1,0:T(8,128)(2,1)S(1)}, f32[1,512]{1,0:T(1,128)S(1)}, f32[8,512]{1,0:T(8,128)S(1)}, f32[8,512]{1,0:T(8,128)S(1)}) custom-call(bf16[512,1024]{1,0:T(8,128)(2,1)S(1)} %get-tuple-element.34.refs_0_, f32[1,512]{1,0:T(1,128)S(1)} %get-tuple-element.35.refs_1_.refs_2_.refs_3_.refs_4_, ...), custom_call_target="tpu_custom_call" | custom-call | flops 1073741824 | bytes 2097152 | tf_op jit(solution)/shard_map/pallas_call | solution.py:23
  39.4 1.9 %shard_map.41 = (bf16[512,1024]{1,0:T(8,128)(2,1)S(1)}, f32[1,512]{1,0:T(1,128)S(1)}, f32[8,512]{1,0:T(8,128)S(1)}, f32[8,512]{1,0:T(8,128)S(1)}, f32[8,512]{1,0:T(8,128)S(1)}) custom-call(bf16[512,1024]{1,0:T(8,128)(2,1)S(1)} %get-tuple-element.34.refs_0_, bf16[512,1024]{1,0:T(8,128)(2,1)S(1)} %get-tuple-element.37.refs_1_, ...), custom_call_target="tpu_custom_call" | custom-call | flops 1610612736 | bytes 3145728 | tf_op jit(solution)/shard_map/pallas_call | solution.py:23
  41.3 1.3 %shard_map.42 = (bf16[256,1024]{1,0:T(8,128)(2,1)S(1)}, f32[1,256]{1,0:T(1,128)S(1)}, f32[8,256]{1,0:T(8,128)S(1)}, f32[8,512]{1,0:T(8,128)S(1)}, f32[8,512]{1,0:T(8,128)S(1)}, /*index=5*/f32[8,512]{1,0:T(8,128)S(1)}) custom-call(bf16[512,1024]{1,0:T(8,128)(2,1)S(1)} %get-tuple-element.34.refs_0_, bf16[512,1024]{1,0:T(8,128)(2,1)S(1)} %get-tuple-element.37.refs_1_, ...), custom_call_target="tpu_custom_call" | custom-call | flops 939524096 | bytes 3670016 | tf_op jit(solution)/shard_map/pallas_call | solution.py:23
  42.7 1.5 %shard_map.43 = f32[32,128]{1,0:T(8,128)S(1)} custom-call(bf16[512,1024]{1,0:T(8,128)(2,1)S(1)} %get-tuple-element.34.refs_0_, bf16[512,1024]{1,0:T(8,128)(2,1)S(1)} %get-tuple-element.37.refs_1_, bf16[512,1024]{1,0:T(8,128)(2,1)S(1)} %get-tuple-element.40.refs_2_, bf16[256,1024]{1,0:T(8,128)(2,1)S(1)} %get-tuple-element.43.refs_3_, ...), custom_call_target="tpu_custom_call" | custom-call | flops 1073741824 | bytes 4194304 | tf_op jit(solution)/shard_map/pallas_call | solution.py:23
  44.2 12.7 %all_to_all.11 = f32[32,1,128]{2,1,0:T(1,128)S(1)} all-to-all(f32[32,1,128]{2,1,0:T(1,128)S(1)} %bitcast.7), channel_id=1, replica_groups=mesh['group'=8,'blk'=4] {'group','blk'}, dimensions={0} | all-to-all | bytes 32768 | tf_op jit(solution)/shard_map/all_to_all | solution.py:346
  56.9 0.7 %shard_map.44 = f32[1,256]{1,0:T(1,128)} custom-call(s32[1,256]{1,0:T(1,128)S(1)} %get-tuple-element.30.pos_ref, f32[32,128]{1,0:T(8,128)S(1)} %bitcast.8), custom_call_target="tpu_custom_call" | custom-call | flops 1000000 | bytes 100000 | tf_op jit(solution)/shard_map/pallas_call | solution.py:23
  (18 shorter events, 0.0 us)
Async XLA Ops:
  0.0 2.8 %collective-permute-start = (bf16[256,1024]{1,0:T(8,128)(2,1)}, bf16[256,1024]{1,0:T(8,128)(2,1)S(1)}, u32[]{:S(2)}, u32[]{:S(2)}) collective-permute-start(bf16[256,1024]{1,0:T(8,128)(2,1)} %emb_ref.1), channel_id=1, source_target_pairs={{0,4},{4,0},{8,12},{12,8},{16,20},{20,16},{24,28},{28,24},{1,5},{5... | collective-permute-start | bytes 1572872 | tf_op jit(solution)/shard_map/ppermute | solution.py:244
  0.5 0.7 %copy-start.2 = (s32[256,1]{0,1:T(1,128)S(1)}, s32[256,1]{0,1:T(1,128)}, u32[]{:S(2)}) copy-start(s32[256,1]{0,1:T(1,128)} %param.4) | copy-start | bytes 3076
  0.5 0.7 %copy-start.1 = (s32[256]{0:T(256)S(1)}, s32[256]{0:T(256)}, u32[]{:S(2)}) copy-start(s32[256]{0:T(256)} %param.5) | copy-start | bytes 3076
  1.2 1.6 %collective-permute-start.1 = (s32[2,256]{1,0:T(2,128)S(1)}, s32[2,256]{1,0:T(2,128)S(1)}, u32[]{:S(2)}, u32[]{:S(2)}) collective-permute-start(s32[2,256]{1,0:T(2,128)S(1)} %pad_add_fusion.code_ref), channel_id=1, source_target_pairs={{0,4},{4,0},{8,12},{12,8},{16,20},{20,16},{24,28},{28,24},{1,5},{5... | collective-permute-start | bytes 6152 | tf_op jit(solution)/shard_map/ppermute | solution.py:244
  1.3 1.0 %copy-start = (bf16[256,1024]{1,0:T(8,128)(2,1)S(1)}, bf16[256,1024]{1,0:T(8,128)(2,1)}, u32[]{:S(2)}) copy-start(bf16[256,1024]{1,0:T(8,128)(2,1)} %emb_ref.1) | copy-start | bytes 1572868
  3.4 10.8 %collective-permute-start.2 = (bf16[1032,128]{1,0:T(8,128)(2,1)S(1)}, bf16[1032,128]{1,0:T(8,128)(2,1)S(1)}, u32[]{:S(2)}, u32[]{:S(2)}) collective-permute-start(bf16[1032,128]{1,0:T(8,128)(2,1)S(1)} %get-tuple-element.33.refs_0_), channel_id=1, source_target_pairs={{0,2},{7,5},{8,10},{15,13},{16,18},{23,21},{24,26},{31,29}} | collective-permute-start | bytes 792584 | tf_op jit(solution)/shard_map/ppermute | solution.py:258
  9.4 8.2 %collective-permute-start.5 = (bf16[1032,128]{1,0:T(8,128)(2,1)S(1)}, bf16[1032,128]{1,0:T(8,128)(2,1)S(1)}, u32[]{:S(2)}, u32[]{:S(2)}) collective-permute-start(bf16[1032,128]{1,0:T(8,128)(2,1)S(1)} %get-tuple-element.36), channel_id=1, source_target_pairs={{0,8},{4,12},{8,0},{12,4},{16,24},{20,28},{24,16},{28,20},{1,9},{5... | collective-permute-start | bytes 792584 | tf_op jit(solution)/shard_map/ppermute | solution.py:241
  10.9 12.0 %collective-permute-start.3 = (bf16[1032,128]{1,0:T(8,128)(2,1)S(1)}, bf16[1032,128]{1,0:T(8,128)(2,1)S(1)}, u32[]{:S(2)}, u32[]{:S(2)}) collective-permute-start(bf16[1032,128]{1,0:T(8,128)(2,1)S(1)} %get-tuple-element.33.refs_0_), channel_id=1, source_target_pairs={{1,2},{6,5},{9,10},{14,13},{17,18},{22,21},{25,26},{30,29}} | collective-permute-start | bytes 792584 | tf_op jit(solution)/shard_map/ppermute | solution.py:258
  11.6 12.0 %collective-permute-start.4 = (bf16[1032,128]{1,0:T(8,128)(2,1)S(1)}, bf16[1032,128]{1,0:T(8,128)(2,1)S(1)}, u32[]{:S(2)}, u32[]{:S(2)}) collective-permute-start(bf16[1032,128]{1,0:T(8,128)(2,1)S(1)} %get-tuple-element.33.refs_0_), channel_id=1, source_target_pairs={{3,2},{4,5},{11,10},{12,13},{19,18},{20,21},{27,26},{28,29}} | collective-permute-start | bytes 792584 | tf_op jit(solution)/shard_map/ppermute | solution.py:258
  12.3 13.7 %collective-permute-start.9 = (bf16[1032,128]{1,0:T(8,128)(2,1)S(1)}, bf16[1032,128]{1,0:T(8,128)(2,1)S(1)}, u32[]{:S(2)}, u32[]{:S(2)}) collective-permute-start(bf16[1032,128]{1,0:T(8,128)(2,1)S(1)} %get-tuple-element.39), channel_id=1, source_target_pairs={{0,16},{4,20},{8,24},{12,28},{16,0},{20,4},{24,8},{28,12},{1,17},{... | collective-permute-start | bytes 792584 | tf_op jit(solution)/shard_map/ppermute | solution.py:241
  14.2 14.5 %collective-permute-start.13 = (bf16[1032,128]{1,0:T(8,128)(2,1)S(1)}, bf16[1032,128]{1,0:T(8,128)(2,1)S(1)}, u32[]{:S(2)}, u32[]{:S(2)}) collective-permute-start(bf16[1032,128]{1,0:T(8,128)(2,1)S(1)} %get-tuple-element.42), channel_id=1, source_target_pairs={{0,24},{4,28},{8,16},{12,20},{16,8},{20,12},{24,0},{28,4},{1,25},{... | collective-permute-start | bytes 792584 | tf_op jit(solution)/shard_map/ppermute | solution.py:241
  17.6 11.8 %collective-permute-start.6 = (bf16[1032,128]{1,0:T(8,128)(2,1)S(1)}, bf16[1032,128]{1,0:T(8,128)(2,1)S(1)}, u32[]{:S(2)}, u32[]{:S(2)}) collective-permute-start(bf16[1032,128]{1,0:T(8,128)(2,1)S(1)} %collective-permute-done.5.refs_2_), channel_id=1, source_target_pairs={{0,2},{7,5},{8,10},{15,13},{16,18},{23,21},{24,26},{31,29}} | collective-permute-start | bytes 792584 | tf_op jit(solution)/shard_map/ppermute | solution.py:258
  22.9 7.2 %collective-permute-start.7 = (bf16[1032,128]{1,0:T(8,128)(2,1)S(1)}, bf16[1032,128]{1,0:T(8,128)(2,1)S(1)}, u32[]{:S(2)}, u32[]{:S(2)}) collective-permute-start(bf16[1032,128]{1,0:T(8,128)(2,1)S(1)} %collective-permute-done.5.refs_2_), channel_id=1, source_target_pairs={{1,2},{6,5},{9,10},{14,13},{17,18},{22,21},{25,26},{30,29}} | collective-permute-start | bytes 792584 | tf_op jit(solution)/shard_map/ppermute | solution.py:258
  23.6 8.0 %collective-permute-start.8 = (bf16[1032,128]{1,0:T(8,128)(2,1)S(1)}, bf16[1032,128]{1,0:T(8,128)(2,1)S(1)}, u32[]{:S(2)}, u32[]{:S(2)}) collective-permute-start(bf16[1032,128]{1,0:T(8,128)(2,1)S(1)} %collective-permute-done.5.refs_2_), channel_id=1, source_target_pairs={{3,2},{4,5},{11,10},{12,13},{19,18},{20,21},{27,26},{28,29}} | collective-permute-start | bytes 792584 | tf_op jit(solution)/shard_map/ppermute | solution.py:258
  25.9 11.3 %collective-permute-start.10 = (bf16[1032,128]{1,0:T(8,128)(2,1)S(1)}, bf16[1032,128]{1,0:T(8,128)(2,1)S(1)}, u32[]{:S(2)}, u32[]{:S(2)}) collective-permute-start(bf16[1032,128]{1,0:T(8,128)(2,1)S(1)} %collective-permute-done.9.refs_4_), channel_id=1, source_target_pairs={{0,2},{7,5},{8,10},{15,13},{16,18},{23,21},{24,26},{31,29}} | collective-permute-start | bytes 792584 | tf_op jit(solution)/shard_map/ppermute | solution.py:258
  28.7 10.6 %collective-permute-start.11 = (bf16[1032,128]{1,0:T(8,128)(2,1)S(1)}, bf16[1032,128]{1,0:T(8,128)(2,1)S(1)}, u32[]{:S(2)}, u32[]{:S(2)}) collective-permute-start(bf16[1032,128]{1,0:T(8,128)(2,1)S(1)} %collective-permute-done.9.refs_4_), channel_id=1, source_target_pairs={{1,2},{6,5},{9,10},{14,13},{17,18},{22,21},{25,26},{30,29}} | collective-permute-start | bytes 792584 | tf_op jit(solution)/shard_map/ppermute | solution.py:258
  29.4 9.9 %collective-permute-start.12 = (bf16[1032,128]{1,0:T(8,128)(2,1)S(1)}, bf16[1032,128]{1,0:T(8,128)(2,1)S(1)}, u32[]{:S(2)}, u32[]{:S(2)}) collective-permute-start(bf16[1032,128]{1,0:T(8,128)(2,1)S(1)} %collective-permute-done.9.refs_4_), channel_id=1, source_target_pairs={{3,2},{4,5},{11,10},{12,13},{19,18},{20,21},{27,26},{28,29}} | collective-permute-start | bytes 792584 | tf_op jit(solution)/shard_map/ppermute | solution.py:258
  30.1 11.2 %collective-permute-start.14 = (bf16[1032,128]{1,0:T(8,128)(2,1)S(1)}, bf16[1032,128]{1,0:T(8,128)(2,1)S(1)}, u32[]{:S(2)}, u32[]{:S(2)}) collective-permute-start(bf16[1032,128]{1,0:T(8,128)(2,1)S(1)} %collective-permute-done.13.refs_6_), channel_id=1, source_target_pairs={{3,2},{4,5},{11,10},{12,13},{19,18},{20,21},{27,26},{28,29}} | collective-permute-start | bytes 792584 | tf_op jit(solution)/shard_map/ppermute | solution.py:258
  31.6 11.0 %collective-permute-start.15 = (bf16[1032,128]{1,0:T(8,128)(2,1)S(1)}, bf16[1032,128]{1,0:T(8,128)(2,1)S(1)}, u32[]{:S(2)}, u32[]{:S(2)}) collective-permute-start(bf16[1032,128]{1,0:T(8,128)(2,1)S(1)} %collective-permute-done.13.refs_6_), channel_id=1, source_target_pairs={{0,2},{7,5},{8,10},{15,13},{16,18},{23,21},{24,26},{31,29}} | collective-permute-start | bytes 792584 | tf_op jit(solution)/shard_map/ppermute | solution.py:258
  37.3 5.4 %collective-permute-start.16 = (bf16[1032,128]{1,0:T(8,128)(2,1)S(1)}, bf16[1032,128]{1,0:T(8,128)(2,1)S(1)}, u32[]{:S(2)}, u32[]{:S(2)}) collective-permute-start(bf16[1032,128]{1,0:T(8,128)(2,1)S(1)} %collective-permute-done.13.refs_6_), channel_id=1, source_target_pairs={{1,2},{6,5},{9,10},{14,13},{17,18},{22,21},{25,26},{30,29}} | collective-permute-start | bytes 792584 | tf_op jit(solution)/shard_map/ppermute | solution.py:258

commit v5 on v4

--- a/solution.py
+++ b/solution.py
@@ -90,16 +90,18 @@
         base += ref.shape[0]
 
 
-def unfold(refs, pieces, x_ref, column_ref, row_ref):
+def unfold(refs, pieces, x_ref, turned_ref, column_ref, row_ref):
     size = pieces * LANES + META
     base = 0
     for ref in refs:
         for b in range(ref.shape[0] // size):
             rows = slice(base, base + LANES)
             for k in range(pieces):
-                x_ref[rows, k * LANES : (k + 1) * LANES] = ref[
-                    b * size + k * LANES : b * size + (k + 1) * LANES, :
-                ]
+                lanes = slice(k * LANES, (k + 1) * LANES)
+                piece = ref[b * size + k * LANES : b * size + (k + 1) * LANES, :]
+                x_ref[rows, lanes] = piece
+                if turned_ref is not None:
+                    turned_ref[lanes, rows] = jnp.transpose(piece)
             meta = ref[b * size + pieces * LANES : (b + 1) * size, :].astype(F32)
             rank = meta[0:1, :] * 256.0 + meta[1:2, :]
             row_ref[:, rows] = rank
@@ -120,24 +122,27 @@
     return jnp.concatenate([column] * (width // LANES), axis=1)
 
 
-def tile_for(count):
-    return next(t for t in (512, 256, 128) if count % t == 0)
-
-
-def fold(keys_ref, rank_ref, best_ref, side_ref, query_ref, query_rank, symmetric):
-    tall, wide = tile_for(keys_ref.shape[0]), tile_for(query_ref.shape[0])
+def fold(keys_ref, rank_ref, best_ref, side_ref, query_ref, query_rank, turned):
+    queries = query_rank.shape[1]
+    tall = next(t for t in (512, 256, 128) if keys_ref.shape[0] % t == 0)
+    wide = next(t for t in (256, 128) if queries % t == 0)
 
     def outer(i, _):
-        mine = pl.ds(pl.multiple_of(i * wide, wide), wide)
+        mine = span(i, wide)
 
         def inner(j, _):
-            keys = pl.ds(pl.multiple_of(j * tall, tall), tall)
-            scores = nt(keys_ref[keys, :], query_ref[mine, :])
+            keys = span(j, tall)
+            if turned:
+                scores = jnp.dot(
+                    keys_ref[keys, :], query_ref[:, mine], preferred_element_type=F32
+                )
+            else:
+                scores = nt(keys_ref[keys, :], query_ref[mine, :])
             earlier = across(rank_ref[keys, :], wide) < query_rank[:, mine]
             best_ref[:, mine] = jnp.maximum(
                 best_ref[:, mine], wide_max(jnp.where(earlier, scores, -1.0))
             )
-            if symmetric:
+            if turned:
                 side_ref[keys, :] = jnp.maximum(
                     side_ref[keys, :], lane_max(jnp.where(earlier, -1.0, scores))
                 )
@@ -146,12 +151,19 @@
         loop(keys_ref.shape[0] // tall, inner)
         return 0
 
-    loop(query_ref.shape[0] // wide, outer)
+    loop(queries // wide, outer)
+
+
+def span(i, size):
+    if isinstance(i, int):
+        return slice(i * size, (i + 1) * size)
+    return pl.ds(pl.multiple_of(i * size, size), size)
 
 
 def loop(count, body):
-    if count == 1:
-        body(0, 0)
+    if count <= 4:
+        for i in range(count):
+            body(i, 0)
     else:
         lax.fori_loop(0, count, body, 0)
 
@@ -168,12 +180,12 @@
     found = take(sum(range(olds + 1))) if places else []
     if places:
         (out,) = take(1)
-        news, (x_ref, row_ref, best_ref) = take(olds), take(3)
+        news, turned_ref, (row_ref, best_ref) = take(olds), None, take(2)
     else:
-        x_ref, row_ref, best_ref = take(3)
+        turned_ref, row_ref, best_ref = take(3)
         news = take(olds)
-    column_ref, side_ref = take(2)
-    unfold(blocks, pieces, x_ref, column_ref, row_ref)
+    x_ref, column_ref, side_ref = take(3)
+    unfold(blocks, pieces, x_ref, turned_ref, column_ref, row_ref)
     best_ref[...] = jnp.full(best_ref.shape, -1.0, F32)
     side_ref[...] = jnp.full(side_ref.shape, -1.0, F32)
     for x, row, new in zip(xs, rows, news):
@@ -207,7 +219,7 @@
 def final_body(planes, pos_ref, table_ref, out_ref):
     groups = table_ref.shape[0] // planes
     pos = pos_ref[...]
-    rows = [g * planes + planes // 2 - (g & 1) for g in range(groups)]
+    rows = [g * planes + planes // 2 - 1 + (g & 1) for g in range(groups)]
     table = jnp.concatenate([table_ref[r : r + 1, :] for r in rows], axis=0)
     for i in range(0, pos.shape[1], LANES):
         here = jnp.broadcast_to(pos[:, i : i + LANES], (groups, LANES))
@@ -243,9 +255,9 @@
     def to_core(value):
         return lax.ppermute(value, "group", [(i, i ^ 1) for i in range(groups)])
 
-    meet = [half, half - 1]
+    meet = [half - 1, half]
     sources = [[z for z in range(planes) if z != half]]
-    sources.append([planes - 1 - z for z in sources[0]])
+    sources.insert(0, [planes - 1 - z for z in sources[0]])
 
     def meeting(step):
         return [
@@ -312,15 +324,16 @@
     xs, ranks, found = [], [], []
     for i, stage in enumerate(stages):
         n = sum(len(chunks[c]) for c, _ in stage) * LANES
-        flops = 2 * n * width * (n + sum(x.shape[0] for x in xs))
-        made = [((n, width), BF16), ((1, n), F32), ((8, n), F32)]
-        kept = [((8, x.shape[0]), F32) for x in xs]
-        spare = [pltpu.VMEM((n, LANES), F32)] * 2
+        count = n + sum(x.shape[1] for x in xs)
+        flops = 2 * n * width * count
+        made = [((width, n), BF16), ((1, n), F32), ((8, n), F32)]
+        kept = [((8, x.shape[1]), F32) for x in xs]
+        spare = [pltpu.VMEM((n, width), BF16)] + [pltpu.VMEM((n, LANES), F32)] * 2
         operands = xs + ranks + [arrived[c][p] for c, p in stage]
         if i == len(stages) - 1:
             operands += found
             outs = floats(groups * planes, LANES)
-            spare = [pltpu.VMEM(*m) for m in kept + made] + spare
+            spare = [pltpu.VMEM(*m) for m in kept + made[1:]] + spare
         else:
             outs = [jax.ShapeDtypeStruct(*m) for m in made + kept]
         best = call(
@@ -335,8 +348,8 @@
             outs,
             operands,
             flops,
-            2 * width * (n + sum(x.shape[0] for x in xs)),
-            6 * width * 2 * n + (12 << 20),
+            2 * width * count,
+            8 * width * 2 * n + (12 << 20),
             scratch=spare,
         )
         if i < len(stages) - 1:

time: 57.9 us -> 57.8 us (level)
  waiting for transfers between devices: 2.01 us -> 5.02 us
  starting transfers between devices: 32.2 us -> 29.5 us
    ppermute x12, waiting for transfers between devices: 0.33 us -> 2.65 us  [gather(): arrived.append(lax.ppermute(value, ('group', 'blk'), meeting(step)))]
    ppermute x3, starting transfers between devices: 6.55 us -> 5.09 us  [to_chip(): return lax.ppermute(value, 'group', [(i, i ^ 2 * s) for i in range(groups)])]
    ppermute x12, starting transfers between devices: 25.1 us -> 23.8 us  [gather(): arrived.append(lax.ppermute(value, ('group', 'blk'), meeting(step)))]
    ppermute x3, waiting for transfers between devices: 1.67 us -> 2.37 us  [to_chip(): return lax.ppermute(value, 'group', [(i, i ^ 2 * s) for i in range(groups)])]
  transfers between devices with their start and end apart: 17 -> 17, of which waited for: 2 -> 4; matrix products, arithmetic and copies ran while one was open for 0% -> 0% of each run, Pallas kernels for 10% -> 10%
where the time goes in v5:
time: 57.8 us; the launch traced here: 57.5 us
  starting transfers between devices  29.5 us (51%)
  blocking collectives  12.4 us (21%)
  Pallas kernels  8.61 us (15%)
  waiting for transfers between devices  5.02 us (9%)
  local copies, waits for them, and re-layouts  1.73 us (3%)
    ppermute x12, starting transfers between devices, gather(): arrived.append(lax.ppermute(value, ('group', 'blk'), meeting(step)))  23.8 us
    all_to_all x1, blocking collectives, on_device(): table = lax.all_to_all(best, ('group', 'blk'), 0, 0, tiled=True)  12.4 us
    pallas_call x8, Pallas kernels, call(): pl.pallas_call(body, out_shape=outs, in_specs=[spec] * len(operands), out...  8.61 us
    ppermute x3, starting transfers between devices, to_chip(): return lax.ppermute(value, 'group', [(i, i ^ 2 * s) for i in range(groups)])  5.09 us
    ppermute x12, waiting for transfers between devices, gather(): arrived.append(lax.ppermute(value, ('group', 'blk'), meeting(step)))  2.65 us
    ppermute x3, waiting for transfers between devices, to_chip(): return lax.ppermute(value, 'group', [(i, i ^ 2 * s) for i in range(groups)])  2.37 us
    unnamed x6, local copies, waits for them, and re-layouts  1.73 us
  transfers between devices with their start and end apart: 17, of which 4 were waited for; matrix products, arithmetic and copies ran while one was open for 0% of the time, Pallas kernels for 10%

profile of v5, /device:TPU:0, one launch (start us, length us, event | category | flops | bytes accessed | tf_op | source)
XLA Modules:
  0.0 57.5 jit_solution(3362710645283412959)
XLA Ops:
  0.0 0.5 collective-permute-start
  0.5 0.7 %copy-done.2 = s32[256,1]{0,1:T(1,128)S(1)} copy-done((s32[256,1]{0,1:T(1,128)S(1)}, s32[256,1]{0,1:T(1,128)}, u32[]{:S(2)}) %copy-start.2) | copy-done | bytes 1048
  1.2 0.1 collective-permute-start.1
  1.3 1.0 %copy-done = bf16[256,1024]{1,0:T(8,128)(2,1)S(1)} copy-done((bf16[256,1024]{1,0:T(8,128)(2,1)S(1)}, bf16[256,1024]{1,0:T(8,128)(2,1)}, u32[]{:S(2)}) %copy-start) | copy-done | bytes 524312
  2.3 0.5 shard_map.37
  2.8 0.5 shard_map.38
  3.4 0.7 %collective-permute-start.2 = (bf16[1032,128]{1,0:T(8,128)(2,1)S(1)}, bf16[1032,128]{1,0:T(8,128)(2,1)S(1)}, u32[]{:S(2)}, u32[]{:S(2)}) collective-permute-start(bf16[1032,128]{1,0:T(8,128)(2,1)S(1)} %get-tuple-element.33.refs_0_), channel_id=1, source_target_pairs={{3,1},{4,6},{11,9},{12,14},{19,17},{20,22},{27,25},{28,30}} | collective-permute-start | bytes 792584 | tf_op jit(solution)/shard_map/ppermute | solution.py:270
  4.1 3.0 %collective-permute-start.5 = (bf16[1032,128]{1,0:T(8,128)(2,1)S(1)}, bf16[1032,128]{1,0:T(8,128)(2,1)S(1)}, u32[]{:S(2)}, u32[]{:S(2)}) collective-permute-start(bf16[1032,128]{1,0:T(8,128)(2,1)S(1)} %get-tuple-element.36), channel_id=1, source_target_pairs={{0,8},{4,12},{8,0},{12,4},{16,24},{20,28},{24,16},{28,20},{1,9},{5... | collective-permute-start | bytes 792584 | tf_op jit(solution)/shard_map/ppermute | solution.py:253
  7.1 0.7 %collective-permute-start.3 = (bf16[1032,128]{1,0:T(8,128)(2,1)S(1)}, bf16[1032,128]{1,0:T(8,128)(2,1)S(1)}, u32[]{:S(2)}, u32[]{:S(2)}) collective-permute-start(bf16[1032,128]{1,0:T(8,128)(2,1)S(1)} %get-tuple-element.33.refs_0_), channel_id=1, source_target_pairs={{2,1},{5,6},{10,9},{13,14},{18,17},{21,22},{26,25},{29,30}} | collective-permute-start | bytes 792584 | tf_op jit(solution)/shard_map/ppermute | solution.py:270
  7.8 4.7 %collective-permute-start.4 = (bf16[1032,128]{1,0:T(8,128)(2,1)S(1)}, bf16[1032,128]{1,0:T(8,128)(2,1)S(1)}, u32[]{:S(2)}, u32[]{:S(2)}) collective-permute-start(bf16[1032,128]{1,0:T(8,128)(2,1)S(1)} %get-tuple-element.33.refs_0_), channel_id=1, source_target_pairs={{0,1},{7,6},{8,9},{15,14},{16,17},{23,22},{24,25},{31,30}} | collective-permute-start | bytes 792584 | tf_op jit(solution)/shard_map/ppermute | solution.py:270
  12.5 1.6 %collective-permute-start.9 = (bf16[1032,128]{1,0:T(8,128)(2,1)S(1)}, bf16[1032,128]{1,0:T(8,128)(2,1)S(1)}, u32[]{:S(2)}, u32[]{:S(2)}) collective-permute-start(bf16[1032,128]{1,0:T(8,128)(2,1)S(1)} %get-tuple-element.39), channel_id=1, source_target_pairs={{0,16},{4,20},{8,24},{12,28},{16,0},{20,4},{24,8},{28,12},{1,17},{... | collective-permute-start | bytes 792584 | tf_op jit(solution)/shard_map/ppermute | solution.py:253
  14.1 0.5 collective-permute-start.13
  14.6 0.7 %collective-permute-start.6 = (bf16[1032,128]{1,0:T(8,128)(2,1)S(1)}, bf16[1032,128]{1,0:T(8,128)(2,1)S(1)}, u32[]{:S(2)}, u32[]{:S(2)}) collective-permute-start(bf16[1032,128]{1,0:T(8,128)(2,1)S(1)} %collective-permute-done.5.refs_2_), channel_id=1, source_target_pairs={{3,1},{4,6},{11,9},{12,14},{19,17},{20,22},{27,25},{28,30}} | collective-permute-start | bytes 792584 | tf_op jit(solution)/shard_map/ppermute | solution.py:270
  15.3 0.7 %collective-permute-start.7 = (bf16[1032,128]{1,0:T(8,128)(2,1)S(1)}, bf16[1032,128]{1,0:T(8,128)(2,1)S(1)}, u32[]{:S(2)}, u32[]{:S(2)}) collective-permute-start(bf16[1032,128]{1,0:T(8,128)(2,1)S(1)} %collective-permute-done.5.refs_2_), channel_id=1, source_target_pairs={{2,1},{5,6},{10,9},{13,14},{18,17},{21,22},{26,25},{29,30}} | collective-permute-start | bytes 792584 | tf_op jit(solution)/shard_map/ppermute | solution.py:270
  16.0 0.4 collective-permute-done.4.refs_3_
  16.4 7.0 %collective-permute-start.8 = (bf16[1032,128]{1,0:T(8,128)(2,1)S(1)}, bf16[1032,128]{1,0:T(8,128)(2,1)S(1)}, u32[]{:S(2)}, u32[]{:S(2)}) collective-permute-start(bf16[1032,128]{1,0:T(8,128)(2,1)S(1)} %collective-permute-done.5.refs_2_), channel_id=1, source_target_pairs={{0,1},{7,6},{8,9},{15,14},{16,17},{23,22},{24,25},{31,30}} | collective-permute-start | bytes 792584 | tf_op jit(solution)/shard_map/ppermute | solution.py:270
  23.4 2.4 %collective-permute-done.9.refs_4_ = bf16[1032,128]{1,0:T(8,128)(2,1)S(1)} collective-permute-done((bf16[1032,128]{1,0:T(8,128)(2,1)S(1)}, bf16[1032,128]{1,0:T(8,128)(2,1)S(1)}, u32[]{:S(2)}, u32[]{:S(2)}) %collective-permute-start.9) | collective-permute-done | bytes 264224 | tf_op jit(solution)/shard_map/ppermute | solution.py:253
  25.7 0.7 %collective-permute-start.10 = (bf16[1032,128]{1,0:T(8,128)(2,1)S(1)}, bf16[1032,128]{1,0:T(8,128)(2,1)S(1)}, u32[]{:S(2)}, u32[]{:S(2)}) collective-permute-start(bf16[1032,128]{1,0:T(8,128)(2,1)S(1)} %collective-permute-done.9.refs_4_), channel_id=1, source_target_pairs={{3,1},{4,6},{11,9},{12,14},{19,17},{20,22},{27,25},{28,30}} | collective-permute-start | bytes 792584 | tf_op jit(solution)/shard_map/ppermute | solution.py:270
  26.4 0.7 %collective-permute-start.11 = (bf16[1032,128]{1,0:T(8,128)(2,1)S(1)}, bf16[1032,128]{1,0:T(8,128)(2,1)S(1)}, u32[]{:S(2)}, u32[]{:S(2)}) collective-permute-start(bf16[1032,128]{1,0:T(8,128)(2,1)S(1)} %collective-permute-done.9.refs_4_), channel_id=1, source_target_pairs={{2,1},{5,6},{10,9},{13,14},{18,17},{21,22},{26,25},{29,30}} | collective-permute-start | bytes 792584 | tf_op jit(solution)/shard_map/ppermute | solution.py:270
  27.1 5.4 %collective-permute-start.12 = (bf16[1032,128]{1,0:T(8,128)(2,1)S(1)}, bf16[1032,128]{1,0:T(8,128)(2,1)S(1)}, u32[]{:S(2)}, u32[]{:S(2)}) collective-permute-start(bf16[1032,128]{1,0:T(8,128)(2,1)S(1)} %collective-permute-done.9.refs_4_), channel_id=1, source_target_pairs={{0,1},{7,6},{8,9},{15,14},{16,17},{23,22},{24,25},{31,30}} | collective-permute-start | bytes 792584 | tf_op jit(solution)/shard_map/ppermute | solution.py:270
  32.6 1.3 %collective-permute-start.14 = (bf16[1032,128]{1,0:T(8,128)(2,1)S(1)}, bf16[1032,128]{1,0:T(8,128)(2,1)S(1)}, u32[]{:S(2)}, u32[]{:S(2)}) collective-permute-start(bf16[1032,128]{1,0:T(8,128)(2,1)S(1)} %collective-permute-done.13.refs_6_), channel_id=1, source_target_pairs={{0,1},{7,6},{8,9},{15,14},{16,17},{23,22},{24,25},{31,30}} | collective-permute-start | bytes 792584 | tf_op jit(solution)/shard_map/ppermute | solution.py:270
  33.9 0.9 %shard_map.39 = (bf16[1024,512]{1,0:T(8,128)(2,1)S(1)}, f32[1,512]{1,0:T(1,128)S(1)}, f32[8,512]{1,0:T(8,128)S(1)}) custom-call(bf16[1032,128]{1,0:T(8,128)(2,1)S(1)} %get-tuple-element.33.refs_0_, bf16[1032,128]{1,0:T(8,128)(2,1)S(1)} %collective-permute-done.2.refs_1_, bf16[1032,128]{1,0:T(8,128)(2,1)S(1)} %collective-permute-done.3.refs_2_, ...), custom_call_target="tpu_custom_call" | custom-call | flops 536870912 | bytes 1048576 | tf_op jit(solution)/shard_map/pallas_call | solution.py:23
  34.7 0.7 %collective-permute-start.15 = (bf16[1032,128]{1,0:T(8,128)(2,1)S(1)}, bf16[1032,128]{1,0:T(8,128)(2,1)S(1)}, u32[]{:S(2)}, u32[]{:S(2)}) collective-permute-start(bf16[1032,128]{1,0:T(8,128)(2,1)S(1)} %collective-permute-done.13.refs_6_), channel_id=1, source_target_pairs={{3,1},{4,6},{11,9},{12,14},{19,17},{20,22},{27,25},{28,30}} | collective-permute-start | bytes 792584 | tf_op jit(solution)/shard_map/ppermute | solution.py:270
  35.4 0.7 %collective-permute-start.16 = (bf16[1032,128]{1,0:T(8,128)(2,1)S(1)}, bf16[1032,128]{1,0:T(8,128)(2,1)S(1)}, u32[]{:S(2)}, u32[]{:S(2)}) collective-permute-start(bf16[1032,128]{1,0:T(8,128)(2,1)S(1)} %collective-permute-done.13.refs_6_), channel_id=1, source_target_pairs={{2,1},{5,6},{10,9},{13,14},{18,17},{21,22},{26,25},{29,30}} | collective-permute-start | bytes 792584 | tf_op jit(solution)/shard_map/ppermute | solution.py:270
  36.1 1.4 %shard_map.40 = (bf16[1024,512]{1,0:T(8,128)(2,1)S(1)}, f32[1,512]{1,0:T(1,128)S(1)}, f32[8,512]{1,0:T(8,128)S(1)}, f32[8,512]{1,0:T(8,128)S(1)}) custom-call(bf16[1024,512]{1,0:T(8,128)(2,1)S(1)} %get-tuple-element.34.refs_0_, f32[1,512]{1,0:T(1,128)S(1)} %get-tuple-element.35.refs_1_.refs_2_.refs_3_.refs_4_, ...), custom_call_target="tpu_custom_call" | custom-call | flops 1073741824 | bytes 2097152 | tf_op jit(solution)/shard_map/pallas_call | solution.py:23
  37.5 1.3 %collective-permute-done.12.refs_7_ = bf16[1032,128]{1,0:T(8,128)(2,1)S(1)} collective-permute-done((bf16[1032,128]{1,0:T(8,128)(2,1)S(1)}, bf16[1032,128]{1,0:T(8,128)(2,1)S(1)}, u32[]{:S(2)}, u32[]{:S(2)}) %collective-permute-start.12) | collective-permute-done | bytes 264224 | tf_op jit(solution)/shard_map/ppermute | solution.py:270
  38.8 1.9 %shard_map.41 = (bf16[1024,512]{1,0:T(8,128)(2,1)S(1)}, f32[1,512]{1,0:T(1,128)S(1)}, f32[8,512]{1,0:T(8,128)S(1)}, f32[8,512]{1,0:T(8,128)S(1)}, f32[8,512]{1,0:T(8,128)S(1)}) custom-call(bf16[1024,512]{1,0:T(8,128)(2,1)S(1)} %get-tuple-element.34.refs_0_, bf16[1024,512]{1,0:T(8,128)(2,1)S(1)} %get-tuple-element.37.refs_1_, ...), custom_call_target="tpu_custom_call" | custom-call | flops 1610612736 | bytes 3145728 | tf_op jit(solution)/shard_map/pallas_call | solution.py:23
  40.7 0.9 %collective-permute-done.14.refs_7_ = bf16[1032,128]{1,0:T(8,128)(2,1)S(1)} collective-permute-done((bf16[1032,128]{1,0:T(8,128)(2,1)S(1)}, bf16[1032,128]{1,0:T(8,128)(2,1)S(1)}, u32[]{:S(2)}, u32[]{:S(2)}) %collective-permute-start.14) | collective-permute-done | bytes 264224 | tf_op jit(solution)/shard_map/ppermute | solution.py:270
  41.6 1.3 %shard_map.42 = (bf16[1024,256]{1,0:T(8,128)(2,1)S(1)}, f32[1,256]{1,0:T(1,128)S(1)}, f32[8,256]{1,0:T(8,128)S(1)}, f32[8,512]{1,0:T(8,128)S(1)}, f32[8,512]{1,0:T(8,128)S(1)}, /*index=5*/f32[8,512]{1,0:T(8,128)S(1)}) custom-call(bf16[1024,512]{1,0:T(8,128)(2,1)S(1)} %get-tuple-element.34.refs_0_, bf16[1024,512]{1,0:T(8,128)(2,1)S(1)} %get-tuple-element.37.refs_1_, ...), custom_call_target="tpu_custom_call" | custom-call | flops 939524096 | bytes 3670016 | tf_op jit(solution)/shard_map/pallas_call | solution.py:23
  43.0 1.5 %shard_map.43 = f32[32,128]{1,0:T(8,128)S(1)} custom-call(bf16[1024,512]{1,0:T(8,128)(2,1)S(1)} %get-tuple-element.34.refs_0_, bf16[1024,512]{1,0:T(8,128)(2,1)S(1)} %get-tuple-element.37.refs_1_, bf16[1024,512]{1,0:T(8,128)(2,1)S(1)} %get-tuple-element.40.refs_2_, bf16[1024,256]{1,0:T(8,128)(2,1)S(1)} %get-tuple-element.43.refs_3_, ...), custom_call_target="tpu_custom_call" | custom-call | flops 1073741824 | bytes 4194304 | tf_op jit(solution)/shard_map/pallas_call | solution.py:23
  44.4 12.4 %all_to_all.11 = f32[32,1,128]{2,1,0:T(1,128)S(1)} all-to-all(f32[32,1,128]{2,1,0:T(1,128)S(1)} %bitcast.7), channel_id=1, replica_groups=mesh['group'=8,'blk'=4] {'group','blk'}, dimensions={0} | all-to-all | bytes 32768 | tf_op jit(solution)/shard_map/all_to_all | solution.py:359
  56.8 0.7 %shard_map.44 = f32[1,256]{1,0:T(1,128)} custom-call(s32[1,256]{1,0:T(1,128)S(1)} %get-tuple-element.30.pos_ref, f32[32,128]{1,0:T(8,128)S(1)} %bitcast.8), custom_call_target="tpu_custom_call" | custom-call | flops 1000000 | bytes 100000 | tf_op jit(solution)/shard_map/pallas_call | solution.py:23
  (18 shorter events, 0.1 us)
Async XLA Ops:
  0.0 2.8 %collective-permute-start = (bf16[256,1024]{1,0:T(8,128)(2,1)}, bf16[256,1024]{1,0:T(8,128)(2,1)S(1)}, u32[]{:S(2)}, u32[]{:S(2)}) collective-permute-start(bf16[256,1024]{1,0:T(8,128)(2,1)} %emb_ref.1), channel_id=1, source_target_pairs={{0,4},{4,0},{8,12},{12,8},{16,20},{20,16},{24,28},{28,24},{1,5},{5... | collective-permute-start | bytes 1572872 | tf_op jit(solution)/shard_map/ppermute | solution.py:256
  0.5 0.7 %copy-start.2 = (s32[256,1]{0,1:T(1,128)S(1)}, s32[256,1]{0,1:T(1,128)}, u32[]{:S(2)}) copy-start(s32[256,1]{0,1:T(1,128)} %param.4) | copy-start | bytes 3076
  0.5 0.7 %copy-start.1 = (s32[256]{0:T(256)S(1)}, s32[256]{0:T(256)}, u32[]{:S(2)}) copy-start(s32[256]{0:T(256)} %param.5) | copy-start | bytes 3076
  1.2 1.6 %collective-permute-start.1 = (s32[2,256]{1,0:T(2,128)S(1)}, s32[2,256]{1,0:T(2,128)S(1)}, u32[]{:S(2)}, u32[]{:S(2)}) collective-permute-start(s32[2,256]{1,0:T(2,128)S(1)} %pad_add_fusion.code_ref), channel_id=1, source_target_pairs={{0,4},{4,0},{8,12},{12,8},{16,20},{20,16},{24,28},{28,24},{1,5},{5... | collective-permute-start | bytes 6152 | tf_op jit(solution)/shard_map/ppermute | solution.py:256
  1.3 1.0 %copy-start = (bf16[256,1024]{1,0:T(8,128)(2,1)S(1)}, bf16[256,1024]{1,0:T(8,128)(2,1)}, u32[]{:S(2)}) copy-start(bf16[256,1024]{1,0:T(8,128)(2,1)} %emb_ref.1) | copy-start | bytes 1572868
  3.4 10.7 %collective-permute-start.2 = (bf16[1032,128]{1,0:T(8,128)(2,1)S(1)}, bf16[1032,128]{1,0:T(8,128)(2,1)S(1)}, u32[]{:S(2)}, u32[]{:S(2)}) collective-permute-start(bf16[1032,128]{1,0:T(8,128)(2,1)S(1)} %get-tuple-element.33.refs_0_), channel_id=1, source_target_pairs={{3,1},{4,6},{11,9},{12,14},{19,17},{20,22},{27,25},{28,30}} | collective-permute-start | bytes 792584 | tf_op jit(solution)/shard_map/ppermute | solution.py:270
  4.1 10.5 %collective-permute-start.5 = (bf16[1032,128]{1,0:T(8,128)(2,1)S(1)}, bf16[1032,128]{1,0:T(8,128)(2,1)S(1)}, u32[]{:S(2)}, u32[]{:S(2)}) collective-permute-start(bf16[1032,128]{1,0:T(8,128)(2,1)S(1)} %get-tuple-element.36), channel_id=1, source_target_pairs={{0,8},{4,12},{8,0},{12,4},{16,24},{20,28},{24,16},{28,20},{1,9},{5... | collective-permute-start | bytes 792584 | tf_op jit(solution)/shard_map/ppermute | solution.py:253
  7.1 8.2 %collective-permute-start.3 = (bf16[1032,128]{1,0:T(8,128)(2,1)S(1)}, bf16[1032,128]{1,0:T(8,128)(2,1)S(1)}, u32[]{:S(2)}, u32[]{:S(2)}) collective-permute-start(bf16[1032,128]{1,0:T(8,128)(2,1)S(1)} %get-tuple-element.33.refs_0_), channel_id=1, source_target_pairs={{2,1},{5,6},{10,9},{13,14},{18,17},{21,22},{26,25},{29,30}} | collective-permute-start | bytes 792584 | tf_op jit(solution)/shard_map/ppermute | solution.py:270
  7.8 8.6 %collective-permute-start.4 = (bf16[1032,128]{1,0:T(8,128)(2,1)S(1)}, bf16[1032,128]{1,0:T(8,128)(2,1)S(1)}, u32[]{:S(2)}, u32[]{:S(2)}) collective-permute-start(bf16[1032,128]{1,0:T(8,128)(2,1)S(1)} %get-tuple-element.33.refs_0_), channel_id=1, source_target_pairs={{0,1},{7,6},{8,9},{15,14},{16,17},{23,22},{24,25},{31,30}} | collective-permute-start | bytes 792584 | tf_op jit(solution)/shard_map/ppermute | solution.py:270
  12.5 13.2 %collective-permute-start.9 = (bf16[1032,128]{1,0:T(8,128)(2,1)S(1)}, bf16[1032,128]{1,0:T(8,128)(2,1)S(1)}, u32[]{:S(2)}, u32[]{:S(2)}) collective-permute-start(bf16[1032,128]{1,0:T(8,128)(2,1)S(1)} %get-tuple-element.39), channel_id=1, source_target_pairs={{0,16},{4,20},{8,24},{12,28},{16,0},{20,4},{24,8},{28,12},{1,17},{... | collective-permute-start | bytes 792584 | tf_op jit(solution)/shard_map/ppermute | solution.py:253
  14.1 12.3 %collective-permute-start.13 = (bf16[1032,128]{1,0:T(8,128)(2,1)S(1)}, bf16[1032,128]{1,0:T(8,128)(2,1)S(1)}, u32[]{:S(2)}, u32[]{:S(2)}) collective-permute-start(bf16[1032,128]{1,0:T(8,128)(2,1)S(1)} %get-tuple-element.42), channel_id=1, source_target_pairs={{0,24},{4,28},{8,16},{12,20},{16,8},{20,12},{24,0},{28,4},{1,25},{... | collective-permute-start | bytes 792584 | tf_op jit(solution)/shard_map/ppermute | solution.py:253
  14.6 12.5 %collective-permute-start.6 = (bf16[1032,128]{1,0:T(8,128)(2,1)S(1)}, bf16[1032,128]{1,0:T(8,128)(2,1)S(1)}, u32[]{:S(2)}, u32[]{:S(2)}) collective-permute-start(bf16[1032,128]{1,0:T(8,128)(2,1)S(1)} %collective-permute-done.5.refs_2_), channel_id=1, source_target_pairs={{3,1},{4,6},{11,9},{12,14},{19,17},{20,22},{27,25},{28,30}} | collective-permute-start | bytes 792584 | tf_op jit(solution)/shard_map/ppermute | solution.py:270
  15.3 17.3 %collective-permute-start.7 = (bf16[1032,128]{1,0:T(8,128)(2,1)S(1)}, bf16[1032,128]{1,0:T(8,128)(2,1)S(1)}, u32[]{:S(2)}, u32[]{:S(2)}) collective-permute-start(bf16[1032,128]{1,0:T(8,128)(2,1)S(1)} %collective-permute-done.5.refs_2_), channel_id=1, source_target_pairs={{2,1},{5,6},{10,9},{13,14},{18,17},{21,22},{26,25},{29,30}} | collective-permute-start | bytes 792584 | tf_op jit(solution)/shard_map/ppermute | solution.py:270
  16.4 18.3 %collective-permute-start.8 = (bf16[1032,128]{1,0:T(8,128)(2,1)S(1)}, bf16[1032,128]{1,0:T(8,128)(2,1)S(1)}, u32[]{:S(2)}, u32[]{:S(2)}) collective-permute-start(bf16[1032,128]{1,0:T(8,128)(2,1)S(1)} %collective-permute-done.5.refs_2_), channel_id=1, source_target_pairs={{0,1},{7,6},{8,9},{15,14},{16,17},{23,22},{24,25},{31,30}} | collective-permute-start | bytes 792584 | tf_op jit(solution)/shard_map/ppermute | solution.py:270
  25.7 9.7 %collective-permute-start.10 = (bf16[1032,128]{1,0:T(8,128)(2,1)S(1)}, bf16[1032,128]{1,0:T(8,128)(2,1)S(1)}, u32[]{:S(2)}, u32[]{:S(2)}) collective-permute-start(bf16[1032,128]{1,0:T(8,128)(2,1)S(1)} %collective-permute-done.9.refs_4_), channel_id=1, source_target_pairs={{3,1},{4,6},{11,9},{12,14},{19,17},{20,22},{27,25},{28,30}} | collective-permute-start | bytes 792584 | tf_op jit(solution)/shard_map/ppermute | solution.py:270
  26.4 11.1 %collective-permute-start.11 = (bf16[1032,128]{1,0:T(8,128)(2,1)S(1)}, bf16[1032,128]{1,0:T(8,128)(2,1)S(1)}, u32[]{:S(2)}, u32[]{:S(2)}) collective-permute-start(bf16[1032,128]{1,0:T(8,128)(2,1)S(1)} %collective-permute-done.9.refs_4_), channel_id=1, source_target_pairs={{2,1},{5,6},{10,9},{13,14},{18,17},{21,22},{26,25},{29,30}} | collective-permute-start | bytes 792584 | tf_op jit(solution)/shard_map/ppermute | solution.py:270
  27.1 11.7 %collective-permute-start.12 = (bf16[1032,128]{1,0:T(8,128)(2,1)S(1)}, bf16[1032,128]{1,0:T(8,128)(2,1)S(1)}, u32[]{:S(2)}, u32[]{:S(2)}) collective-permute-start(bf16[1032,128]{1,0:T(8,128)(2,1)S(1)} %collective-permute-done.9.refs_4_), channel_id=1, source_target_pairs={{0,1},{7,6},{8,9},{15,14},{16,17},{23,22},{24,25},{31,30}} | collective-permute-start | bytes 792584 | tf_op jit(solution)/shard_map/ppermute | solution.py:270
  32.6 9.1 %collective-permute-start.14 = (bf16[1032,128]{1,0:T(8,128)(2,1)S(1)}, bf16[1032,128]{1,0:T(8,128)(2,1)S(1)}, u32[]{:S(2)}, u32[]{:S(2)}) collective-permute-start(bf16[1032,128]{1,0:T(8,128)(2,1)S(1)} %collective-permute-done.13.refs_6_), channel_id=1, source_target_pairs={{0,1},{7,6},{8,9},{15,14},{16,17},{23,22},{24,25},{31,30}} | collective-permute-start | bytes 792584 | tf_op jit(solution)/shard_map/ppermute | solution.py:270
  34.7 8.2 %collective-permute-start.15 = (bf16[1032,128]{1,0:T(8,128)(2,1)S(1)}, bf16[1032,128]{1,0:T(8,128)(2,1)S(1)}, u32[]{:S(2)}, u32[]{:S(2)}) collective-permute-start(bf16[1032,128]{1,0:T(8,128)(2,1)S(1)} %collective-permute-done.13.refs_6_), channel_id=1, source_target_pairs={{3,1},{4,6},{11,9},{12,14},{19,17},{20,22},{27,25},{28,30}} | collective-permute-start | bytes 792584 | tf_op jit(solution)/shard_map/ppermute | solution.py:270
  35.4 7.5 %collective-permute-start.16 = (bf16[1032,128]{1,0:T(8,128)(2,1)S(1)}, bf16[1032,128]{1,0:T(8,128)(2,1)S(1)}, u32[]{:S(2)}, u32[]{:S(2)}) collective-permute-start(bf16[1032,128]{1,0:T(8,128)(2,1)S(1)} %collective-permute-done.13.refs_6_), channel_id=1, source_target_pairs={{2,1},{5,6},{10,9},{13,14},{18,17},{21,22},{26,25},{29,30}} | collective-permute-start | bytes 792584 | tf_op jit(solution)/shard_map/ppermute | solution.py:270

commit v6 on v5

--- a/solution.py
+++ b/solution.py
@@ -31,12 +31,15 @@
     )(*operands)
 
 
-def gathered(emb_ref, code_ref, chip, core, chips, cap):
-    rows = emb_ref.shape[0]
-    clusters = max(16, 2 * chips)
+def unit_of(emb_ref):
     values = emb_ref[...].astype(F32)
     norm = lax.rsqrt(jnp.sum(values * values, axis=1, keepdims=True) + 1e-06)
-    unit = (values * norm).astype(BF16)
+    return (values * norm).astype(BF16)
+
+
+def picked(code_ref, chip, core, chips, cap):
+    rows = code_ref.shape[1]
+    clusters = max(16, 2 * chips)
     dest, rank = code_ref[0:1, :], code_ref[1:2, :]
     onehot = (lax.broadcasted_iota(jnp.int32, (clusters, rows), 0) == dest).astype(F32)
     row = lax.broadcasted_iota(jnp.int32, (rows, rows), 0)
@@ -55,23 +58,29 @@
     digits = nt(digits.astype(F32).astype(BF16), pick)
     top = lax.broadcasted_iota(jnp.int32, digits.shape, 0) == 0
     digits = jnp.where(top & (digits[2:3, :] < 0.5), 256.0, digits)
-    packed = jnp.dot(pick, unit, preferred_element_type=F32).astype(BF16)
-    return packed, digits, where, dest
-
-
-def own_body(cap, chips, emb_ref, code_ref, packed_ref, digits_ref, pos_ref):
+    return pick, digits, where, dest
+
+
+def index_body(cap, chips, code_ref, pick_ref, digits_ref, pos_ref):
     group = lax.axis_index("group")
-    packed, digits, where, dest = gathered(emb_ref, code_ref, group >> 1, group & 1, chips, cap)
-    packed_ref[...] = packed
+    pick, digits, where, dest = picked(code_ref, group >> 1, group & 1, chips, cap)
+    pick_ref[...] = pick
     digits_ref[...] = digits
     parity = dest & 1
     pos_ref[...] = dest * LANES + where % cap + cap * (parity ^ (group & 1))
 
 
+def own_body(pick_ref, emb_ref, packed_ref):
+    packed_ref[...] = jnp.dot(
+        pick_ref[...], unit_of(emb_ref), preferred_element_type=F32
+    ).astype(BF16)
+
+
 def pack_body(cap, chips, emb_ref, code_ref, own, own_digits, *refs):
     group = lax.axis_index("group")
     pieces = emb_ref.shape[1] // LANES
-    mate, mate_digits, _, _ = gathered(emb_ref, code_ref, group >> 1, group & 1, chips, cap)
+    pick, mate_digits, _, _ = picked(code_ref, group >> 1, group & 1, chips, cap)
+    mate = jnp.dot(pick, unit_of(emb_ref), preferred_element_type=F32).astype(BF16)
     for s in range(chips):
         part = slice(s * cap, (s + 1) * cap)
         for k in range(pieces):
@@ -274,14 +283,22 @@
     mate = to_core(embeddings)
     mate_code = to_core(code)
     flops = 2 * chips * cap * rows * width
-    own = call(
-        functools.partial(own_body, cap, chips),
+    pick, own_digits, pos = call(
+        functools.partial(index_body, cap, chips),
         [
-            jax.ShapeDtypeStruct((chips * cap, width), BF16),
+            jax.ShapeDtypeStruct((chips * cap, rows), BF16),
             floats(2 * META, chips * cap),
             jax.ShapeDtypeStruct((1, rows), jnp.int32),
         ],
-        [embeddings, code],
+        [code],
+        8 * flops,
+        4 * rows * width,
+        8 << 20,
+    )
+    own = call(
+        own_body,
+        jax.ShapeDtypeStruct((chips * cap, width), BF16),
+        [pick, embeddings],
         flops,
         4 * rows * width,
         16 << 20,
@@ -289,12 +306,11 @@
     packed = call(
         functools.partial(pack_body, cap, chips),
         [blocks(1)] * chips,
-        [mate, mate_code, own[0], own[1]],
+        [mate, mate_code, own, own_digits],
         flops,
         8 * rows * width,
         16 << 20,
     )
-    pos = own[2]
     sent = [packed[0]]
     for s in range(1, chips):
         sent.append(to_chip(packed[s], s))

time: 57.8 us -> 56.8 us (0.983)
  starting transfers between devices: 29.5 us -> 27 us
  waiting for transfers between devices: 5.02 us -> 6.46 us
    ppermute x12, starting transfers between devices: 23.8 us -> 21.8 us  [gather(): arrived.append(lax.ppermute(value, ('group', 'blk'), meeting(step)))]
    ppermute x3, waiting for transfers between devices: 2.37 us -> 3.32 us  [to_chip(): return lax.ppermute(value, 'group', [(i, i ^ 2 * s) for i in range(groups)])]
    pallas_call x8 -> x9, Pallas kernels: 8.61 us -> 8.88 us  [call(): pl.pallas_call(body, out_shape=outs, in_specs=[spec] * len(operands), out...]
  transfers between devices with their start and end apart: 17 -> 17, of which waited for: 4 -> 4; matrix products, arithmetic and copies ran while one was open for 0% -> 0% of each run, Pallas kernels for 10% -> 11%
where the time goes in v6:
time: 56.8 us; the launch traced here: 56.4 us
  starting transfers between devices  27 us (48%)
  blocking collectives  12.6 us (22%)
  Pallas kernels  8.88 us (16%)
  waiting for transfers between devices  6.46 us (11%)
  local copies, waits for them, and re-layouts  1.31 us (2%)
    ppermute x12, starting transfers between devices, gather(): arrived.append(lax.ppermute(value, ('group', 'blk'), meeting(step)))  21.8 us
    all_to_all x1, blocking collectives, on_device(): table = lax.all_to_all(best, ('group', 'blk'), 0, 0, tiled=True)  12.6 us
    pallas_call x9, Pallas kernels, call(): pl.pallas_call(body, out_shape=outs, in_specs=[spec] * len(operands), out...  8.88 us
    ppermute x3, starting transfers between devices, to_chip(): return lax.ppermute(value, 'group', [(i, i ^ 2 * s) for i in range(groups)])  4.61 us
    ppermute x3, waiting for transfers between devices, to_chip(): return lax.ppermute(value, 'group', [(i, i ^ 2 * s) for i in range(groups)])  3.32 us
    ppermute x12, waiting for transfers between devices, gather(): arrived.append(lax.ppermute(value, ('group', 'blk'), meeting(step)))  3.13 us
    unnamed x6, local copies, waits for them, and re-layouts  1.31 us
  transfers between devices with their start and end apart: 17, of which 4 were waited for; matrix products, arithmetic and copies ran while one was open for 0% of the time, Pallas kernels for 11%

profile of v6, /device:TPU:0, one launch (start us, length us, event | category | flops | bytes accessed | tf_op | source)
XLA Modules:
  0.0 56.4 jit_solution(2629003981063306831)
XLA Ops:
  0.0 0.5 collective-permute-start
  0.5 0.7 %copy-done.2 = s32[256,1]{0,1:T(1,128)S(1)} copy-done((s32[256,1]{0,1:T(1,128)S(1)}, s32[256,1]{0,1:T(1,128)}, u32[]{:S(2)}) %copy-start.2) | copy-done | bytes 1048
  1.3 0.3 shard_map.37
  1.6 0.6 %copy-done = bf16[256,1024]{1,0:T(8,128)(2,1)S(1)} copy-done((bf16[256,1024]{1,0:T(8,128)(2,1)S(1)}, bf16[256,1024]{1,0:T(8,128)(2,1)}, u32[]{:S(2)}) %copy-start) | copy-done | bytes 524312
  2.2 0.5 shard_map.38.own
  2.7 0.5 shard_map.39
  3.3 0.7 %collective-permute-start.2 = (bf16[1032,128]{1,0:T(8,128)(2,1)S(1)}, bf16[1032,128]{1,0:T(8,128)(2,1)S(1)}, u32[]{:S(2)}, u32[]{:S(2)}) collective-permute-start(bf16[1032,128]{1,0:T(8,128)(2,1)S(1)} %get-tuple-element.33.refs_0_), channel_id=1, source_target_pairs={{3,1},{4,6},{11,9},{12,14},{19,17},{20,22},{27,25},{28,30}} | collective-permute-start | bytes 792584 | tf_op jit(solution)/shard_map/ppermute | solution.py:279
  3.9 2.5 %collective-permute-start.5 = (bf16[1032,128]{1,0:T(8,128)(2,1)S(1)}, bf16[1032,128]{1,0:T(8,128)(2,1)S(1)}, u32[]{:S(2)}, u32[]{:S(2)}) collective-permute-start(bf16[1032,128]{1,0:T(8,128)(2,1)S(1)} %get-tuple-element.36), channel_id=1, source_target_pairs={{0,8},{4,12},{8,0},{12,4},{16,24},{20,28},{24,16},{28,20},{1,9},{5... | collective-permute-start | bytes 792584 | tf_op jit(solution)/shard_map/ppermute | solution.py:262
  6.5 0.7 %collective-permute-start.3 = (bf16[1032,128]{1,0:T(8,128)(2,1)S(1)}, bf16[1032,128]{1,0:T(8,128)(2,1)S(1)}, u32[]{:S(2)}, u32[]{:S(2)}) collective-permute-start(bf16[1032,128]{1,0:T(8,128)(2,1)S(1)} %get-tuple-element.33.refs_0_), channel_id=1, source_target_pairs={{2,1},{5,6},{10,9},{13,14},{18,17},{21,22},{26,25},{29,30}} | collective-permute-start | bytes 792584 | tf_op jit(solution)/shard_map/ppermute | solution.py:279
  7.2 4.7 %collective-permute-start.4 = (bf16[1032,128]{1,0:T(8,128)(2,1)S(1)}, bf16[1032,128]{1,0:T(8,128)(2,1)S(1)}, u32[]{:S(2)}, u32[]{:S(2)}) collective-permute-start(bf16[1032,128]{1,0:T(8,128)(2,1)S(1)} %get-tuple-element.33.refs_0_), channel_id=1, source_target_pairs={{0,1},{7,6},{8,9},{15,14},{16,17},{23,22},{24,25},{31,30}} | collective-permute-start | bytes 792584 | tf_op jit(solution)/shard_map/ppermute | solution.py:279
  11.9 1.6 %collective-permute-start.9 = (bf16[1032,128]{1,0:T(8,128)(2,1)S(1)}, bf16[1032,128]{1,0:T(8,128)(2,1)S(1)}, u32[]{:S(2)}, u32[]{:S(2)}) collective-permute-start(bf16[1032,128]{1,0:T(8,128)(2,1)S(1)} %get-tuple-element.39), channel_id=1, source_target_pairs={{0,16},{4,20},{8,24},{12,28},{16,0},{20,4},{24,8},{28,12},{1,17},{... | collective-permute-start | bytes 792584 | tf_op jit(solution)/shard_map/ppermute | solution.py:262
  13.5 0.5 collective-permute-start.13
  14.0 0.7 %collective-permute-start.6 = (bf16[1032,128]{1,0:T(8,128)(2,1)S(1)}, bf16[1032,128]{1,0:T(8,128)(2,1)S(1)}, u32[]{:S(2)}, u32[]{:S(2)}) collective-permute-start(bf16[1032,128]{1,0:T(8,128)(2,1)S(1)} %collective-permute-done.5.refs_2_), channel_id=1, source_target_pairs={{3,1},{4,6},{11,9},{12,14},{19,17},{20,22},{27,25},{28,30}} | collective-permute-start | bytes 792584 | tf_op jit(solution)/shard_map/ppermute | solution.py:279
  14.7 0.7 %collective-permute-start.7 = (bf16[1032,128]{1,0:T(8,128)(2,1)S(1)}, bf16[1032,128]{1,0:T(8,128)(2,1)S(1)}, u32[]{:S(2)}, u32[]{:S(2)}) collective-permute-start(bf16[1032,128]{1,0:T(8,128)(2,1)S(1)} %collective-permute-done.5.refs_2_), channel_id=1, source_target_pairs={{2,1},{5,6},{10,9},{13,14},{18,17},{21,22},{26,25},{29,30}} | collective-permute-start | bytes 792584 | tf_op jit(solution)/shard_map/ppermute | solution.py:279
  15.3 0.4 collective-permute-done.4.refs_3_
  15.8 6.5 %collective-permute-start.8 = (bf16[1032,128]{1,0:T(8,128)(2,1)S(1)}, bf16[1032,128]{1,0:T(8,128)(2,1)S(1)}, u32[]{:S(2)}, u32[]{:S(2)}) collective-permute-start(bf16[1032,128]{1,0:T(8,128)(2,1)S(1)} %collective-permute-done.5.refs_2_), channel_id=1, source_target_pairs={{0,1},{7,6},{8,9},{15,14},{16,17},{23,22},{24,25},{31,30}} | collective-permute-start | bytes 792584 | tf_op jit(solution)/shard_map/ppermute | solution.py:279
  22.3 3.3 %collective-permute-done.9.refs_4_ = bf16[1032,128]{1,0:T(8,128)(2,1)S(1)} collective-permute-done((bf16[1032,128]{1,0:T(8,128)(2,1)S(1)}, bf16[1032,128]{1,0:T(8,128)(2,1)S(1)}, u32[]{:S(2)}, u32[]{:S(2)}) %collective-permute-start.9) | collective-permute-done | bytes 264224 | tf_op jit(solution)/shard_map/ppermute | solution.py:262
  25.6 0.7 %collective-permute-start.10 = (bf16[1032,128]{1,0:T(8,128)(2,1)S(1)}, bf16[1032,128]{1,0:T(8,128)(2,1)S(1)}, u32[]{:S(2)}, u32[]{:S(2)}) collective-permute-start(bf16[1032,128]{1,0:T(8,128)(2,1)S(1)} %collective-permute-done.9.refs_4_), channel_id=1, source_target_pairs={{3,1},{4,6},{11,9},{12,14},{19,17},{20,22},{27,25},{28,30}} | collective-permute-start | bytes 792584 | tf_op jit(solution)/shard_map/ppermute | solution.py:279
  26.3 0.7 %collective-permute-start.11 = (bf16[1032,128]{1,0:T(8,128)(2,1)S(1)}, bf16[1032,128]{1,0:T(8,128)(2,1)S(1)}, u32[]{:S(2)}, u32[]{:S(2)}) collective-permute-start(bf16[1032,128]{1,0:T(8,128)(2,1)S(1)} %collective-permute-done.9.refs_4_), channel_id=1, source_target_pairs={{2,1},{5,6},{10,9},{13,14},{18,17},{21,22},{26,25},{29,30}} | collective-permute-start | bytes 792584 | tf_op jit(solution)/shard_map/ppermute | solution.py:279
  27.0 3.8 %collective-permute-start.12 = (bf16[1032,128]{1,0:T(8,128)(2,1)S(1)}, bf16[1032,128]{1,0:T(8,128)(2,1)S(1)}, u32[]{:S(2)}, u32[]{:S(2)}) collective-permute-start(bf16[1032,128]{1,0:T(8,128)(2,1)S(1)} %collective-permute-done.9.refs_4_), channel_id=1, source_target_pairs={{0,1},{7,6},{8,9},{15,14},{16,17},{23,22},{24,25},{31,30}} | collective-permute-start | bytes 792584 | tf_op jit(solution)/shard_map/ppermute | solution.py:279
  30.9 1.3 %collective-permute-start.14 = (bf16[1032,128]{1,0:T(8,128)(2,1)S(1)}, bf16[1032,128]{1,0:T(8,128)(2,1)S(1)}, u32[]{:S(2)}, u32[]{:S(2)}) collective-permute-start(bf16[1032,128]{1,0:T(8,128)(2,1)S(1)} %collective-permute-done.13.refs_6_), channel_id=1, source_target_pairs={{0,1},{7,6},{8,9},{15,14},{16,17},{23,22},{24,25},{31,30}} | collective-permute-start | bytes 792584 | tf_op jit(solution)/shard_map/ppermute | solution.py:279
  32.2 0.8 %shard_map.40 = (bf16[1024,512]{1,0:T(8,128)(2,1)S(1)}, f32[1,512]{1,0:T(1,128)S(1)}, f32[8,512]{1,0:T(8,128)S(1)}) custom-call(bf16[1032,128]{1,0:T(8,128)(2,1)S(1)} %get-tuple-element.33.refs_0_, bf16[1032,128]{1,0:T(8,128)(2,1)S(1)} %collective-permute-done.2.refs_1_, bf16[1032,128]{1,0:T(8,128)(2,1)S(1)} %collective-permute-done.3.refs_2_, ...), custom_call_target="tpu_custom_call" | custom-call | flops 536870912 | bytes 1048576 | tf_op jit(solution)/shard_map/pallas_call | solution.py:23
  33.0 0.7 %collective-permute-start.15 = (bf16[1032,128]{1,0:T(8,128)(2,1)S(1)}, bf16[1032,128]{1,0:T(8,128)(2,1)S(1)}, u32[]{:S(2)}, u32[]{:S(2)}) collective-permute-start(bf16[1032,128]{1,0:T(8,128)(2,1)S(1)} %collective-permute-done.13.refs_6_), channel_id=1, source_target_pairs={{3,1},{4,6},{11,9},{12,14},{19,17},{20,22},{27,25},{28,30}} | collective-permute-start | bytes 792584 | tf_op jit(solution)/shard_map/ppermute | solution.py:279
  33.7 0.7 %collective-permute-start.16 = (bf16[1032,128]{1,0:T(8,128)(2,1)S(1)}, bf16[1032,128]{1,0:T(8,128)(2,1)S(1)}, u32[]{:S(2)}, u32[]{:S(2)}) collective-permute-start(bf16[1032,128]{1,0:T(8,128)(2,1)S(1)} %collective-permute-done.13.refs_6_), channel_id=1, source_target_pairs={{2,1},{5,6},{10,9},{13,14},{18,17},{21,22},{26,25},{29,30}} | collective-permute-start | bytes 792584 | tf_op jit(solution)/shard_map/ppermute | solution.py:279
  34.4 1.4 %shard_map.41 = (bf16[1024,512]{1,0:T(8,128)(2,1)S(1)}, f32[1,512]{1,0:T(1,128)S(1)}, f32[8,512]{1,0:T(8,128)S(1)}, f32[8,512]{1,0:T(8,128)S(1)}) custom-call(bf16[1024,512]{1,0:T(8,128)(2,1)S(1)} %get-tuple-element.34.refs_0_, f32[1,512]{1,0:T(1,128)S(1)} %get-tuple-element.35.refs_1_.refs_2_.refs_3_.refs_4_, ...), custom_call_target="tpu_custom_call" | custom-call | flops 1073741824 | bytes 2097152 | tf_op jit(solution)/shard_map/pallas_call | solution.py:23
  35.8 0.2 collective-permute-done.12.refs_7_
  36.0 1.9 %shard_map.42 = (bf16[1024,512]{1,0:T(8,128)(2,1)S(1)}, f32[1,512]{1,0:T(1,128)S(1)}, f32[8,512]{1,0:T(8,128)S(1)}, f32[8,512]{1,0:T(8,128)S(1)}, f32[8,512]{1,0:T(8,128)S(1)}) custom-call(bf16[1024,512]{1,0:T(8,128)(2,1)S(1)} %get-tuple-element.34.refs_0_, bf16[1024,512]{1,0:T(8,128)(2,1)S(1)} %get-tuple-element.37.refs_1_, ...), custom_call_target="tpu_custom_call" | custom-call | flops 1610612736 | bytes 3145728 | tf_op jit(solution)/shard_map/pallas_call | solution.py:23
  37.9 2.5 %collective-permute-done.14.refs_7_ = bf16[1032,128]{1,0:T(8,128)(2,1)S(1)} collective-permute-done((bf16[1032,128]{1,0:T(8,128)(2,1)S(1)}, bf16[1032,128]{1,0:T(8,128)(2,1)S(1)}, u32[]{:S(2)}, u32[]{:S(2)}) %collective-permute-start.14) | collective-permute-done | bytes 264224 | tf_op jit(solution)/shard_map/ppermute | solution.py:279
  40.4 1.3 %shard_map.43 = (bf16[1024,256]{1,0:T(8,128)(2,1)S(1)}, f32[1,256]{1,0:T(1,128)S(1)}, f32[8,256]{1,0:T(8,128)S(1)}, f32[8,512]{1,0:T(8,128)S(1)}, f32[8,512]{1,0:T(8,128)S(1)}, /*index=5*/f32[8,512]{1,0:T(8,128)S(1)}) custom-call(bf16[1024,512]{1,0:T(8,128)(2,1)S(1)} %get-tuple-element.34.refs_0_, bf16[1024,512]{1,0:T(8,128)(2,1)S(1)} %get-tuple-element.37.refs_1_, ...), custom_call_target="tpu_custom_call" | custom-call | flops 939524096 | bytes 3670016 | tf_op jit(solution)/shard_map/pallas_call | solution.py:23
  41.7 1.5 %shard_map.44 = f32[32,128]{1,0:T(8,128)S(1)} custom-call(bf16[1024,512]{1,0:T(8,128)(2,1)S(1)} %get-tuple-element.34.refs_0_, bf16[1024,512]{1,0:T(8,128)(2,1)S(1)} %get-tuple-element.37.refs_1_, bf16[1024,512]{1,0:T(8,128)(2,1)S(1)} %get-tuple-element.40.refs_2_, bf16[1024,256]{1,0:T(8,128)(2,1)S(1)} %get-tuple-element.43.refs_3_, ...), custom_call_target="tpu_custom_call" | custom-call | flops 1073741824 | bytes 4194304 | tf_op jit(solution)/shard_map/pallas_call | solution.py:23
  43.2 12.6 %all_to_all.11 = f32[32,1,128]{2,1,0:T(1,128)S(1)} all-to-all(f32[32,1,128]{2,1,0:T(1,128)S(1)} %bitcast.7), channel_id=1, replica_groups=mesh['group'=8,'blk'=4] {'group','blk'}, dimensions={0} | all-to-all | bytes 32768 | tf_op jit(solution)/shard_map/all_to_all | solution.py:375
  55.8 0.7 %shard_map.45 = f32[1,256]{1,0:T(1,128)} custom-call(s32[1,256]{1,0:T(1,128)S(1)} %get-tuple-element.30.pos_ref, f32[32,128]{1,0:T(8,128)S(1)} %bitcast.8), custom_call_target="tpu_custom_call" | custom-call | flops 1000000 | bytes 100000 | tf_op jit(solution)/shard_map/pallas_call | solution.py:23
  (19 shorter events, 0.1 us)
Async XLA Ops:
  0.0 2.7 %collective-permute-start = (bf16[256,1024]{1,0:T(8,128)(2,1)}, bf16[256,1024]{1,0:T(8,128)(2,1)S(1)}, u32[]{:S(2)}, u32[]{:S(2)}) collective-permute-start(bf16[256,1024]{1,0:T(8,128)(2,1)} %emb_ref.1), channel_id=1, source_target_pairs={{0,4},{4,0},{8,12},{12,8},{16,20},{20,16},{24,28},{28,24},{1,5},{5... | collective-permute-start | bytes 1572872 | tf_op jit(solution)/shard_map/ppermute | solution.py:265
  0.5 0.7 %copy-start.2 = (s32[256,1]{0,1:T(1,128)S(1)}, s32[256,1]{0,1:T(1,128)}, u32[]{:S(2)}) copy-start(s32[256,1]{0,1:T(1,128)} %param.4) | copy-start | bytes 3076
  0.5 0.7 %copy-start.1 = (s32[256]{0:T(256)S(1)}, s32[256]{0:T(256)}, u32[]{:S(2)}) copy-start(s32[256]{0:T(256)} %param.5) | copy-start | bytes 3076
  1.2 1.0 %copy-start = (bf16[256,1024]{1,0:T(8,128)(2,1)S(1)}, bf16[256,1024]{1,0:T(8,128)(2,1)}, u32[]{:S(2)}) copy-start(bf16[256,1024]{1,0:T(8,128)(2,1)} %emb_ref.1) | copy-start | bytes 1572868
  1.2 1.5 %collective-permute-start.1 = (s32[2,256]{1,0:T(2,128)S(1)}, s32[2,256]{1,0:T(2,128)S(1)}, u32[]{:S(2)}, u32[]{:S(2)}) collective-permute-start(s32[2,256]{1,0:T(2,128)S(1)} %pad_add_fusion.code_ref), channel_id=1, source_target_pairs={{0,4},{4,0},{8,12},{12,8},{16,20},{20,16},{24,28},{28,24},{1,5},{5... | collective-permute-start | bytes 6152 | tf_op jit(solution)/shard_map/ppermute | solution.py:265
  3.3 10.2 %collective-permute-start.2 = (bf16[1032,128]{1,0:T(8,128)(2,1)S(1)}, bf16[1032,128]{1,0:T(8,128)(2,1)S(1)}, u32[]{:S(2)}, u32[]{:S(2)}) collective-permute-start(bf16[1032,128]{1,0:T(8,128)(2,1)S(1)} %get-tuple-element.33.refs_0_), channel_id=1, source_target_pairs={{3,1},{4,6},{11,9},{12,14},{19,17},{20,22},{27,25},{28,30}} | collective-permute-start | bytes 792584 | tf_op jit(solution)/shard_map/ppermute | solution.py:279
  3.9 10.0 %collective-permute-start.5 = (bf16[1032,128]{1,0:T(8,128)(2,1)S(1)}, bf16[1032,128]{1,0:T(8,128)(2,1)S(1)}, u32[]{:S(2)}, u32[]{:S(2)}) collective-permute-start(bf16[1032,128]{1,0:T(8,128)(2,1)S(1)} %get-tuple-element.36), channel_id=1, source_target_pairs={{0,8},{4,12},{8,0},{12,4},{16,24},{20,28},{24,16},{28,20},{1,9},{5... | collective-permute-start | bytes 792584 | tf_op jit(solution)/shard_map/ppermute | solution.py:262
  6.5 8.2 %collective-permute-start.3 = (bf16[1032,128]{1,0:T(8,128)(2,1)S(1)}, bf16[1032,128]{1,0:T(8,128)(2,1)S(1)}, u32[]{:S(2)}, u32[]{:S(2)}) collective-permute-start(bf16[1032,128]{1,0:T(8,128)(2,1)S(1)} %get-tuple-element.33.refs_0_), channel_id=1, source_target_pairs={{2,1},{5,6},{10,9},{13,14},{18,17},{21,22},{26,25},{29,30}} | collective-permute-start | bytes 792584 | tf_op jit(solution)/shard_map/ppermute | solution.py:279
  7.2 8.6 %collective-permute-start.4 = (bf16[1032,128]{1,0:T(8,128)(2,1)S(1)}, bf16[1032,128]{1,0:T(8,128)(2,1)S(1)}, u32[]{:S(2)}, u32[]{:S(2)}) collective-permute-start(bf16[1032,128]{1,0:T(8,128)(2,1)S(1)} %get-tuple-element.33.refs_0_), channel_id=1, source_target_pairs={{0,1},{7,6},{8,9},{15,14},{16,17},{23,22},{24,25},{31,30}} | collective-permute-start | bytes 792584 | tf_op jit(solution)/shard_map/ppermute | solution.py:279
  11.9 13.7 %collective-permute-start.9 = (bf16[1032,128]{1,0:T(8,128)(2,1)S(1)}, bf16[1032,128]{1,0:T(8,128)(2,1)S(1)}, u32[]{:S(2)}, u32[]{:S(2)}) collective-permute-start(bf16[1032,128]{1,0:T(8,128)(2,1)S(1)} %get-tuple-element.39), channel_id=1, source_target_pairs={{0,16},{4,20},{8,24},{12,28},{16,0},{20,4},{24,8},{28,12},{1,17},{... | collective-permute-start | bytes 792584 | tf_op jit(solution)/shard_map/ppermute | solution.py:262
  13.5 12.8 %collective-permute-start.13 = (bf16[1032,128]{1,0:T(8,128)(2,1)S(1)}, bf16[1032,128]{1,0:T(8,128)(2,1)S(1)}, u32[]{:S(2)}, u32[]{:S(2)}) collective-permute-start(bf16[1032,128]{1,0:T(8,128)(2,1)S(1)} %get-tuple-element.42), channel_id=1, source_target_pairs={{0,24},{4,28},{8,16},{12,20},{16,8},{20,12},{24,0},{28,4},{1,25},{... | collective-permute-start | bytes 792584 | tf_op jit(solution)/shard_map/ppermute | solution.py:262
  14.0 13.0 %collective-permute-start.6 = (bf16[1032,128]{1,0:T(8,128)(2,1)S(1)}, bf16[1032,128]{1,0:T(8,128)(2,1)S(1)}, u32[]{:S(2)}, u32[]{:S(2)}) collective-permute-start(bf16[1032,128]{1,0:T(8,128)(2,1)S(1)} %collective-permute-done.5.refs_2_), channel_id=1, source_target_pairs={{3,1},{4,6},{11,9},{12,14},{19,17},{20,22},{27,25},{28,30}} | collective-permute-start | bytes 792584 | tf_op jit(solution)/shard_map/ppermute | solution.py:279
  14.7 16.2 %collective-permute-start.7 = (bf16[1032,128]{1,0:T(8,128)(2,1)S(1)}, bf16[1032,128]{1,0:T(8,128)(2,1)S(1)}, u32[]{:S(2)}, u32[]{:S(2)}) collective-permute-start(bf16[1032,128]{1,0:T(8,128)(2,1)S(1)} %collective-permute-done.5.refs_2_), channel_id=1, source_target_pairs={{2,1},{5,6},{10,9},{13,14},{18,17},{21,22},{26,25},{29,30}} | collective-permute-start | bytes 792584 | tf_op jit(solution)/shard_map/ppermute | solution.py:279
  15.8 17.3 %collective-permute-start.8 = (bf16[1032,128]{1,0:T(8,128)(2,1)S(1)}, bf16[1032,128]{1,0:T(8,128)(2,1)S(1)}, u32[]{:S(2)}, u32[]{:S(2)}) collective-permute-start(bf16[1032,128]{1,0:T(8,128)(2,1)S(1)} %collective-permute-done.5.refs_2_), channel_id=1, source_target_pairs={{0,1},{7,6},{8,9},{15,14},{16,17},{23,22},{24,25},{31,30}} | collective-permute-start | bytes 792584 | tf_op jit(solution)/shard_map/ppermute | solution.py:279
  25.6 8.1 %collective-permute-start.10 = (bf16[1032,128]{1,0:T(8,128)(2,1)S(1)}, bf16[1032,128]{1,0:T(8,128)(2,1)S(1)}, u32[]{:S(2)}, u32[]{:S(2)}) collective-permute-start(bf16[1032,128]{1,0:T(8,128)(2,1)S(1)} %collective-permute-done.9.refs_4_), channel_id=1, source_target_pairs={{3,1},{4,6},{11,9},{12,14},{19,17},{20,22},{27,25},{28,30}} | collective-permute-start | bytes 792584 | tf_op jit(solution)/shard_map/ppermute | solution.py:279
  26.3 9.5 %collective-permute-start.11 = (bf16[1032,128]{1,0:T(8,128)(2,1)S(1)}, bf16[1032,128]{1,0:T(8,128)(2,1)S(1)}, u32[]{:S(2)}, u32[]{:S(2)}) collective-permute-start(bf16[1032,128]{1,0:T(8,128)(2,1)S(1)} %collective-permute-done.9.refs_4_), channel_id=1, source_target_pairs={{2,1},{5,6},{10,9},{13,14},{18,17},{21,22},{26,25},{29,30}} | collective-permute-start | bytes 792584 | tf_op jit(solution)/shard_map/ppermute | solution.py:279
  27.0 9.0 %collective-permute-start.12 = (bf16[1032,128]{1,0:T(8,128)(2,1)S(1)}, bf16[1032,128]{1,0:T(8,128)(2,1)S(1)}, u32[]{:S(2)}, u32[]{:S(2)}) collective-permute-start(bf16[1032,128]{1,0:T(8,128)(2,1)S(1)} %collective-permute-done.9.refs_4_), channel_id=1, source_target_pairs={{0,1},{7,6},{8,9},{15,14},{16,17},{23,22},{24,25},{31,30}} | collective-permute-start | bytes 792584 | tf_op jit(solution)/shard_map/ppermute | solution.py:279
  30.9 9.5 %collective-permute-start.14 = (bf16[1032,128]{1,0:T(8,128)(2,1)S(1)}, bf16[1032,128]{1,0:T(8,128)(2,1)S(1)}, u32[]{:S(2)}, u32[]{:S(2)}) collective-permute-start(bf16[1032,128]{1,0:T(8,128)(2,1)S(1)} %collective-permute-done.13.refs_6_), channel_id=1, source_target_pairs={{0,1},{7,6},{8,9},{15,14},{16,17},{23,22},{24,25},{31,30}} | collective-permute-start | bytes 792584 | tf_op jit(solution)/shard_map/ppermute | solution.py:279
  33.0 8.7 %collective-permute-start.15 = (bf16[1032,128]{1,0:T(8,128)(2,1)S(1)}, bf16[1032,128]{1,0:T(8,128)(2,1)S(1)}, u32[]{:S(2)}, u32[]{:S(2)}) collective-permute-start(bf16[1032,128]{1,0:T(8,128)(2,1)S(1)} %collective-permute-done.13.refs_6_), channel_id=1, source_target_pairs={{3,1},{4,6},{11,9},{12,14},{19,17},{20,22},{27,25},{28,30}} | collective-permute-start | bytes 792584 | tf_op jit(solution)/shard_map/ppermute | solution.py:279
  33.7 8.0 %collective-permute-start.16 = (bf16[1032,128]{1,0:T(8,128)(2,1)S(1)}, bf16[1032,128]{1,0:T(8,128)(2,1)S(1)}, u32[]{:S(2)}, u32[]{:S(2)}) collective-permute-start(bf16[1032,128]{1,0:T(8,128)(2,1)S(1)} %collective-permute-done.13.refs_6_), channel_id=1, source_target_pairs={{2,1},{5,6},{10,9},{13,14},{18,17},{21,22},{26,25},{29,30}} | collective-permute-start | bytes 792584 | tf_op jit(solution)/shard_map/ppermute | solution.py:279
